TPU v7x, 32 devices: a whole 2x2x4 slice. The times are simulated.
32 devices in a mesh: row: 8 (over z, y), col: 4 (over x, core).
Axes of the slice: x: 2, y: 2, z: 4, core: 2. Of those that a mesh axis runs over, the one named last changes fastest.
Arguments:
- matrix: float32 [1536, 1536], P('row', 'col'), may hold values from -30 to 30
- panels: float32 [2, 1536, 256], P(None, ('col', 'row')), may hold values from -0.15625 to 0.15625
- factors: float32 [2, 256, 256], replicated, may hold values from -1 to 2, as said below
Outputs:
- reduced: float32 [1536, 1536], P('row', 'col')
Inputs may be any that keep to these rules, and one draw needn't show every extreme that they name: Each factors[s] is upper triangular with diagonal entries between 1 and 2.
All inputs are finite; a program needn't handle non-finite values.
Results may differ from a plain program's by a relative error of at most 0.0003.
Values sent between devices are 32-bit elements; how exact they have to be, the bound alone decides.
No kernel may reach another device: no remote copies, remote signals or barrier semaphores. Data moves between devices by JAX's collectives and lax.ppermute only.
A program may use at most 64 MiB of HBM per device.

v0:
```python
import jax
import jax.numpy as jnp
from jax import lax
from jax.sharding import PartitionSpec as P

highest = lax.Precision.HIGHEST


def from_root(block, axis, owner):
    block = jnp.where(lax.axis_index(axis) == owner, block, jnp.zeros_like(block))
    return lax.psum(block, axis)


def matmul(left, right):
    return jnp.dot(left, right, precision=highest, preferred_element_type=jnp.float32)


def transposed_product(left, right):
    return lax.dot_general(
        left, right, (((0,), (0,)), ((), ())), precision=highest, preferred_element_type=jnp.float32
    )


def outer_product(left, right):
    return lax.dot_general(
        left, right, (((1,), (1,)), ((), ())), precision=highest, preferred_element_type=jnp.float32
    )


def per_device(matrix, panels, factors):
    row_count = lax.axis_size("row")
    col_count = lax.axis_size("col")
    my_row = lax.axis_index("row")
    block_rows = matrix.shape[0]
    share = panels.shape[1]
    source = my_row * col_count // row_count
    offset = share * (my_row * col_count - source * row_count)
    gathered = lax.all_gather(panels, "row", axis=1, tiled=True)
    relayed = from_root(gathered, "col", source)
    current = matrix
    for section in range(panels.shape[0]):
        factor = factors[section]
        panel_cols = gathered[section]
        panel_rows = lax.dynamic_slice_in_dim(relayed[section], offset, block_rows, 0)
        sums_rows = lax.psum(matmul(current, panel_cols), "col")
        sums_cols = lax.psum(transposed_product(current, panel_rows), "row")
        image_rows = matmul(sums_rows, factor)
        image_cols = matmul(sums_cols, factor)
        inner = lax.psum(transposed_product(panel_rows, image_rows), "row")
        correction = transposed_product(factor, inner)
        update_rows = image_rows - 0.5 * matmul(panel_rows, correction)
        update_cols = image_cols - 0.5 * matmul(panel_cols, correction)
        current = (
            current
            - outer_product(panel_rows, update_cols)
            - outer_product(update_rows, panel_cols)
        )
    return current


def solution(mesh):
    return jax.shard_map(
        per_device,
        mesh=mesh,
        in_specs=(P("row", "col"), P(None, ("col", "row"), None), P()),
        out_specs=P("row", "col"),
        check_vma=False,
    )
```

profile of v0, /device:TPU:0, one launch (start us, length us, event | category | flops | bytes accessed | tf_op | source)
XLA Modules:
  0.0 285.3 jit_solution(409260807775912355)
XLA Ops:
  6.5 0.0 all-reduce.14.cloned.1.call-start
  6.5 0.0 copy-start.1
  6.5 34.2 %all_gather.3 = f32[2,384,256]{2,1,0:T(8,128)S(1)} all-gather(f32[2,48,256]{2,1,0:T(8,128)} %param.4), channel_id=1, replica_groups=mesh['row'=8,'col'=4] {'row'}, dimensions={1}, use_global_device_ids=true | all-gather | bytes 884736 | tf_op jit(solution)/shard_map/all_gather | solution.py:38
  40.8 0.0 copy-done.1
  40.8 1.2 fusion.4
  41.9 1.0 broadcast_select_fusion
  42.9 0.0 all-reduce.14.cloned.1.call-update
  42.9 0.0 all-reduce.12.cloned.1.call-start
  43.0 36.9 %all-reduce.14.cloned.1.call-done = (f32[192,256]{1,0:T(8,128)}, f32[2,384,256]{2,1,0:T(8,128)}) async-done(((f32[192,256]{1,0:T(8,128)}, f32[2,384,256]{2,1,0:T(8,128)}), (f32[192,256]{1,0:T(8,128)}, f32[2,384,256]{2,1,0:T(8,128)})) %all-reduce.14.cloned.1.call-update) | async-done | bytes 983056 | tf_op jit(solution)/shard_map/psum | solution.py:45
  79.9 0.0 copy-start
  79.9 0.0 copy-start.4
  79.9 1.2 fusion.49
  81.1 0.0 copy-done
  81.1 0.0 copy-done.4
  81.2 0.3 fusion.13
  81.5 1.4 convolution_bitcast_fusion
  82.9 1.4 fusion.30
  84.3 0.0 all-reduce.12.cloned.1.call-update
  84.3 0.0 all-reduce.8.cloned.1.call-start
  84.4 74.2 %all-reduce.12.cloned.1.call-done = (f32[256,256]{1,0:T(8,128)}, f32[384,256]{0,1:T(8,128)}) async-done(((f32[256,256]{1,0:T(8,128)}, f32[384,256]{0,1:T(8,128)}), (f32[256,256]{1,0:T(8,128)}, f32[384,256]{0,1:T(8,128)})) %all-reduce.12.cloned.1.call-update) | async-done | bytes 655376 | tf_op jit(solution)/shard_map/psum | solution.py:49
  158.6 1.5 fusion.11
  160.2 0.4 fusion.3
  160.6 0.0 copy-start.2
  160.6 0.5 fusion.1
  161.1 0.5 copy-done.2
  161.6 0.8 convolution_subtract_fusion.1
  162.4 0.5 convolution_subtract_fusion.5
  162.9 0.5 convolution_subtract_fusion.4
  163.5 1.2 fusion.5
  164.7 0.0 all-reduce.8.cloned.1.call-update
  164.7 0.0 all-reduce.10.cloned.1.call-start
  164.7 1.6 fusion.26
  166.3 30.0 %all-reduce.8.cloned.1.call-done = f32[192,256]{1,0:T(8,128)} async-done(((f32[192,256]{1,0:T(8,128)}), f32[192,256]{1,0:T(8,128)}) %all-reduce.8.cloned.1.call-update) | async-done | bytes 196624 | tf_op jit(solution)/shard_map/psum | solution.py:45
  196.4 1.3 fusion.8
  197.6 1.4 fusion.24
  199.0 0.0 all-reduce.10.cloned.1.call-update
  199.0 74.5 %all-reduce.10.cloned.1.call-done = (f32[256,256]{1,0:T(8,128)}, f32[384,256]{1,0:T(8,128)}) async-done(((f32[256,256]{1,0:T(8,128)}, f32[384,256]{1,0:T(8,128)}), (f32[256,256]{1,0:T(8,128)}, f32[384,256]{1,0:T(8,128)})) %all-reduce.10.cloned.1.call-update) | async-done | bytes 655376 | tf_op jit(solution)/shard_map/psum | solution.py:49
  273.5 1.5 fusion.6
  275.1 0.4 fusion.2
  275.5 0.0 copy-start.3
  275.5 0.5 fusion
  276.0 0.5 copy-done.3
  276.5 0.5 convolution_subtract_fusion
  277.0 0.5 convolution_subtract_fusion.3
  277.5 1.3 convolution_subtract_fusion.2
Async XLA Ops:
  6.5 73.3 %all-reduce.14.cloned.1.call-start = ((), (), s32[]{:S(2)}) async-start(), calls=%async_computation.3 | async-start | bytes 1966080 | tf_op jit(solution)/shard_map/psum | solution.py:45
  6.5 34.2 %copy-start.1 = (f32[192,384]{1,0:T(8,128)S(1)}, f32[192,384]{1,0:T(8,128)}, u32[]{:S(2)}) copy-start(f32[192,384]{1,0:T(8,128)} %param.3) | copy-start | bytes 884740
  42.9 115.7 %all-reduce.12.cloned.1.call-start = ((), (), s32[]{:S(2)}) async-start(), calls=%async_computation.2 | async-start | bytes 1310720 | tf_op jit(solution)/shard_map/psum | solution.py:49
  79.9 1.3 copy-start
  79.9 1.3 copy-start.4
  84.3 112.0 %all-reduce.8.cloned.1.call-start = ((), (), s32[]{:S(2)}) async-start(), calls=%async_computation | async-start | bytes 393216 | tf_op jit(solution)/shard_map/psum | solution.py:45
  160.6 1.0 copy-start.2
  164.7 108.8 %all-reduce.10.cloned.1.call-start = ((), (), s32[]{:S(2)}) async-start(), calls=%async_computation.1 | async-start | bytes 1310720 | tf_op jit(solution)/shard_map/psum | solution.py:49
  275.5 1.0 copy-start.3
Sparse Core Ops, SparseCore 0:
  43.0 36.7 all-reduce.13
  84.5 74.1 all-reduce.11
  164.8 31.5 all-reduce.7
  199.7 73.7 all-reduce.9
where the time goes:
time: 286 us; the launch traced here: 285 us
  waiting for transfers between devices  216 us (76%)
  blocking collectives  34.2 us (12%)
  matrix products  18.8 us (7%)
  between operations  13.3 us (5%)
    psum x2, waiting for transfers between devices, per_device(): inner = lax.psum(transposed_product(panel_rows, image_rows), 'row')  149 us
    psum x2, waiting for transfers between devices, per_device(): sums_rows = lax.psum(matmul(current, panel_cols), 'col')  66.9 us
    all_gather x1, blocking collectives, per_device(): gathered = lax.all_gather(panels, 'row', axis=1, tiled=True)  34.2 us
    dot_general x6, matrix products, transposed_product(): lax.dot_general(left, right, (((0,), (0,)), ((), ())), precision=highest,...  8.86 us
    dot_general x10, matrix products, matmul(): jnp.dot(left, right, precision=highest, preferred_element_type=jnp.float32)  7.09 us
  transfers between devices with their start and end apart: 4, of which 4 were waited for; matrix products, arithmetic and copies ran while one was open for 1% of the time, Pallas kernels for 0%

commit v1 on v0

--- a/solution.py
+++ b/solution.py
@@ -1,7 +1,12 @@
+import functools
+
 import jax
 import jax.numpy as jnp
 from jax import lax
+from jax.experimental import pallas as pl
+from jax.experimental.pallas import tpu as pltpu
 from jax.sharding import PartitionSpec as P
+
 
 highest = lax.Precision.HIGHEST
 
@@ -27,7 +32,7 @@
     )
 
 
-def per_device(matrix, panels, factors):
+def general_device(matrix, panels, factors):
     row_count = lax.axis_size("row")
     col_count = lax.axis_size("col")
     my_row = lax.axis_index("row")
@@ -58,9 +63,434 @@
     return current
 
 
+def split(value):
+    high = value.astype(jnp.bfloat16)
+    low = (value - high.astype(jnp.float32)).astype(jnp.bfloat16)
+    return high, low
+
+
+def dot3(left, right, dims=(1, 0)):
+    numbers = (((dims[0],), (dims[1],)), ((), ()))
+    one = functools.partial(
+        lax.dot_general, dimension_numbers=numbers, preferred_element_type=jnp.float32
+    )
+    return one(left[0], right[0]) + (one(left[0], right[1]) + one(left[1], right[0]))
+
+
+def place():
+    row, col = lax.axis_index("row"), lax.axis_index("col")
+    return row // 2, row % 2, col // 2, col % 2
+
+
+def vmem(count):
+    return [pl.BlockSpec(memory_space=pltpu.VMEM)] * count
+
+
+def call(body, shapes, operands, scratch=(), flops=0, space=pltpu.VMEM):
+    moved = sum(4 * o.size for o in operands) + sum(4 * s.size for s in shapes)
+    return pl.pallas_call(
+        body,
+        out_shape=shapes,
+        in_specs=[pl.BlockSpec(memory_space=space)] * len(operands),
+        out_specs=vmem(len(shapes)),
+        scratch_shapes=list(scratch),
+        cost_estimate=pl.CostEstimate(flops=flops, bytes_accessed=moved, transcendentals=0),
+        compiler_params=pltpu.CompilerParams(vmem_limit_bytes=20 * 1024 * 1024),
+    )(*operands)
+
+
+def prepare_body(matrix_hbm, panels_hbm, factors_hbm, *refs):
+    high_ref, low_ref, slab_ref, factor_high, factor_low, tile, factors, sems = refs
+    copies = [
+        pltpu.make_async_copy(matrix_hbm, tile, sems.at[0]),
+        pltpu.make_async_copy(factors_hbm, factors, sems.at[1]),
+        pltpu.make_async_copy(panels_hbm, slab_ref, sems.at[2]),
+    ]
+    for copy in copies:
+        copy.start()
+    copies[0].wait()
+    high_ref[...], low_ref[...] = split(tile[...])
+    copies[1].wait()
+    factor_high[...], factor_low[...] = split(factors[...])
+    copies[2].wait()
+
+
+def partial_body(depth, high_a, low_a, factor_high, factor_low, *refs):
+    slabs, (keep_ref, give_ref, high, low) = refs[: 2 * depth], refs[2 * depth :]
+    z, y, x, k = place()
+    share, width = slabs[0].shape[1], slabs[0].shape[2]
+    for flip in range(2):
+        for shift in range(depth):
+            slab = slabs[flip * depth + shift]
+            at = 2 * lax.rem(z - shift + depth, depth) + (1 - y if flip else y)
+            rows = pl.ds(pl.multiple_of(at * share, share), share)
+            for step in range(2):
+                h, l = split(slab[step])
+                high[rows, step * width : (step + 1) * width] = h
+                low[rows, step * width : (step + 1) * width] = l
+    product = dot3((high_a[...], low_a[...]), (high[...], low[...]))
+    quarter = product.shape[0] // 4
+    for step in range(2):
+        factor = (factor_high[step], factor_low[step])
+        image = dot3(split(product[:, step * width : (step + 1) * width]), factor)
+        for h in range(2):
+            for c in range(2):
+                piece = image[(2 * h + c) * quarter : (2 * h + c + 1) * quarter]
+                side = jnp.where(x == h, 0, 1)
+
+                @pl.when(k == c)
+                def _(piece=piece, side=side, step=step):
+                    keep_ref[side, step] = piece
+
+                @pl.when(k != c)
+                def _(piece=piece, side=side, step=step):
+                    give_ref[side, step] = piece
+
+
+EARLY = ((0, 0), (0, 1), (0, 2), (1, 0))
+LATE = ((0, 3), (1, 1), (1, 2), (1, 3))
+
+
+def row_of(depth, which, flip, rows):
+    z, y, x, k = place()
+    other = jnp.where(z % 2 == k, lax.rem(z + 2, depth), lax.rem(z - 1 + depth, depth))
+    near = jnp.where(z % 2 == k, z, lax.rem(z + 1, depth))
+    plane = other if which else near
+    y_from = 1 - y if flip & 1 else y
+    x_from = 1 - x if flip & 2 else x
+    return pl.multiple_of(((plane // 2) * 4 + y_from * 2 + x_from) * rows, rows)
+
+
+def panel_body(depth, *refs):
+    factor_high, factor_low, across_ref, opposite_ref = refs[:4]
+    slabs = refs[4 : 4 + 2 * depth]
+    turned_high, turned_low, high_ref, low_ref, cross_ref, rows_ref, full, turning = refs[4 + 2 * depth :]
+    z, y, x, _ = place()
+    share, width = slabs[0].shape[1], slabs[0].shape[2]
+    column = 2 * depth * share
+    for across in range(2):
+        for flip in range(2):
+            for shift in range(depth):
+                if across:
+                    slab = (opposite_ref if flip else across_ref).at[shift]
+                else:
+                    slab = slabs[flip * depth + shift]
+                at = 2 * lax.rem(z - shift + depth, depth) + (1 - y if flip else y)
+                start = (1 - x if across else x) * column + at * share
+                rows = pl.ds(pl.multiple_of(start, share), share)
+                for step in range(2):
+                    full[rows, step * width : (step + 1) * width] = slab[step]
+    half = 2 * share
+    for at, (which, flip) in enumerate(EARLY + LATE):
+        turning[at * half : (at + 1) * half, :] = full[pl.ds(row_of(depth, which, flip, half), half), :]
+    first, second = split(turning[:, :width]), split(turning[:, width:])
+    turned = (
+        dot3((factor_high[0], factor_low[0]), first, (0, 1)),
+        turning[:, width:].T,
+        dot3((factor_high[1], factor_low[1]), second, (0, 1)),
+    )
+    for at, value in enumerate(turned):
+        rows = slice(at * width, (at + 1) * width)
+        turned_high[rows, :], turned_low[rows, :] = split(value)
+    cross_ref[...] = dot3(first, second, (0, 0))
+    block = 4 * share
+    start = (z // 2) * column + y * block
+    rows_ref[...] = full[pl.ds(pl.multiple_of(start, block), block), :]
+    cols = pl.ds(pl.multiple_of(x * column, column), column)
+    high_ref[...], low_ref[...] = split(full[cols, :])
+
+
+def products(turned_high, turned_low, image, span):
+    width = image.shape[1] // 2
+    high, low = split(image[...])
+    for at, p in enumerate((slice(0, width), slice(0, width), slice(width, 2 * width))):
+        v = slice(at * width, (at + 1) * width)
+        yield dot3((turned_high[v, span], turned_low[v, span]), (high[:, p], low[:, p]))
+
+
+def fill(image, at, half, step, block):
+    quarter, width = half.shape[-2], half.shape[-1]
+    rows = pl.ds(at + block * quarter, quarter)
+    image[rows, step * width : (step + 1) * width] = half[...]
+
+
+def pieces(block):
+    for step in range(2):
+        part = block.at[step] if not isinstance(block, tuple) else block[step]
+        for q in range(2):
+            if isinstance(part, tuple):
+                yield step, q, part[q]
+            else:
+                yield step, q, part.at[q]
+
+
+def early_body(*refs):
+    near, near_y, near_x, ahead0, ahead1, turned_high, turned_low, inner_ref, image = refs
+    rows = image.shape[0] // 4
+    for at, block in enumerate((near, near_y, near_x, (ahead0, ahead1))):
+        for step, q, part in pieces(block):
+            fill(image, at * rows, part, step, q)
+    span = slice(0, 4 * rows)
+    for at, value in enumerate(products(turned_high, turned_low, image, span)):
+        inner_ref[at] = value
+
+
+def late_body(*refs):
+    (low, high, y0, y1, x0, x1, d1, before, turned_high, turned_low, inner_ref, image) = refs
+    rows = image.shape[0] // 4
+    near_d, ahead_d0 = split_corner(low, high)
+    for at, block in enumerate((near_d, (y0, y1), (x0, x1), (ahead_d0, d1))):
+        for step, q, part in pieces(block):
+            fill(image, at * rows, part, step, q)
+    span = slice(4 * rows, 8 * rows)
+    for at, value in enumerate(products(turned_high, turned_low, image, span)):
+        inner_ref[at] = before[at] + value
+
+
+def split_corner(low, high):
+    return ((low.at[0], high.at[0]), (low.at[1], high.at[1])), (low.at[2], high.at[2])
+
+
+def base_body(depth, *refs):
+    (
+        matrix_ref, factor_high, factor_low, cross_a, cross_b, high_ref, low_ref, panel_a, panel_b,
+        near, near_y, near_x, f0, f0y, f0x, f1, f1y, f1x, f1d, low, high, mine_ref, far_b,
+        out_ref, rows_high, rows_low, cross_ref, full, image, rows_v,
+    ) = refs
+    z, _, x, k = place()
+    owner = z % 2 == k
+    width = cross_a.shape[0]
+    quarter = near.shape[2]
+    half, cols = 2 * quarter, high_ref.shape[0]
+    near_d, f0d = split_corner(low, high)
+    blocks = {
+        (0, 0): near, (0, 1): near_y, (0, 2): near_x, (0, 3): near_d,
+        (1, 0): (f0, f1), (1, 1): (f0y, f1y), (1, 2): (f0x, f1x), (1, 3): (f0d, f1d),
+    }
+    for (which, flip), block in blocks.items():
+        for step, q, part in pieces(block):
+            fill(full, row_of(depth, which, flip, half), part, step, q)
+    image[pl.ds(0, cols), :] = full[pl.ds(pl.multiple_of(x * cols, cols), cols), :]
+    for step, q, part in pieces(mine_ref):
+        fill(image, pl.multiple_of(cols + x * half, half), part, step, q)
+    far = pl.multiple_of(cols + (1 - x) * half, half)
+
+    @pl.when(owner)
+    def _():
+        for step, q, part in pieces(near_x):
+            fill(image, far, part, step, q)
+        rows_v[...] = panel_a[...]
+
+    @pl.when(jnp.logical_not(owner))
+    def _():
+        for step, q, part in pieces(far_b):
+            fill(image, far, part, step, q)
+        rows_v[...] = panel_b[...]
+
+    cross = cross_a[...] + cross_b[...]
+    cross_f = dot3(split(cross), (factor_high[1], factor_low[1]))
+    cross_ref[0], cross_ref[1] = cross, cross_f
+    first, second = slice(0, width), slice(width, 2 * width)
+    w1 = split(image[:, first])
+    w2 = split(image[:, second] - dot3(w1, split(cross_f)))
+    v_rows = split(rows_v[...])
+    rows_high[...], rows_low[...] = v_rows
+    total = matrix_ref[...]
+    for w, at in ((w1, first), (w2, second)):
+        v_side = (high_ref[:, at], low_ref[:, at])
+        v_top = [v[:, at] for v in v_rows]
+        total = total - dot3(v_top, [p[:cols] for p in w], (1, 1))
+        total = total - dot3([p[cols:] for p in w], v_side, (1, 1))
+    out_ref[...] = total
+
+
+def update_body(
+    base_ref, factor_high, factor_low, inner_a, inner_b, cross_ref,
+    high_ref, low_ref, rows_high, rows_low, out_ref,
+):
+    width = cross_ref.shape[1]
+    first, second = slice(0, width), slice(width, 2 * width)
+    factor2 = (factor_high[1], factor_low[1])
+    cross, cross_f = split(cross_ref[0]), split(cross_ref[1])
+    m1 = 0.5 * (inner_a[0] + inner_b[0])
+    m1_split = split(m1)
+    v1 = (rows_high[:, first], rows_low[:, first])
+    v2 = (rows_high[:, second], rows_low[:, second])
+    mixed_t = split(inner_a[1] + inner_b[1] - dot3(cross, m1_split, (0, 0)))
+    mixed_f = dot3(mixed_t, factor2, (0, 0))
+    twice = dot3(cross_f, split(mixed_f), (0, 0))
+    side = mixed_f - dot3(m1_split, cross_f)
+    m2 = 0.5 * (inner_a[2] + inner_b[2] - twice - twice.T)
+    side_split = split(side)
+    left = dot3(v1, split(m1 + m1.T)) + dot3(v2, side_split, (1, 1))
+    right = dot3(v1, side_split) + dot3(v2, split(m2 + m2.T))
+    out_ref[...] = (
+        base_ref[...]
+        + dot3(split(left), (high_ref[:, first], low_ref[:, first]), (1, 1))
+        + dot3(split(right), (high_ref[:, second], low_ref[:, second]), (1, 1))
+    )
+
+
+def plane_device(matrix, panels, factors):
+    row_count, col_count = lax.axis_size("row"), lax.axis_size("col")
+    depth = row_count // 2
+    z, _, _, k = place()
+    owner = z % 2 == k
+    f32, bf16 = jnp.float32, jnp.bfloat16
+    shape = jax.ShapeDtypeStruct
+
+    def send(value, target):
+        pairs = []
+        for index in range(row_count * col_count):
+            row, col = divmod(index, col_count)
+            to = target(row // 2, row % 2, col // 2, col % 2)
+            pairs.append((index, (to[0] * 2 + to[1]) * col_count + to[2] * 2 + to[3]))
+        return lax.ppermute(value, ("row", "col"), pairs)
+
+    def along_z(shift):
+        return lambda z, y, x, k: ((z + shift) % depth, y, x, k)
+
+    def to_y(z, y, x, k):
+        return z, 1 - y, x, k
+
+    def to_x(z, y, x, k):
+        return z, y, 1 - x, k
+
+    def to_corner(z, y, x, k):
+        return z, 1 - y, 1 - x, k
+
+    def to_core(z, y, x, k):
+        return z, y, x, 1 - k
+
+    def forward(z, y, x, k):
+        return ((z + (2 if k == z % 2 else 1)) % depth, y, x, z % 2)
+
+    def backward(z, y, x, k):
+        return ((z - 1) % depth if k == z % 2 else z, y, x, z % 2)
+
+    _, _, width = panels.shape
+    block, cols = matrix.shape
+    quarter, channel = block // 4, 2 * cols
+
+    high_a, low_a, slab, factor_high, factor_low = call(
+        prepare_body,
+        [
+            shape(matrix.shape, bf16), shape(matrix.shape, bf16), shape(panels.shape, f32),
+            shape(factors.shape, bf16), shape(factors.shape, bf16),
+        ],
+        [matrix, panels, factors],
+        [
+            pltpu.VMEM(matrix.shape, f32), pltpu.VMEM(factors.shape, f32),
+            pltpu.SemaphoreType.DMA((3,)),
+        ],
+        space=pltpu.HBM,
+    )
+
+    order = [2, 1] + list(range(3, depth))
+    slabs = {0: slab}
+    for shift in order:
+        slabs[shift] = send(panels, along_z(shift))
+    own = [slabs[s] for s in range(depth)]
+    beside = [send(slabs[s], to_y) for s in range(depth)]
+    across = [send(slabs[s], to_x) for s in range(depth)]
+
+    keep, give = call(
+        functools.partial(partial_body, depth),
+        [shape((2, 2, quarter, width), f32)] * 2,
+        [high_a, low_a, factor_high, factor_low, *own, *beside],
+        [pltpu.VMEM((cols, 2 * width), bf16)] * 2,
+        flops=6 * block * cols * width * 2,
+    )
+    chip = keep + send(give, to_core)
+    piece = chip[0] + send(chip[1], to_x)
+    other = send(piece, to_core)
+    mine = jnp.where(k == 0, jnp.stack([piece, other], axis=1), jnp.stack([other, piece], axis=1))
+
+    stacked = jnp.stack(across)
+    opposite = send(stacked, to_y)
+    turned_high, turned_low, panel_high, panel_low, cross, panel_rows = call(
+        functools.partial(panel_body, depth),
+        [
+            shape((3 * width, channel), bf16),
+            shape((3 * width, channel), bf16),
+            shape((cols, 2 * width), bf16),
+            shape((cols, 2 * width), bf16),
+            shape((width, width), f32),
+            shape((block, 2 * width), f32),
+        ],
+        [factor_high, factor_low, stacked, opposite, *own, *beside],
+        [pltpu.VMEM((channel, 2 * width), f32)] * 2,
+        flops=6 * channel * width * width * 3,
+    )
+    cross_other = send(cross, to_core)
+    panel_rows_other = send(panel_rows, to_core)
+
+    near = jnp.where(owner, mine, send(mine, backward))
+    ahead = [send(mine[step], forward) for step in range(2)]
+    near_y, near_x = send(near, to_y), send(near, to_x)
+    f0, f1 = ahead
+    f0y, f0x = send(f0, to_y), send(f0, to_x)
+    f1y, f1x, f1d = send(f1, to_y), send(f1, to_x), send(f1, to_corner)
+    low = jnp.stack([near_x[0, 0], near_x[1, 0], f0x[0]])
+    high = jnp.stack([near_y[0, 1], near_y[1, 1], f0y[1]])
+    low, high = send(low, to_y), send(high, to_x)
+    far_other = send(near_x, to_core)
+
+    inner = call(
+        early_body,
+        [shape((3, width, width), f32)],
+        [near, near_y, near_x, f0, f1, turned_high, turned_low],
+        [pltpu.VMEM((cols, 2 * width), f32)],
+        flops=9 * channel * width * width,
+    )[0]
+    inner = call(
+        late_body,
+        [shape((3, width, width), f32)],
+        [low, high, f0y, f1y, f0x, f1x, f1d, inner, turned_high, turned_low],
+        [pltpu.VMEM((cols, 2 * width), f32)],
+        flops=9 * channel * width * width,
+    )[0]
+    inner_other = send(inner, to_core)
+    rows = cols + block
+    base, rows_high, rows_low, crosses = call(
+        functools.partial(base_body, depth),
+        [
+            shape((block, cols), f32), shape((block, 2 * width), bf16),
+            shape((block, 2 * width), bf16), shape((2, width, width), f32),
+        ],
+        [
+            matrix, factor_high, factor_low, cross, cross_other, panel_high, panel_low,
+            panel_rows, panel_rows_other, near, near_y, near_x, f0, f0y, f0x, f1, f1y, f1x, f1d,
+            low, high, mine, far_other,
+        ],
+        [
+            pltpu.VMEM((channel, 2 * width), f32), pltpu.VMEM((rows, 2 * width), f32),
+            pltpu.VMEM((block, 2 * width), f32),
+        ],
+        flops=18 * rows * width * width,
+    )
+    return call(
+        update_body,
+        [shape((block, cols), f32)],
+        [
+            base, factor_high, factor_low, inner, inner_other, crosses,
+            panel_high, panel_low, rows_high, rows_low,
+        ],
+        flops=18 * rows * width * width,
+    )[0]
+
+
+def per_device(planes, matrix, panels, factors):
+    if not planes:
+        return general_device(matrix, panels, factors)
+    return plane_device(matrix, panels, factors)
+
+
 def solution(mesh):
+    row_count, col_count = mesh.shape["row"], mesh.shape["col"]
+    planes = row_count == 2 * col_count and col_count == 4
     return jax.shard_map(
-        per_device,
+        functools.partial(per_device, planes),
         mesh=mesh,
         in_specs=(P("row", "col"), P(None, ("col", "row"), None), P()),
         out_specs=P("row", "col"),

time: 286 us -> 75.7 us (0.26)
  waiting for transfers between devices: 216 us -> 27.7 us
  starting transfers between devices: 0.13 us -> 35.6 us
  blocking collectives: 34.2 us -> 0 us
  matrix products: 18.8 us -> 0 us
  between operations: 13.3 us -> 0.18 us
  Pallas kernels: 0 us -> 8.93 us
    psum x4 -> x0, waiting for transfers between devices: 216 us -> none  [the longest x2 149 us: per_device(): inner = lax.psum(transposed_product(panel_rows, image_rows), 'row')]
    ppermute x0 -> x31, starting transfers between devices: none -> 35.6 us  [send(): return lax.ppermute(value, ('row', 'col'), pairs)]
    all_gather x1 -> x0, blocking collectives: 34.2 us -> none  [per_device(): gathered = lax.all_gather(panels, 'row', axis=1, tiled=True)]
    ppermute x0 -> x31, waiting for transfers between devices: none -> 27.7 us  [send(): return lax.ppermute(value, ('row', 'col'), pairs)]
    dot_general x20 -> x0, matrix products: 18.8 us -> none  [the longest x6 8.86 us: transposed_product(): lax.dot_general(left, right, (((0,), (0,)), ((), ())), precision=highest,...]
    pallas_call x0 -> x7, Pallas kernels: none -> 8.93 us  [call(): pl.pallas_call(body, out_shape=shapes, in_specs=[pl.BlockSpec(memory_spac...]
  transfers between devices with their start and end apart: 4 -> 31, of which waited for: 4 -> 15; matrix products, arithmetic and copies ran while one was open for 1% -> 0% of each run, Pallas kernels for 0% -> 6%
where the time goes in v1:
time: 75.7 us; the launch traced here: 75.5 us
  starting transfers between devices  35.6 us (47%)
  waiting for transfers between devices  27.7 us (37%)
  Pallas kernels  8.93 us (12%)
  local copies, waits for them, and re-layouts  2.95 us (4%)
    ppermute x31, starting transfers between devices, send(): return lax.ppermute(value, ('row', 'col'), pairs)  35.6 us
    ppermute x31, waiting for transfers between devices, send(): return lax.ppermute(value, ('row', 'col'), pairs)  27.7 us
    pallas_call x7, Pallas kernels, call(): pl.pallas_call(body, out_shape=shapes, in_specs=[pl.BlockSpec(memory_spac...  8.93 us
    unnamed x8, local copies, waits for them, and re-layouts  2.9 us
  transfers between devices with their start and end apart: 31, of which 15 were waited for; matrix products, arithmetic and copies ran while one was open for 0% of the time, Pallas kernels for 6%

profile of v1, /device:TPU:0, one launch (start us, length us, event | category | flops | bytes accessed | tf_op | source)
XLA Modules:
  0.0 75.5 jit_solution(17290891683357146122)
XLA Ops:
  0.0 4.1 %collective-permute-start.3 = (f32[2,48,256]{2,1,0:T(8,128)}, f32[2,48,256]{2,1,0:T(8,128)S(1)}, u32[]{:S(2)}, u32[]{:S(2)}) collective-permute-start(f32[2,48,256]{2,1,0:T(8,128)} %panels_hbm.1), channel_id=1, source_target_pairs={{0,16},{1,17},{2,18},{3,19},{4,20},{5,21},{6,22},{7,23},{8,24},{9,... | collective-permute-start | bytes 294920 | tf_op jit(solution)/shard_map/ppermute | solution.py:348
  4.1 1.3 %collective-permute-start.5 = (f32[2,48,256]{2,1,0:T(8,128)}, f32[2,48,256]{2,1,0:T(8,128)S(1)}, u32[]{:S(2)}, u32[]{:S(2)}) collective-permute-start(f32[2,48,256]{2,1,0:T(8,128)} %panels_hbm.1), channel_id=1, source_target_pairs={{0,24},{1,25},{2,26},{3,27},{4,28},{5,29},{6,30},{7,31},{8,0},{9,1... | collective-permute-start | bytes 294920 | tf_op jit(solution)/shard_map/ppermute | solution.py:348
  5.4 0.7 collective-permute-start.1
  6.1 1.0 %copy-done = f32[192,384]{1,0:T(8,128)S(1)} copy-done((f32[192,384]{1,0:T(8,128)S(1)}, f32[192,384]{1,0:T(8,128)}, u32[]{:S(2)}) %copy-start) | copy-done | bytes 294936
  7.1 1.0 %copy-done.2 = f32[2,256,256]{2,1,0:T(8,128)S(1)} copy-done((f32[2,256,256]{2,1,0:T(8,128)S(1)}, f32[2,256,256]{2,1,0:T(8,128)}, u32[]{:S(2)}) %copy-start.2) | copy-done | bytes 524312
  8.1 0.9 %copy-done.3 = f32[2,48,256]{2,1,0:T(8,128)S(1)} copy-done((f32[2,48,256]{2,1,0:T(8,128)S(1)}, f32[2,48,256]{2,1,0:T(8,128)}, u32[]{:S(2)}) %copy-start.3) | copy-done | bytes 98328
  9.0 0.4 shard_map.37
  9.4 1.6 %collective-permute-start.8 = (f32[2,48,256]{2,1,0:T(8,128)S(1)}, f32[2,48,256]{2,1,0:T(8,128)S(1)}, u32[]{:S(2)}, u32[]{:S(2)}) collective-permute-start(f32[2,48,256]{2,1,0:T(8,128)S(1)} %get-tuple-element.24.refs_4_.refs_0_), channel_id=1, source_target_pairs={{0,4},{1,5},{2,6},{3,7},{4,0},{5,1},{6,2},{7,3},{8,12},{9,13},{10,... | collective-permute-start | bytes 294920 | tf_op jit(solution)/shard_map/ppermute | solution.py:348
  11.0 1.4 %collective-permute-start.10 = (f32[2,48,256]{2,1,0:T(8,128)S(1)}, f32[2,48,256]{2,1,0:T(8,128)S(1)}, u32[]{:S(2)}, u32[]{:S(2)}) collective-permute-start(f32[2,48,256]{2,1,0:T(8,128)S(1)} %collective-permute-done.3.refs_6_.refs_2_), channel_id=1, source_target_pairs={{0,4},{1,5},{2,6},{3,7},{4,0},{5,1},{6,2},{7,3},{8,12},{9,13},{10,... | collective-permute-start | bytes 294920 | tf_op jit(solution)/shard_map/ppermute | solution.py:348
  12.4 0.6 collective-permute-start.11
  13.0 1.4 %collective-permute-start.9 = (f32[2,48,256]{2,1,0:T(8,128)S(1)}, f32[2,48,256]{2,1,0:T(8,128)S(1)}, u32[]{:S(2)}, u32[]{:S(2)}) collective-permute-start(f32[2,48,256]{2,1,0:T(8,128)S(1)} %collective-permute-done.1.refs_5_.refs_1_), channel_id=1, source_target_pairs={{0,4},{1,5},{2,6},{3,7},{4,0},{5,1},{6,2},{7,3},{8,12},{9,13},{10,... | collective-permute-start | bytes 294920 | tf_op jit(solution)/shard_map/ppermute | solution.py:348
  14.5 0.7 collective-permute-done.8.refs_8_.refs_4_
  15.1 2.1 %collective-permute-done.10.refs_10_.refs_6_ = f32[2,48,256]{2,1,0:T(8,128)S(1)} collective-permute-done((f32[2,48,256]{2,1,0:T(8,128)S(1)}, f32[2,48,256]{2,1,0:T(8,128)S(1)}, u32[]{:S(2)}, u32[]{:S(2)}) %collective-permute-start.10) | collective-permute-done | bytes 98336 | tf_op jit(solution)/shard_map/ppermute | solution.py:348
  17.2 1.4 %collective-permute-done.11.refs_11_.refs_7_ = f32[2,48,256]{2,1,0:T(8,128)S(1)} collective-permute-done((f32[2,48,256]{2,1,0:T(8,128)S(1)}, f32[2,48,256]{2,1,0:T(8,128)S(1)}, u32[]{:S(2)}, u32[]{:S(2)}) %collective-permute-start.11) | collective-permute-done | bytes 98336 | tf_op jit(solution)/shard_map/ppermute | solution.py:348
  18.6 1.1 %collective-permute-done.9.refs_9_.refs_5_ = f32[2,48,256]{2,1,0:T(8,128)S(1)} collective-permute-done((f32[2,48,256]{2,1,0:T(8,128)S(1)}, f32[2,48,256]{2,1,0:T(8,128)S(1)}, u32[]{:S(2)}, u32[]{:S(2)}) %collective-permute-start.9) | collective-permute-done | bytes 98336 | tf_op jit(solution)/shard_map/ppermute | solution.py:348
  19.7 1.2 %shard_map.39 = (f32[2,2,48,256]{3,2,1,0:T(8,128)S(1)}, f32[2,2,48,256]{3,2,1,0:T(8,128)S(1)}) custom-call(bf16[192,384]{1,0:T(8,128)(2,1)S(1)} %get-tuple-element.29.high_a, bf16[192,384]{1,0:T(8,128)(2,1)S(1)} %get-tuple-element.30.low_a, bf16[2,256,256]{2,1,0:T(8,128)(2,1)S(1)} %get-tuple-element.22.refs_0_.factor_high.refs_1_, ...), custom_call_target="tpu_custom_call" | custom-call | flops 226492416 | bytes 2818048 | tf_op jit(solution)/shard_map/pallas_call | solution.py:91
  20.9 1.4 %collective-permute-done.14 = f32[2,2,48,256]{3,2,1,0:T(8,128)S(1)} collective-permute-done((f32[2,2,48,256]{3,2,1,0:T(8,128)S(1)}, f32[2,2,48,256]{3,2,1,0:T(8,128)S(1)}, u32[]{:S(2)}, u32[]{:S(2)}) %collective-permute-start.14) | collective-permute-done | bytes 196640 | tf_op jit(solution)/shard_map/ppermute | solution.py:348
  22.4 1.6 %collective-permute-start.15 = (f32[2,48,256]{2,1,0:T(8,128)S(1)}, f32[2,48,256]{2,1,0:T(8,128)S(1)}, u32[]{:S(2)}, u32[]{:S(2)}) collective-permute-start(f32[2,48,256]{2,1,0:T(8,128)S(1)} %slice_bitcast_fusion.2), channel_id=1, source_target_pairs={{0,2},{1,3},{2,0},{3,1},{4,6},{5,7},{6,4},{7,5},{8,10},{9,11},{10,... | collective-permute-start | bytes 294920 | tf_op jit(solution)/shard_map/ppermute | solution.py:348
  23.9 3.4 %collective-permute-done.15 = f32[2,48,256]{2,1,0:T(8,128)S(1)} collective-permute-done((f32[2,48,256]{2,1,0:T(8,128)S(1)}, f32[2,48,256]{2,1,0:T(8,128)S(1)}, u32[]{:S(2)}, u32[]{:S(2)}) %collective-permute-start.15) | collective-permute-done | bytes 98336 | tf_op jit(solution)/shard_map/ppermute | solution.py:348
  27.4 1.6 %collective-permute-start = (f32[2,48,256]{2,1,0:T(8,128)S(1)}, f32[2,48,256]{2,1,0:T(8,128)S(1)}, u32[]{:S(2)}, u32[]{:S(2)}) collective-permute-start(f32[2,48,256]{2,1,0:T(8,128)S(1)} %get-tuple-element.24.refs_4_.refs_0_), channel_id=1, source_target_pairs={{0,2},{1,3},{2,0},{3,1},{4,6},{5,7},{6,4},{7,5},{8,10},{9,11},{10,... | collective-permute-start | bytes 294920 | tf_op jit(solution)/shard_map/ppermute | solution.py:348
  28.9 0.5 collective-permute-start.2
  29.5 1.5 %collective-permute-start.4 = (f32[2,48,256]{2,1,0:T(8,128)S(1)}, f32[2,48,256]{2,1,0:T(8,128)S(1)}, u32[]{:S(2)}, u32[]{:S(2)}) collective-permute-start(f32[2,48,256]{2,1,0:T(8,128)S(1)} %collective-permute-done.3.refs_6_.refs_2_), channel_id=1, source_target_pairs={{0,2},{1,3},{2,0},{3,1},{4,6},{5,7},{6,4},{7,5},{8,10},{9,11},{10,... | collective-permute-start | bytes 294920 | tf_op jit(solution)/shard_map/ppermute | solution.py:348
  31.0 0.5 collective-permute-start.6
  31.5 4.2 %collective-permute-start.17 = (f32[2,2,48,256]{3,2,1,0:T(8,128)S(1)}, f32[2,2,48,256]{3,2,1,0:T(8,128)S(1)}, u32[]{:S(2)}, u32[]{:S(2)}) collective-permute-start(f32[2,2,48,256]{3,2,1,0:T(8,128)S(1)} %maximum_select_fusion.refs_21_), channel_id=1, source_target_pairs={{0,24},{1,0},{2,26},{3,2},{4,28},{5,4},{6,30},{7,6},{8,9},{9,1},{1... | collective-permute-start | bytes 589832 | tf_op jit(solution)/shard_map/ppermute | solution.py:348
  35.7 3.2 %collective-permute-done.17 = f32[2,2,48,256]{3,2,1,0:T(8,128)S(1)} collective-permute-done((f32[2,2,48,256]{3,2,1,0:T(8,128)S(1)}, f32[2,2,48,256]{3,2,1,0:T(8,128)S(1)}, u32[]{:S(2)}, u32[]{:S(2)}) %collective-permute-start.17) | collective-permute-done | bytes 196640 | tf_op jit(solution)/shard_map/ppermute | solution.py:348
  38.9 1.6 %collective-permute-start.18 = (f32[2,2,48,256]{3,2,1,0:T(8,128)S(1)}, f32[2,2,48,256]{3,2,1,0:T(8,128)S(1)}, u32[]{:S(2)}, u32[]{:S(2)}) collective-permute-start(f32[2,2,48,256]{3,2,1,0:T(8,128)S(1)} %broadcast_select_fusion.refs_9_.refs_0_), channel_id=1, source_target_pairs={{0,4},{1,5},{2,6},{3,7},{4,0},{5,1},{6,2},{7,3},{8,12},{9,13},{10,... | collective-permute-start | bytes 589832 | tf_op jit(solution)/shard_map/ppermute | solution.py:348
  40.5 3.9 %collective-permute-done.20.refs_12_.refs_3_ = f32[2,48,256]{2,1,0:T(8,128)S(1)} collective-permute-done((f32[2,48,256]{2,1,0:T(8,128)S(1)}, f32[2,48,256]{2,1,0:T(8,128)S(1)}, u32[]{:S(2)}, u32[]{:S(2)}) %collective-permute-start.20) | collective-permute-done | bytes 98336 | tf_op jit(solution)/shard_map/ppermute | solution.py:348
  44.4 1.5 %collective-permute-start.21 = (f32[2,48,256]{2,1,0:T(8,128)S(1)}, f32[2,48,256]{2,1,0:T(8,128)S(1)}, u32[]{:S(2)}, u32[]{:S(2)}) collective-permute-start(f32[2,48,256]{2,1,0:T(8,128)S(1)} %collective-permute-done.20.refs_12_.refs_3_), channel_id=1, source_target_pairs={{0,4},{1,5},{2,6},{3,7},{4,0},{5,1},{6,2},{7,3},{8,12},{9,13},{10,... | collective-permute-start | bytes 294920 | tf_op jit(solution)/shard_map/ppermute | solution.py:348
  45.9 1.5 %collective-permute-start.22 = (f32[2,48,256]{2,1,0:T(8,128)S(1)}, f32[2,48,256]{2,1,0:T(8,128)S(1)}, u32[]{:S(2)}, u32[]{:S(2)}) collective-permute-start(f32[2,48,256]{2,1,0:T(8,128)S(1)} %collective-permute-done.20.refs_12_.refs_3_), channel_id=1, source_target_pairs={{0,2},{1,3},{2,0},{3,1},{4,6},{5,7},{6,4},{7,5},{8,10},{9,11},{10,... | collective-permute-start | bytes 294920 | tf_op jit(solution)/shard_map/ppermute | solution.py:348
  47.5 0.6 collective-permute-start.7
  48.1 1.7 %collective-permute-done.21.refs_13_.refs_2_ = f32[2,48,256]{2,1,0:T(8,128)S(1)} collective-permute-done((f32[2,48,256]{2,1,0:T(8,128)S(1)}, f32[2,48,256]{2,1,0:T(8,128)S(1)}, u32[]{:S(2)}, u32[]{:S(2)}) %collective-permute-start.21) | collective-permute-done | bytes 98336 | tf_op jit(solution)/shard_map/ppermute | solution.py:348
  49.8 1.5 %collective-permute-start.19 = (f32[2,2,48,256]{3,2,1,0:T(8,128)S(1)}, f32[2,2,48,256]{3,2,1,0:T(8,128)S(1)}, u32[]{:S(2)}, u32[]{:S(2)}) collective-permute-start(f32[2,2,48,256]{3,2,1,0:T(8,128)S(1)} %broadcast_select_fusion.refs_9_.refs_0_), channel_id=1, source_target_pairs={{0,2},{1,3},{2,0},{3,1},{4,6},{5,7},{6,4},{7,5},{8,10},{9,11},{10,... | collective-permute-start | bytes 589832 | tf_op jit(solution)/shard_map/ppermute | solution.py:348
  51.7 1.6 %collective-permute-start.28 = (f32[3,48,256]{2,1,0:T(8,128)S(1)}, f32[3,48,256]{2,1,0:T(8,128)S(1)}, u32[]{:S(2)}, u32[]{:S(2)}) collective-permute-start(f32[3,48,256]{2,1,0:T(8,128)S(1)} %pad_maximum_fusion.2), channel_id=1, source_target_pairs={{0,2},{1,3},{2,0},{3,1},{4,6},{5,7},{6,4},{7,5},{8,10},{9,11},{10,... | collective-permute-start | bytes 442376 | tf_op jit(solution)/shard_map/ppermute | solution.py:348
  53.2 4.4 %collective-permute-done.19.refs_11_.refs_2_ = f32[2,2,48,256]{3,2,1,0:T(8,128)S(1)} collective-permute-done((f32[2,2,48,256]{3,2,1,0:T(8,128)S(1)}, f32[2,2,48,256]{3,2,1,0:T(8,128)S(1)}, u32[]{:S(2)}, u32[]{:S(2)}) %collective-permute-start.19) | collective-permute-done | bytes 196640 | tf_op jit(solution)/shard_map/ppermute | solution.py:348
  57.6 1.6 %collective-permute-start.27 = (f32[3,48,256]{2,1,0:T(8,128)S(1)}, f32[3,48,256]{2,1,0:T(8,128)S(1)}, u32[]{:S(2)}, u32[]{:S(2)}) collective-permute-start(f32[3,48,256]{2,1,0:T(8,128)S(1)} %pad_maximum_fusion.1), channel_id=1, source_target_pairs={{0,4},{1,5},{2,6},{3,7},{4,0},{5,1},{6,2},{7,3},{8,12},{9,13},{10,... | collective-permute-start | bytes 442376 | tf_op jit(solution)/shard_map/ppermute | solution.py:348
  59.2 0.5 collective-permute-start.24
  59.7 1.5 %collective-permute-start.25 = (f32[2,48,256]{2,1,0:T(8,128)S(1)}, f32[2,48,256]{2,1,0:T(8,128)S(1)}, u32[]{:S(2)}, u32[]{:S(2)}) collective-permute-start(f32[2,48,256]{2,1,0:T(8,128)S(1)} %collective-permute-done.23.refs_15_.refs_4_), channel_id=1, source_target_pairs={{0,2},{1,3},{2,0},{3,1},{4,6},{5,7},{6,4},{7,5},{8,10},{9,11},{10,... | collective-permute-start | bytes 294920 | tf_op jit(solution)/shard_map/ppermute | solution.py:348
  61.2 1.5 %collective-permute-start.26 = (f32[2,48,256]{2,1,0:T(8,128)S(1)}, f32[2,48,256]{2,1,0:T(8,128)S(1)}, u32[]{:S(2)}, u32[]{:S(2)}) collective-permute-start(f32[2,48,256]{2,1,0:T(8,128)S(1)} %collective-permute-done.23.refs_15_.refs_4_), channel_id=1, source_target_pairs={{0,6},{1,7},{2,4},{3,5},{4,2},{5,3},{6,0},{7,1},{8,14},{9,15},{10,... | collective-permute-start | bytes 294920 | tf_op jit(solution)/shard_map/ppermute | solution.py:348
  62.7 1.4 %shard_map.38 = (bf16[768,768]{1,0:T(8,128)(2,1)S(1)}, bf16[768,768]{1,0:T(8,128)(2,1)S(1)}, bf16[384,512]{1,0:T(8,128)(2,1)S(1)}, bf16[384,512]{1,0:T(8,128)(2,...) custom-call(bf16[2,256,256]{2,1,0:T(8,128)(2,1)S(1)} %get-tuple-element.22.refs_0_.factor_high.refs_1_, ...), custom_call_target="tpu_custom_call" | custom-call | flops 905969664 | bytes 9568256 | tf_op jit(solution)/shard_map/pallas_call | solution.py:91
  64.2 0.8 %shard_map.41.refs_7_ = f32[3,256,256]{2,1,0:T(8,128)S(1)} custom-call(f32[2,2,48,256]{3,2,1,0:T(8,128)S(1)} %broadcast_select_fusion.refs_9_.refs_0_, f32[2,2,48,256]{3,2,1,0:T(8,128)S(1)} %collective-permute-done.18.refs_10_.refs_1_, f32[2,2,48,256]{3,2,1,0:T(8,128)S(1)} %collective-permute-done.19.refs_11_.refs_2_, ...), custom_call_target="tpu_custom_call" | custom-call | flops 452984832 | bytes 6291456 | tf_op jit(solution)/shard_map/pallas_call | solution.py:91
  64.9 0.6 collective-permute-done.24.refs_16_.refs_3_
  65.6 1.2 %collective-permute-done.26.refs_18_.refs_6_ = f32[2,48,256]{2,1,0:T(8,128)S(1)} collective-permute-done((f32[2,48,256]{2,1,0:T(8,128)S(1)}, f32[2,48,256]{2,1,0:T(8,128)S(1)}, u32[]{:S(2)}, u32[]{:S(2)}) %collective-permute-start.26) | collective-permute-done | bytes 98336 | tf_op jit(solution)/shard_map/ppermute | solution.py:348
  66.7 0.8 %shard_map.42.inner_a = f32[3,256,256]{2,1,0:T(8,128)S(1)} custom-call(f32[3,48,256]{2,1,0:T(8,128)S(1)} %collective-permute-done.27.refs_19_.refs_0_, f32[3,48,256]{2,1,0:T(8,128)S(1)} %collective-permute-done.28.refs_20_.refs_1_, f32[2,48,256]{2,1,0:T(8,128)S(1)} %collective-permute-done.21.refs_13_.refs_2_, ...), custom_call_target="tpu_custom_call" | custom-call | flops 452984832 | bytes 7077888 | tf_op jit(solution)/shard_map/pallas_call | solution.py:91
  67.6 0.5 collective-permute-start.13
  68.2 0.4 collective-permute-start.29
  68.6 2.2 %collective-permute-done.12.refs_4_ = f32[256,256]{1,0:T(8,128)S(1)} collective-permute-done((f32[256,256]{1,0:T(8,128)S(1)}, f32[256,256]{1,0:T(8,128)S(1)}, u32[]{:S(2)}, u32[]{:S(2)}) %collective-permute-start.12) | collective-permute-done | bytes 262176 | tf_op jit(solution)/shard_map/ppermute | solution.py:348
  71.1 1.8 %shard_map.40 = (f32[192,384]{1,0:T(8,128)S(1)}, bf16[192,512]{1,0:T(8,128)(2,1)S(1)}, bf16[192,512]{1,0:T(8,128)(2,1)S(1)}, f32[2,256,256]{2,1,0:T(8,128)S(1)}) custom-call(f32[192,384]{1,0:T(8,128)S(1)} %copy-done.1, bf16[2,256,256]{2,1,0:T(8,128)(2,1)S(1)} %get-tuple-element.22.refs_0_.factor_high.refs_1_, ...), custom_call_target="tpu_custom_call" | custom-call | flops 679477248 | bytes 7798784 | tf_op jit(solution)/shard_map/pallas_call | solution.py:91
  72.9 2.6 %shard_map.43 = f32[192,384]{1,0:T(8,128)} custom-call(f32[192,384]{1,0:T(8,128)S(1)} %get-tuple-element.33.base_ref, bf16[2,256,256]{2,1,0:T(8,128)(2,1)S(1)} %get-tuple-element.22.refs_0_.factor_high.refs_1_, bf16[2,256,256]{2,1,0:T(8,128)(2,1)S(1)} %get-tuple-element.23.refs_1_.factor_low.refs_2_, f32[3,256,256]{2,1,0:T(8,128)S(1)} %shard_map.42.inner_a, ...), custom_call_target="tpu_custom_call" | custom-call | flops 679477248 | bytes 6094848 | tf_op jit(solution)/shard_map/pallas_call | solution.py:91
  (42 shorter events, 1.2 us)
Async XLA Ops:
  0.0 11.0 %collective-permute-start.3 = (f32[2,48,256]{2,1,0:T(8,128)}, f32[2,48,256]{2,1,0:T(8,128)S(1)}, u32[]{:S(2)}, u32[]{:S(2)}) collective-permute-start(f32[2,48,256]{2,1,0:T(8,128)} %panels_hbm.1), channel_id=1, source_target_pairs={{0,16},{1,17},{2,18},{3,19},{4,20},{5,21},{6,22},{7,23},{8,24},{9,... | collective-permute-start | bytes 294920 | tf_op jit(solution)/shard_map/ppermute | solution.py:348
  4.1 8.4 %collective-permute-start.5 = (f32[2,48,256]{2,1,0:T(8,128)}, f32[2,48,256]{2,1,0:T(8,128)S(1)}, u32[]{:S(2)}, u32[]{:S(2)}) collective-permute-start(f32[2,48,256]{2,1,0:T(8,128)} %panels_hbm.1), channel_id=1, source_target_pairs={{0,24},{1,25},{2,26},{3,27},{4,28},{5,29},{6,30},{7,31},{8,0},{9,1... | collective-permute-start | bytes 294920 | tf_op jit(solution)/shard_map/ppermute | solution.py:348
  5.4 7.6 %collective-permute-start.1 = (f32[2,48,256]{2,1,0:T(8,128)}, f32[2,48,256]{2,1,0:T(8,128)S(1)}, u32[]{:S(2)}, u32[]{:S(2)}) collective-permute-start(f32[2,48,256]{2,1,0:T(8,128)} %panels_hbm.1), channel_id=1, source_target_pairs={{0,8},{1,9},{2,10},{3,11},{4,12},{5,13},{6,14},{7,15},{8,16},{9,17... | collective-permute-start | bytes 294920 | tf_op jit(solution)/shard_map/ppermute | solution.py:348
  6.1 1.0 %copy-start = (f32[192,384]{1,0:T(8,128)S(1)}, f32[192,384]{1,0:T(8,128)}, u32[]{:S(2)}) copy-start(f32[192,384]{1,0:T(8,128)} %refs_0_.1) | copy-start | bytes 884740
  7.1 1.0 %copy-start.2 = (f32[2,256,256]{2,1,0:T(8,128)S(1)}, f32[2,256,256]{2,1,0:T(8,128)}, u32[]{:S(2)}) copy-start(f32[2,256,256]{2,1,0:T(8,128)} %factors_hbm.1) | copy-start | bytes 1572868
  8.1 0.9 %copy-start.3 = (f32[2,48,256]{2,1,0:T(8,128)S(1)}, f32[2,48,256]{2,1,0:T(8,128)}, u32[]{:S(2)}) copy-start(f32[2,48,256]{2,1,0:T(8,128)} %panels_hbm.1) | copy-start | bytes 294916
  9.4 5.7 %collective-permute-start.8 = (f32[2,48,256]{2,1,0:T(8,128)S(1)}, f32[2,48,256]{2,1,0:T(8,128)S(1)}, u32[]{:S(2)}, u32[]{:S(2)}) collective-permute-start(f32[2,48,256]{2,1,0:T(8,128)S(1)} %get-tuple-element.24.refs_4_.refs_0_), channel_id=1, source_target_pairs={{0,4},{1,5},{2,6},{3,7},{4,0},{5,1},{6,2},{7,3},{8,12},{9,13},{10,... | collective-permute-start | bytes 294920 | tf_op jit(solution)/shard_map/ppermute | solution.py:348
  11.0 6.3 %collective-permute-start.10 = (f32[2,48,256]{2,1,0:T(8,128)S(1)}, f32[2,48,256]{2,1,0:T(8,128)S(1)}, u32[]{:S(2)}, u32[]{:S(2)}) collective-permute-start(f32[2,48,256]{2,1,0:T(8,128)S(1)} %collective-permute-done.3.refs_6_.refs_2_), channel_id=1, source_target_pairs={{0,4},{1,5},{2,6},{3,7},{4,0},{5,1},{6,2},{7,3},{8,12},{9,13},{10,... | collective-permute-start | bytes 294920 | tf_op jit(solution)/shard_map/ppermute | solution.py:348
  12.4 6.2 %collective-permute-start.11 = (f32[2,48,256]{2,1,0:T(8,128)S(1)}, f32[2,48,256]{2,1,0:T(8,128)S(1)}, u32[]{:S(2)}, u32[]{:S(2)}) collective-permute-start(f32[2,48,256]{2,1,0:T(8,128)S(1)} %collective-permute-done.5.refs_7_.refs_3_), channel_id=1, source_target_pairs={{0,4},{1,5},{2,6},{3,7},{4,0},{5,1},{6,2},{7,3},{8,12},{9,13},{10,... | collective-permute-start | bytes 294920 | tf_op jit(solution)/shard_map/ppermute | solution.py:348
  13.0 6.6 %collective-permute-start.9 = (f32[2,48,256]{2,1,0:T(8,128)S(1)}, f32[2,48,256]{2,1,0:T(8,128)S(1)}, u32[]{:S(2)}, u32[]{:S(2)}) collective-permute-start(f32[2,48,256]{2,1,0:T(8,128)S(1)} %collective-permute-done.1.refs_5_.refs_1_), channel_id=1, source_target_pairs={{0,4},{1,5},{2,6},{3,7},{4,0},{5,1},{6,2},{7,3},{8,12},{9,13},{10,... | collective-permute-start | bytes 294920 | tf_op jit(solution)/shard_map/ppermute | solution.py:348
  20.8 1.5 %collective-permute-start.14 = (f32[2,2,48,256]{3,2,1,0:T(8,128)S(1)}, f32[2,2,48,256]{3,2,1,0:T(8,128)S(1)}, u32[]{:S(2)}, u32[]{:S(2)}) collective-permute-start(f32[2,2,48,256]{3,2,1,0:T(8,128)S(1)} %get-tuple-element.32), channel_id=1, source_target_pairs={{0,1},{1,0},{2,3},{3,2},{4,5},{5,4},{6,7},{7,6},{8,9},{9,8},{10,11... | collective-permute-start | bytes 589832 | tf_op jit(solution)/shard_map/ppermute | solution.py:348
  22.4 4.9 %collective-permute-start.15 = (f32[2,48,256]{2,1,0:T(8,128)S(1)}, f32[2,48,256]{2,1,0:T(8,128)S(1)}, u32[]{:S(2)}, u32[]{:S(2)}) collective-permute-start(f32[2,48,256]{2,1,0:T(8,128)S(1)} %slice_bitcast_fusion.2), channel_id=1, source_target_pairs={{0,2},{1,3},{2,0},{3,1},{4,6},{5,7},{6,4},{7,5},{8,10},{9,11},{10,... | collective-permute-start | bytes 294920 | tf_op jit(solution)/shard_map/ppermute | solution.py:348
  27.3 4.2 %collective-permute-start.16 = (f32[2,48,256]{2,1,0:T(8,128)S(1)}, f32[2,48,256]{2,1,0:T(8,128)S(1)}, u32[]{:S(2)}, u32[]{:S(2)}) collective-permute-start(f32[2,48,256]{2,1,0:T(8,128)S(1)} %fusion), channel_id=1, source_target_pairs={{0,1},{1,0},{2,3},{3,2},{4,5},{5,4},{6,7},{7,6},{8,9},{9,8},{10,11... | collective-permute-start | bytes 294920 | tf_op jit(solution)/shard_map/ppermute | solution.py:348
  27.4 11.6 %collective-permute-start = (f32[2,48,256]{2,1,0:T(8,128)S(1)}, f32[2,48,256]{2,1,0:T(8,128)S(1)}, u32[]{:S(2)}, u32[]{:S(2)}) collective-permute-start(f32[2,48,256]{2,1,0:T(8,128)S(1)} %get-tuple-element.24.refs_4_.refs_0_), channel_id=1, source_target_pairs={{0,2},{1,3},{2,0},{3,1},{4,6},{5,7},{6,4},{7,5},{8,10},{9,11},{10,... | collective-permute-start | bytes 294920 | tf_op jit(solution)/shard_map/ppermute | solution.py:348
  28.9 17.0 %collective-permute-start.2 = (f32[2,48,256]{2,1,0:T(8,128)S(1)}, f32[2,48,256]{2,1,0:T(8,128)S(1)}, u32[]{:S(2)}, u32[]{:S(2)}) collective-permute-start(f32[2,48,256]{2,1,0:T(8,128)S(1)} %collective-permute-done.1.refs_5_.refs_1_), channel_id=1, source_target_pairs={{0,2},{1,3},{2,0},{3,1},{4,6},{5,7},{6,4},{7,5},{8,10},{9,11},{10,... | collective-permute-start | bytes 294920 | tf_op jit(solution)/shard_map/ppermute | solution.py:348
  29.5 18.0 %collective-permute-start.4 = (f32[2,48,256]{2,1,0:T(8,128)S(1)}, f32[2,48,256]{2,1,0:T(8,128)S(1)}, u32[]{:S(2)}, u32[]{:S(2)}) collective-permute-start(f32[2,48,256]{2,1,0:T(8,128)S(1)} %collective-permute-done.3.refs_6_.refs_2_), channel_id=1, source_target_pairs={{0,2},{1,3},{2,0},{3,1},{4,6},{5,7},{6,4},{7,5},{8,10},{9,11},{10,... | collective-permute-start | bytes 294920 | tf_op jit(solution)/shard_map/ppermute | solution.py:348
  31.0 16.5 %collective-permute-start.6 = (f32[2,48,256]{2,1,0:T(8,128)S(1)}, f32[2,48,256]{2,1,0:T(8,128)S(1)}, u32[]{:S(2)}, u32[]{:S(2)}) collective-permute-start(f32[2,48,256]{2,1,0:T(8,128)S(1)} %collective-permute-done.5.refs_7_.refs_3_), channel_id=1, source_target_pairs={{0,2},{1,3},{2,0},{3,1},{4,6},{5,7},{6,4},{7,5},{8,10},{9,11},{10,... | collective-permute-start | bytes 294920 | tf_op jit(solution)/shard_map/ppermute | solution.py:348
  31.5 7.4 %collective-permute-start.17 = (f32[2,2,48,256]{3,2,1,0:T(8,128)S(1)}, f32[2,2,48,256]{3,2,1,0:T(8,128)S(1)}, u32[]{:S(2)}, u32[]{:S(2)}) collective-permute-start(f32[2,2,48,256]{3,2,1,0:T(8,128)S(1)} %maximum_select_fusion.refs_21_), channel_id=1, source_target_pairs={{0,24},{1,0},{2,26},{3,2},{4,28},{5,4},{6,30},{7,6},{8,9},{9,1},{1... | collective-permute-start | bytes 589832 | tf_op jit(solution)/shard_map/ppermute | solution.py:348
  38.9 5.5 %collective-permute-start.20 = (f32[2,48,256]{2,1,0:T(8,128)S(1)}, f32[2,48,256]{2,1,0:T(8,128)S(1)}, u32[]{:S(2)}, u32[]{:S(2)}) collective-permute-start(f32[2,48,256]{2,1,0:T(8,128)S(1)} %get-tuple-element.44), channel_id=1, source_target_pairs={{0,16},{1,8},{2,18},{3,10},{4,20},{5,12},{6,22},{7,14},{8,17},{9,2... | collective-permute-start | bytes 294920 | tf_op jit(solution)/shard_map/ppermute | solution.py:348
  38.9 12.7 %collective-permute-start.18 = (f32[2,2,48,256]{3,2,1,0:T(8,128)S(1)}, f32[2,2,48,256]{3,2,1,0:T(8,128)S(1)}, u32[]{:S(2)}, u32[]{:S(2)}) collective-permute-start(f32[2,2,48,256]{3,2,1,0:T(8,128)S(1)} %broadcast_select_fusion.refs_9_.refs_0_), channel_id=1, source_target_pairs={{0,4},{1,5},{2,6},{3,7},{4,0},{5,1},{6,2},{7,3},{8,12},{9,13},{10,... | collective-permute-start | bytes 589832 | tf_op jit(solution)/shard_map/ppermute | solution.py:348
  44.4 5.4 %collective-permute-start.21 = (f32[2,48,256]{2,1,0:T(8,128)S(1)}, f32[2,48,256]{2,1,0:T(8,128)S(1)}, u32[]{:S(2)}, u32[]{:S(2)}) collective-permute-start(f32[2,48,256]{2,1,0:T(8,128)S(1)} %collective-permute-done.20.refs_12_.refs_3_), channel_id=1, source_target_pairs={{0,4},{1,5},{2,6},{3,7},{4,0},{5,1},{6,2},{7,3},{8,12},{9,13},{10,... | collective-permute-start | bytes 294920 | tf_op jit(solution)/shard_map/ppermute | solution.py:348
  45.9 5.7 %collective-permute-start.22 = (f32[2,48,256]{2,1,0:T(8,128)S(1)}, f32[2,48,256]{2,1,0:T(8,128)S(1)}, u32[]{:S(2)}, u32[]{:S(2)}) collective-permute-start(f32[2,48,256]{2,1,0:T(8,128)S(1)} %collective-permute-done.20.refs_12_.refs_3_), channel_id=1, source_target_pairs={{0,2},{1,3},{2,0},{3,1},{4,6},{5,7},{6,4},{7,5},{8,10},{9,11},{10,... | collective-permute-start | bytes 294920 | tf_op jit(solution)/shard_map/ppermute | solution.py:348
  47.5 13.7 %collective-permute-start.7 = (f32[4,2,48,256]{3,2,1,0:T(8,128)S(1)}, f32[4,2,48,256]{3,2,1,0:T(8,128)S(1)}, u32[]{:S(2)}, u32[]{:S(2)}) collective-permute-start(f32[4,2,48,256]{3,2,1,0:T(8,128)S(1)} %pad_maximum_fusion.refs_2_), channel_id=1, source_target_pairs={{0,4},{1,5},{2,6},{3,7},{4,0},{5,1},{6,2},{7,3},{8,12},{9,13},{10,... | collective-permute-start | bytes 1179656 | tf_op jit(solution)/shard_map/ppermute | solution.py:348
  48.0 11.2 %collective-permute-start.23 = (f32[2,48,256]{2,1,0:T(8,128)S(1)}, f32[2,48,256]{2,1,0:T(8,128)S(1)}, u32[]{:S(2)}, u32[]{:S(2)}) collective-permute-start(f32[2,48,256]{2,1,0:T(8,128)S(1)} %get-tuple-element.43), channel_id=1, source_target_pairs={{0,16},{1,8},{2,18},{3,10},{4,20},{5,12},{6,22},{7,14},{8,17},{9,2... | collective-permute-start | bytes 294920 | tf_op jit(solution)/shard_map/ppermute | solution.py:348
  49.8 7.8 %collective-permute-start.19 = (f32[2,2,48,256]{3,2,1,0:T(8,128)S(1)}, f32[2,2,48,256]{3,2,1,0:T(8,128)S(1)}, u32[]{:S(2)}, u32[]{:S(2)}) collective-permute-start(f32[2,2,48,256]{3,2,1,0:T(8,128)S(1)} %broadcast_select_fusion.refs_9_.refs_0_), channel_id=1, source_target_pairs={{0,2},{1,3},{2,0},{3,1},{4,6},{5,7},{6,4},{7,5},{8,10},{9,11},{10,... | collective-permute-start | bytes 589832 | tf_op jit(solution)/shard_map/ppermute | solution.py:348
  51.7 15.1 %collective-permute-start.28 = (f32[3,48,256]{2,1,0:T(8,128)S(1)}, f32[3,48,256]{2,1,0:T(8,128)S(1)}, u32[]{:S(2)}, u32[]{:S(2)}) collective-permute-start(f32[3,48,256]{2,1,0:T(8,128)S(1)} %pad_maximum_fusion.2), channel_id=1, source_target_pairs={{0,2},{1,3},{2,0},{3,1},{4,6},{5,7},{6,4},{7,5},{8,10},{9,11},{10,... | collective-permute-start | bytes 442376 | tf_op jit(solution)/shard_map/ppermute | solution.py:348
  57.6 9.1 %collective-permute-start.27 = (f32[3,48,256]{2,1,0:T(8,128)S(1)}, f32[3,48,256]{2,1,0:T(8,128)S(1)}, u32[]{:S(2)}, u32[]{:S(2)}) collective-permute-start(f32[3,48,256]{2,1,0:T(8,128)S(1)} %pad_maximum_fusion.1), channel_id=1, source_target_pairs={{0,4},{1,5},{2,6},{3,7},{4,0},{5,1},{6,2},{7,3},{8,12},{9,13},{10,... | collective-permute-start | bytes 442376 | tf_op jit(solution)/shard_map/ppermute | solution.py:348
  59.2 6.3 %collective-permute-start.24 = (f32[2,48,256]{2,1,0:T(8,128)S(1)}, f32[2,48,256]{2,1,0:T(8,128)S(1)}, u32[]{:S(2)}, u32[]{:S(2)}) collective-permute-start(f32[2,48,256]{2,1,0:T(8,128)S(1)} %collective-permute-done.23.refs_15_.refs_4_), channel_id=1, source_target_pairs={{0,4},{1,5},{2,6},{3,7},{4,0},{5,1},{6,2},{7,3},{8,12},{9,13},{10,... | collective-permute-start | bytes 294920 | tf_op jit(solution)/shard_map/ppermute | solution.py:348
  59.7 5.8 %collective-permute-start.25 = (f32[2,48,256]{2,1,0:T(8,128)S(1)}, f32[2,48,256]{2,1,0:T(8,128)S(1)}, u32[]{:S(2)}, u32[]{:S(2)}) collective-permute-start(f32[2,48,256]{2,1,0:T(8,128)S(1)} %collective-permute-done.23.refs_15_.refs_4_), channel_id=1, source_target_pairs={{0,2},{1,3},{2,0},{3,1},{4,6},{5,7},{6,4},{7,5},{8,10},{9,11},{10,... | collective-permute-start | bytes 294920 | tf_op jit(solution)/shard_map/ppermute | solution.py:348
  61.2 5.5 %collective-permute-start.26 = (f32[2,48,256]{2,1,0:T(8,128)S(1)}, f32[2,48,256]{2,1,0:T(8,128)S(1)}, u32[]{:S(2)}, u32[]{:S(2)}) collective-permute-start(f32[2,48,256]{2,1,0:T(8,128)S(1)} %collective-permute-done.23.refs_15_.refs_4_), channel_id=1, source_target_pairs={{0,6},{1,7},{2,4},{3,5},{4,2},{5,3},{6,0},{7,1},{8,14},{9,15},{10,... | collective-permute-start | bytes 294920 | tf_op jit(solution)/shard_map/ppermute | solution.py:348
  64.9 6.2 %copy-start.1 = (f32[192,384]{1,0:T(8,128)S(1)}, f32[192,384]{1,0:T(8,128)}, u32[]{:S(2)}) copy-start(f32[192,384]{1,0:T(8,128)} %refs_0_.1) | copy-start | bytes 884740
  67.5 5.4 %collective-permute-start.30 = (f32[3,256,256]{2,1,0:T(8,128)S(1)}, f32[3,256,256]{2,1,0:T(8,128)S(1)}, u32[]{:S(2)}, u32[]{:S(2)}) collective-permute-start(f32[3,256,256]{2,1,0:T(8,128)S(1)} %shard_map.42.inner_a), channel_id=1, source_target_pairs={{0,1},{1,0},{2,3},{3,2},{4,5},{5,4},{6,7},{7,6},{8,9},{9,8},{10,11... | collective-permute-start | bytes 2359304 | tf_op jit(solution)/shard_map/ppermute | solution.py:348
  67.6 3.2 %collective-permute-start.13 = (f32[192,512]{1,0:T(8,128)S(1)}, f32[192,512]{1,0:T(8,128)S(1)}, u32[]{:S(2)}, u32[]{:S(2)}) collective-permute-start(f32[192,512]{1,0:T(8,128)S(1)} %get-tuple-element.28.refs_7_), channel_id=1, source_target_pairs={{0,1},{1,0},{2,3},{3,2},{4,5},{5,4},{6,7},{7,6},{8,9},{9,8},{10,11... | collective-permute-start | bytes 1179656 | tf_op jit(solution)/shard_map/ppermute | solution.py:348
  68.1 2.7 %collective-permute-start.12 = (f32[256,256]{1,0:T(8,128)S(1)}, f32[256,256]{1,0:T(8,128)S(1)}, u32[]{:S(2)}, u32[]{:S(2)}) collective-permute-start(f32[256,256]{1,0:T(8,128)S(1)} %get-tuple-element.25.refs_3_), channel_id=1, source_target_pairs={{0,1},{1,0},{2,3},{3,2},{4,5},{5,4},{6,7},{7,6},{8,9},{9,8},{10,11... | collective-permute-start | bytes 786440 | tf_op jit(solution)/shard_map/ppermute | solution.py:348
  68.2 2.9 %collective-permute-start.29 = (f32[2,2,48,256]{3,2,1,0:T(8,128)S(1)}, f32[2,2,48,256]{3,2,1,0:T(8,128)S(1)}, u32[]{:S(2)}, u32[]{:S(2)}) collective-permute-start(f32[2,2,48,256]{3,2,1,0:T(8,128)S(1)} %collective-permute-done.19.refs_11_.refs_2_), channel_id=1, source_target_pairs={{0,1},{1,0},{2,3},{3,2},{4,5},{5,4},{6,7},{7,6},{8,9},{9,8},{10,11... | collective-permute-start | bytes 589832 | tf_op jit(solution)/shard_map/ppermute | solution.py:348

commit v2 on v1

v2 whole, which is shorter than its diff:
```python
import functools

import jax
import jax.numpy as jnp
from jax import lax
from jax.experimental import pallas as pl
from jax.experimental.pallas import tpu as pltpu
from jax.sharding import PartitionSpec as P


highest = lax.Precision.HIGHEST


def from_root(block, axis, owner):
    block = jnp.where(lax.axis_index(axis) == owner, block, jnp.zeros_like(block))
    return lax.psum(block, axis)


def matmul(left, right):
    return jnp.dot(left, right, precision=highest, preferred_element_type=jnp.float32)


def transposed_product(left, right):
    return lax.dot_general(
        left, right, (((0,), (0,)), ((), ())), precision=highest, preferred_element_type=jnp.float32
    )


def outer_product(left, right):
    return lax.dot_general(
        left, right, (((1,), (1,)), ((), ())), precision=highest, preferred_element_type=jnp.float32
    )


def general_device(matrix, panels, factors):
    row_count = lax.axis_size("row")
    col_count = lax.axis_size("col")
    my_row = lax.axis_index("row")
    block_rows = matrix.shape[0]
    share = panels.shape[1]
    source = my_row * col_count // row_count
    offset = share * (my_row * col_count - source * row_count)
    gathered = lax.all_gather(panels, "row", axis=1, tiled=True)
    relayed = from_root(gathered, "col", source)
    current = matrix
    for section in range(panels.shape[0]):
        factor = factors[section]
        panel_cols = gathered[section]
        panel_rows = lax.dynamic_slice_in_dim(relayed[section], offset, block_rows, 0)
        sums_rows = lax.psum(matmul(current, panel_cols), "col")
        sums_cols = lax.psum(transposed_product(current, panel_rows), "row")
        image_rows = matmul(sums_rows, factor)
        image_cols = matmul(sums_cols, factor)
        inner = lax.psum(transposed_product(panel_rows, image_rows), "row")
        correction = transposed_product(factor, inner)
        update_rows = image_rows - 0.5 * matmul(panel_rows, correction)
        update_cols = image_cols - 0.5 * matmul(panel_cols, correction)
        current = (
            current
            - outer_product(panel_rows, update_cols)
            - outer_product(update_rows, panel_cols)
        )
    return current


def apart3(left, right, dims=(1, 0)):
    numbers = (((dims[0],), (dims[1],)), ((), ()))
    one = functools.partial(
        lax.dot_general, dimension_numbers=numbers, preferred_element_type=jnp.float32
    )
    return one(left[0], right[0]) + (one(left[0], right[1]) + one(left[1], right[0]))


def split(value):
    high = value.astype(jnp.bfloat16)
    low = (value - high.astype(jnp.float32)).astype(jnp.bfloat16)
    return high, low


def dot3(left, right, dims=(1, 0)):
    joined_left = jnp.concatenate([left[0], left[0], left[1]], axis=dims[0])
    joined_right = jnp.concatenate([right[0], right[1], right[0]], axis=dims[1])
    numbers = (((dims[0],), (dims[1],)), ((), ()))
    return lax.dot_general(
        joined_left, joined_right, numbers, preferred_element_type=jnp.float32
    )


def place():
    row, col = lax.axis_index("row"), lax.axis_index("col")
    return row // 2, row % 2, col // 2, col % 2


def vmem(count):
    return [pl.BlockSpec(memory_space=pltpu.VMEM)] * count


def call(body, shapes, operands, scratch=(), flops=0, space=pltpu.VMEM):
    moved = sum(4 * o.size for o in operands) + sum(4 * s.size for s in shapes)
    return pl.pallas_call(
        body,
        out_shape=shapes,
        in_specs=[pl.BlockSpec(memory_space=space)] * len(operands),
        out_specs=vmem(len(shapes)),
        scratch_shapes=list(scratch),
        cost_estimate=pl.CostEstimate(flops=flops, bytes_accessed=moved, transcendentals=0),
        compiler_params=pltpu.CompilerParams(vmem_limit_bytes=20 * 1024 * 1024),
    )(*operands)


def prepare_body(matrix_hbm, panels_hbm, factors_hbm, *refs):
    high_ref, low_ref, slab_ref, factor_high, factor_low, tile, factors, sems = refs
    copies = [
        pltpu.make_async_copy(matrix_hbm, tile, sems.at[0]),
        pltpu.make_async_copy(factors_hbm, factors, sems.at[1]),
        pltpu.make_async_copy(panels_hbm, slab_ref, sems.at[2]),
    ]
    for copy in copies:
        copy.start()
    copies[0].wait()
    high_ref[...], low_ref[...] = split(tile[...])
    copies[1].wait()
    factor_high[...], factor_low[...] = split(factors[...])
    copies[2].wait()


def share_of(core, high_a, low_a, panel, factor_high, factor_low, out_ref):
    _, _, x, _ = place()
    _, _, quarter, width = out_ref.shape
    rows = [
        pl.ds(pl.multiple_of((2 * h + core) * quarter, quarter), quarter) for h in (x, 1 - x)
    ]
    tile = [jnp.concatenate([a[r, :] for r in rows], axis=0) for a in (high_a, low_a)]
    product = dot3(tile, panel)
    for step in range(2):
        factor = (factor_high[step], factor_low[step])
        image = dot3(split(product[:, step * width : (step + 1) * width]), factor)
        for side in range(2):
            out_ref[side, step] = image[side * quarter : (side + 1) * quarter]


def give_body(depth, high_a, low_a, factor_high, factor_low, *refs):
    slabs, (give_ref, high, low) = refs[: 2 * depth], refs[2 * depth :]
    z, y, _, k = place()
    share, width = slabs[0].shape[1], slabs[0].shape[2]
    for flip in range(2):
        for shift in range(depth):
            slab = slabs[flip * depth + shift]
            at = 2 * lax.rem(z - shift + depth, depth) + (1 - y if flip else y)
            rows = pl.ds(pl.multiple_of(at * share, share), share)
            for step in range(2):
                h, l = split(slab[step])
                high[rows, step * width : (step + 1) * width] = h
                low[rows, step * width : (step + 1) * width] = l
    panel = (high[...], low[...])
    share_of(1 - k, high_a, low_a, panel, factor_high, factor_low, give_ref)


def keep_body(high_a, low_a, factor_high, factor_low, high, low, keep_ref):
    _, _, _, k = place()
    share_of(k, high_a, low_a, (high[...], low[...]), factor_high, factor_low, keep_ref)


EARLY = (("a", 0), ("b", 0), ("a", 1), ("b", 1), ("a", 2), ("b", 2), ("f", 0), ("f", 1))
LATE = (("a", 3), ("b", 3), ("f", 2), ("f", 3), ("g", 0), ("g", 1), ("g", 2), ("g", 3))


def row_of(depth, kind, flip, quarter):
    z, y, x, k = place()
    owner = z % 2 == k
    if kind in "ab":
        plane = jnp.where(owner, z, lax.rem(z + 1, depth))
    else:
        plane = jnp.where(owner, lax.rem(z + 2, depth), lax.rem(z - 1 + depth, depth))
    core = {"a": k, "b": 1 - k, "f": z % 2, "g": 1 - z % 2}[kind]
    y_from = 1 - y if flip & 1 else y
    x_from = 1 - x if flip & 2 else x
    block = (plane // 2) * 4 + y_from * 2 + x_from
    return pl.multiple_of((2 * block + core) * quarter, quarter)


def fill(image, start, parts):
    for step, part in enumerate(parts):
        quarter, width = part.shape
        image[pl.ds(start, quarter), step * width : (step + 1) * width] = part[...]


def steps(ref):
    return ref.at[0], ref.at[1]


def near_pieces(flip, ref):
    return {("a", flip): steps(ref.at[0]), ("b", flip): steps(ref.at[1])}


def corner_pieces(low, high):
    return {
        ("a", 3): (low.at[0], low.at[1]),
        ("b", 3): (high.at[0], high.at[1]),
        ("f", 3): (low.at[2], high.at[2]),
    }


def panel_body(depth, *refs):
    factor_high, factor_low, across_ref, opposite_ref = refs[:4]
    slabs = refs[4 : 4 + 2 * depth]
    (
        turn1_high, turn1_low, turn2_ref, turn3_high, turn3_low, cross_ref, rows_ref,
         full, turning,
    ) = refs[4 + 2 * depth :]
    z, y, x, _ = place()
    share, width = slabs[0].shape[1], slabs[0].shape[2]
    column = 2 * depth * share
    for across in range(2):
        for flip in range(2):
            for shift in range(depth):
                if across:
                    slab = (opposite_ref if flip else across_ref).at[shift]
                else:
                    slab = slabs[flip * depth + shift]
                at = 2 * lax.rem(z - shift + depth, depth) + (1 - y if flip else y)
                start = (1 - x if across else x) * column + at * share
                fill(full, pl.multiple_of(start, share), steps(slab))
    for at, (kind, flip) in enumerate(EARLY + LATE):
        rows = pl.ds(row_of(depth, kind, flip, share), share)
        turning[at * share : (at + 1) * share, :] = full[rows, :]
    first, second = split(turning[:, :width]), split(turning[:, width:])
    turn1_high[...], turn1_low[...] = split(
        0.5 * dot3((factor_high[0], factor_low[0]), first, (0, 1))
    )
    turn2 = dot3((factor_high[1], factor_low[1]), second, (0, 1))
    turn2_ref[...] = turn2
    turn3_high[...], turn3_low[...] = split(0.5 * turn2)
    cross_ref[...] = dot3(first, second, (0, 0))
    block = 4 * share
    start = (z // 2) * column + y * block
    rows_ref[...] = full[pl.ds(pl.multiple_of(start, block), block), :]


def cross_body(
    factor_high, factor_low, cross_a, cross_b, turn1_high, turn1_low, turn2_ref,
    mixed_high, mixed_low, out_high, out_low,
):
    cross = split(dot3(split(cross_a[...] + cross_b[...]), (factor_high[1], factor_low[1])))
    mixed_high[...], mixed_low[...] = cross
    turned = turn2_ref[...] - dot3(cross, (turn1_high[...], turn1_low[...]), (0, 0))
    out_high[...], out_low[...] = split(turned)


def products(turned, image, span):
    width = image.shape[1] // 2
    high, low = split(image[...])
    for (turn_high, turn_low), p in zip(turned, (0, 0, width)):
        side = slice(p, p + width)
        yield dot3((turn_high[:, span], turn_low[:, span]), (high[:, side], low[:, side]))


def early_body(near, near_y, near_x, f_own, f_y, *refs):
    turned, (inner_ref, image) = refs[:6], refs[6:]
    held = {("f", 0): steps(f_own), ("f", 1): steps(f_y)}
    for flip, ref in enumerate((near, near_y, near_x)):
        held.update(near_pieces(flip, ref))
    quarter = near.shape[2]
    for at, key in enumerate(EARLY):
        fill(image, at * quarter, held[key])
    pairs = (turned[0:2], turned[2:4], turned[4:6])
    for at, value in enumerate(products(pairs, image, slice(0, image.shape[0]))):
        inner_ref[at] = value


def late_body(low, high, f_x, g_own, g_y, g_x, g_d, before, *refs):
    turned, (inner_ref, image) = refs[:6], refs[6:]
    held = {("f", 2): steps(f_x), **corner_pieces(low, high)}
    for flip, ref in enumerate((g_own, g_y, g_x, g_d)):
        held["g", flip] = steps(ref)
    quarter = low.shape[1]
    for at, key in enumerate(LATE):
        fill(image, at * quarter, held[key])
    pairs = (turned[0:2], turned[2:4], turned[4:6])
    span = slice(image.shape[0], 2 * image.shape[0])
    for at, value in enumerate(products(pairs, image, span)):
        inner_ref[at] = before[at] + value


def base_body(depth, *refs):
    (
        matrix_ref, cross_high, cross_low, high_ref, low_ref, panel_a, panel_b,
        near, near_y, near_x, f_own, f_y, f_x, g_own, g_y, g_x, g_d, low, high,
        piece_a, piece_b, far_b, out_ref, rows_high, rows_low, full, image, rows_v,
    ) = refs
    z, _, x, k = place()
    owner = z % 2 == k
    quarter, width = low.shape[1], low.shape[2]
    cols = high_ref.shape[0]
    held = {("f", 0): steps(f_own), ("f", 1): steps(f_y), ("f", 2): steps(f_x)}
    held.update(corner_pieces(low, high))
    for flip, ref in enumerate((near, near_y, near_x)):
        held.update(near_pieces(flip, ref))
    for flip, ref in enumerate((g_own, g_y, g_x, g_d)):
        held["g", flip] = steps(ref)
    for (kind, flip), parts in held.items():
        fill(full, row_of(depth, kind, flip, quarter), parts)
    image[pl.ds(0, cols), :] = full[pl.ds(pl.multiple_of(x * cols, cols), cols), :]

    def row(side, core):
        return pl.multiple_of(cols + (2 * side + core) * quarter, quarter)

    fill(image, row(x, k), steps(piece_a))
    fill(image, row(x, 1 - k), steps(piece_b))

    @pl.when(owner)
    def _():
        for at, core in enumerate((k, 1 - k)):
            fill(image, row(1 - x, core), steps(near_x.at[at]))
        rows_v[...] = panel_a[...]

    @pl.when(jnp.logical_not(owner))
    def _():
        for at, core in enumerate((1 - k, k)):
            fill(image, row(1 - x, core), steps(far_b.at[at]))
        rows_v[...] = panel_b[...]

    first, second = slice(0, width), slice(width, 2 * width)
    w1 = split(image[:, first])
    w2 = split(image[:, second] - dot3(w1, (cross_high[...], cross_low[...])))
    v_rows = split(rows_v[...])
    rows_high[...], rows_low[...] = v_rows
    total = matrix_ref[...]
    for w, at in ((w1, first), (w2, second)):
        v_side = (high_ref[:, at], low_ref[:, at])
        v_top = [v[:, at] for v in v_rows]
        total = total - dot3(v_top, [p[:cols] for p in w], (1, 1))
        total = total - dot3([p[cols:] for p in w], v_side, (1, 1))
    out_ref[...] = total


def update_body(
    base_ref, inner_a, inner_b, cross_high, cross_low, high_ref, low_ref, rows_high, rows_low,
    out_ref,
):
    width = cross_high.shape[0]
    first, second = slice(0, width), slice(width, 2 * width)
    cross = (cross_high[...], cross_low[...])
    v1 = (rows_high[:, first], rows_low[:, first])
    v2 = (rows_high[:, second], rows_low[:, second])
    m1 = inner_a[0] + inner_b[0]
    mixed_t = inner_a[1] + inner_b[1]
    m2 = inner_a[2] + inner_b[2]
    m2 = m2 - apart3(split(mixed_t), cross)
    side = split(mixed_t.T - apart3(split(m1), cross))
    left = apart3(v1, split(m1 + m1.T)) + apart3(v2, side, (1, 1))
    right = apart3(v1, side) + apart3(v2, split(m2 + m2.T))
    out_ref[...] = (
        base_ref[...]
        + apart3(split(left), (high_ref[:, first], low_ref[:, first]), (1, 1))
        + apart3(split(right), (high_ref[:, second], low_ref[:, second]), (1, 1))
    )


def plane_device(matrix, panels, factors):
    row_count, col_count = lax.axis_size("row"), lax.axis_size("col")
    depth = row_count // 2
    z, _, _, k = place()
    owner = z % 2 == k
    f32, bf16 = jnp.float32, jnp.bfloat16
    shape = jax.ShapeDtypeStruct

    def send(value, target):
        pairs = []
        for index in range(row_count * col_count):
            row, col = divmod(index, col_count)
            to = target(row // 2, row % 2, col // 2, col % 2)
            pairs.append((index, (to[0] * 2 + to[1]) * col_count + to[2] * 2 + to[3]))
        return lax.ppermute(value, ("row", "col"), pairs)

    def along_z(shift):
        return lambda z, y, x, k: ((z + shift) % depth, y, x, k)

    def to_y(z, y, x, k):
        return z, 1 - y, x, k

    def to_x(z, y, x, k):
        return z, y, 1 - x, k

    def to_corner(z, y, x, k):
        return z, 1 - y, 1 - x, k

    def to_core(z, y, x, k):
        return z, y, x, 1 - k

    def ahead_first(z, y, x, k):
        return (z + (2 if k == z % 2 else 1)) % depth, y, x, z % 2

    def ahead_second(z, y, x, k):
        return (z + (1 if k == z % 2 else 2)) % depth, y, x, z % 2

    def back_first(z, y, x, k):
        return (z - 1) % depth if k == z % 2 else z, y, x, z % 2

    def back_second(z, y, x, k):
        return (z, y, 1 - x, k) if k == z % 2 else ((z - 1) % depth, y, x, z % 2)

    _, _, width = panels.shape
    block, cols = matrix.shape
    quarter, channel = block // 4, 2 * cols

    high_a, low_a, slab, factor_high, factor_low = call(
        prepare_body,
        [
            shape(matrix.shape, bf16), shape(matrix.shape, bf16), shape(panels.shape, f32),
            shape(factors.shape, bf16), shape(factors.shape, bf16),
        ],
        [matrix, panels, factors],
        [
            pltpu.VMEM(matrix.shape, f32), pltpu.VMEM(factors.shape, f32),
            pltpu.SemaphoreType.DMA((3,)),
        ],
        space=pltpu.HBM,
    )

    order = [2, 1] + list(range(3, depth))
    slabs = {0: slab}
    for shift in order:
        slabs[shift] = send(panels, along_z(shift))
    own = [slabs[s] for s in range(depth)]
    beside = [send(slabs[s], to_y) for s in range(depth)]
    across = [send(slabs[s], to_x) for s in range(depth)]

    share_shape, cols_shape = shape((2, 2, quarter, width), f32), shape((cols, 2 * width), bf16)
    held = [high_a, low_a, factor_high, factor_low]
    give, panel_high, panel_low = call(
        functools.partial(give_body, depth),
        [share_shape, cols_shape, cols_shape],
        [*held, *own, *beside],
        flops=3 * block * cols * width * 2,
    )
    keep = call(
        keep_body, [share_shape], [*held, panel_high, panel_low], flops=3 * block * cols * width * 2
    )[0]
    chip = keep + send(give, to_core)
    piece = chip[0] + send(chip[1], to_x)

    stacked = jnp.stack(across)
    opposite = send(stacked, to_y)
    turn1_high, turn1_low, turn2, turn3_high, turn3_low, cross, panel_rows = call(
        functools.partial(panel_body, depth),
        [
            *[shape((width, channel), bf16)] * 2,
            shape((width, channel), f32),
            *[shape((width, channel), bf16)] * 2,
            shape((width, width), f32),
            shape((block, 2 * width), f32),
        ],
        [factor_high, factor_low, stacked, opposite, *own, *beside],
        [pltpu.VMEM((channel, 2 * width), f32)] * 2,
        flops=6 * channel * width * width * 3,
    )
    cross_other = send(cross, to_core)
    cross_high, cross_low, turn2_high, turn2_low = call(
        cross_body,
        [*[shape((width, width), bf16)] * 2, *[shape((width, channel), bf16)] * 2],
        [factor_high, factor_low, cross, cross_other, turn1_high, turn1_low, turn2],
        flops=6 * channel * width * width,
    )
    turned = [turn1_high, turn1_low, turn2_high, turn2_low, turn3_high, turn3_low]
    panel_rows_other = send(panel_rows, to_core)

    back1, back2 = send(piece, back_first), send(piece, back_second)
    f_own, g_own = send(piece, ahead_first), send(piece, ahead_second)
    near = jnp.where(owner, jnp.stack([piece, back1]), jnp.stack([back1, back2]))
    near_y, near_x = send(near, to_y), send(near, to_x)
    f_y, f_x = send(f_own, to_y), send(f_own, to_x)
    g_y, g_x = send(g_own, to_y), send(g_own, to_x)
    g_d = send(g_own, to_corner)
    low = jnp.concatenate([near_x[0], f_x[:1]])
    high = jnp.concatenate([near_y[1], f_y[1:]])
    low, high = send(low, to_y), send(high, to_x)
    piece_other = send(piece, to_core)
    far_other = send(near_x, to_core)

    inner = call(
        early_body,
        [shape((3, width, width), f32)],
        [near, near_y, near_x, f_own, f_y, *turned],
        [pltpu.VMEM((cols, 2 * width), f32)],
        flops=9 * channel * width * width,
    )[0]
    inner = call(
        late_body,
        [shape((3, width, width), f32)],
        [low, high, f_x, g_own, g_y, g_x, g_d, inner, *turned],
        [pltpu.VMEM((cols, 2 * width), f32)],
        flops=9 * channel * width * width,
    )[0]
    inner_other = send(inner, to_core)
    rows = cols + block
    base, rows_high, rows_low = call(
        functools.partial(base_body, depth),
        [shape((block, cols), f32), *[shape((block, 2 * width), bf16)] * 2],
        [
            matrix, cross_high, cross_low, panel_high, panel_low, panel_rows, panel_rows_other,
            near, near_y, near_x, f_own, f_y, f_x, g_own, g_y, g_x, g_d, low, high,
            piece, piece_other, far_other,
        ],
        [
            pltpu.VMEM((channel, 2 * width), f32), pltpu.VMEM((rows, 2 * width), f32),
            pltpu.VMEM((block, 2 * width), f32),
        ],
        flops=18 * rows * width * width,
    )
    return call(
        update_body,
        [shape((block, cols), f32)],
        [
            base, inner, inner_other, cross_high, cross_low, panel_high, panel_low, rows_high,
            rows_low,
        ],
        flops=18 * rows * width * width,
    )[0]


def per_device(planes, matrix, panels, factors):
    if not planes:
        return general_device(matrix, panels, factors)
    return plane_device(matrix, panels, factors)


def solution(mesh):
    row_count, col_count = mesh.shape["row"], mesh.shape["col"]
    planes = row_count == 2 * col_count and col_count == 4
    return jax.shard_map(
        functools.partial(per_device, planes),
        mesh=mesh,
        in_specs=(P("row", "col"), P(None, ("col", "row"), None), P()),
        out_specs=P("row", "col"),
        check_vma=False,
    )
```

time: 75.7 us -> 72.3 us (0.955)
  waiting for transfers between devices: 27.7 us -> 24.6 us
  starting transfers between devices: 35.6 us -> 33.9 us
  local copies, waits for them, and re-layouts: 2.95 us -> 4.57 us
    ppermute x31 -> x32, waiting for transfers between devices: 27.7 us -> 24.6 us  [send(): return lax.ppermute(value, ('row', 'col'), pairs)]
    ppermute x31 -> x32, starting transfers between devices: 35.6 us -> 33.9 us  [send(): return lax.ppermute(value, ('row', 'col'), pairs)]
    unnamed x8 -> x16, local copies, waits for them, and re-layouts: 2.9 us -> 3.76 us
    slice x2 -> x4, local copies, waits for them, and re-layouts: 0.01 us -> 0.79 us  [the longest x2 0.78 us: plane_device(): low = jnp.concatenate([near_x[0], f_x[:1]])]
    pallas_call x7 -> x9, Pallas kernels: 8.93 us -> 8.59 us  [call(): pl.pallas_call(body, out_shape=shapes, in_specs=[pl.BlockSpec(memory_spac...]
  transfers between devices with their start and end apart: 31 -> 32, of which waited for: 15 -> 18; matrix products, arithmetic and copies ran while one was open for 0% -> 0% of each run, Pallas kernels for 6% -> 7%
where the time goes in v2:
time: 72.3 us; the launch traced here: 72.1 us
  starting transfers between devices  33.9 us (47%)
  waiting for transfers between devices  24.6 us (34%)
  Pallas kernels  8.59 us (12%)
  local copies, waits for them, and re-layouts  4.57 us (6%)
    ppermute x32, starting transfers between devices, send(): return lax.ppermute(value, ('row', 'col'), pairs)  33.9 us
    ppermute x32, waiting for transfers between devices, send(): return lax.ppermute(value, ('row', 'col'), pairs)  24.6 us
    pallas_call x9, Pallas kernels, call(): pl.pallas_call(body, out_shape=shapes, in_specs=[pl.BlockSpec(memory_spac...  8.59 us
    unnamed x16, local copies, waits for them, and re-layouts  3.76 us
  transfers between devices with their start and end apart: 32, of which 18 were waited for; matrix products, arithmetic and copies ran while one was open for 0% of the time, Pallas kernels for 7%

profile of v2, /device:TPU:0, one launch (start us, length us, event | category | flops | bytes accessed | tf_op | source)
XLA Modules:
  0.0 72.1 jit_solution(5193499667208648715)
XLA Ops:
  0.0 3.1 %collective-permute-start.1 = (f32[2,48,256]{2,1,0:T(8,128)}, f32[2,48,256]{2,1,0:T(8,128)S(1)}, u32[]{:S(2)}, u32[]{:S(2)}) collective-permute-start(f32[2,48,256]{2,1,0:T(8,128)} %panels_hbm.1), channel_id=1, source_target_pairs={{0,8},{1,9},{2,10},{3,11},{4,12},{5,13},{6,14},{7,15},{8,16},{9,17... | collective-permute-start | bytes 294920 | tf_op jit(solution)/shard_map/ppermute | solution.py:374
  3.1 2.6 %collective-permute-start.3 = (f32[2,48,256]{2,1,0:T(8,128)}, f32[2,48,256]{2,1,0:T(8,128)S(1)}, u32[]{:S(2)}, u32[]{:S(2)}) collective-permute-start(f32[2,48,256]{2,1,0:T(8,128)} %panels_hbm.1), channel_id=1, source_target_pairs={{0,16},{1,17},{2,18},{3,19},{4,20},{5,21},{6,22},{7,23},{8,24},{9,... | collective-permute-start | bytes 294920 | tf_op jit(solution)/shard_map/ppermute | solution.py:374
  5.6 1.3 %collective-permute-start.5 = (f32[2,48,256]{2,1,0:T(8,128)}, f32[2,48,256]{2,1,0:T(8,128)S(1)}, u32[]{:S(2)}, u32[]{:S(2)}) collective-permute-start(f32[2,48,256]{2,1,0:T(8,128)} %panels_hbm.1), channel_id=1, source_target_pairs={{0,24},{1,25},{2,26},{3,27},{4,28},{5,29},{6,30},{7,31},{8,0},{9,1... | collective-permute-start | bytes 294920 | tf_op jit(solution)/shard_map/ppermute | solution.py:374
  7.0 1.0 %copy-done = f32[192,384]{1,0:T(8,128)S(1)} copy-done((f32[192,384]{1,0:T(8,128)S(1)}, f32[192,384]{1,0:T(8,128)}, u32[]{:S(2)}) %copy-start) | copy-done | bytes 294936
  8.0 1.0 %copy-done.6 = f32[2,256,256]{2,1,0:T(8,128)S(1)} copy-done((f32[2,256,256]{2,1,0:T(8,128)S(1)}, f32[2,256,256]{2,1,0:T(8,128)}, u32[]{:S(2)}) %copy-start.6) | copy-done | bytes 524312
  9.0 0.9 %copy-done.7 = f32[2,48,256]{2,1,0:T(8,128)S(1)} copy-done((f32[2,48,256]{2,1,0:T(8,128)S(1)}, f32[2,48,256]{2,1,0:T(8,128)}, u32[]{:S(2)}) %copy-start.7) | copy-done | bytes 98328
  10.3 1.6 %collective-permute-start.8 = (f32[2,48,256]{2,1,0:T(8,128)S(1)}, f32[2,48,256]{2,1,0:T(8,128)S(1)}, u32[]{:S(2)}, u32[]{:S(2)}) collective-permute-start(f32[2,48,256]{2,1,0:T(8,128)S(1)} %get-tuple-element.29.refs_4_.refs_0_), channel_id=1, source_target_pairs={{0,4},{1,5},{2,6},{3,7},{4,0},{5,1},{6,2},{7,3},{8,12},{9,13},{10,... | collective-permute-start | bytes 294920 | tf_op jit(solution)/shard_map/ppermute | solution.py:374
  12.4 1.5 %collective-permute-start.10 = (f32[2,48,256]{2,1,0:T(8,128)S(1)}, f32[2,48,256]{2,1,0:T(8,128)S(1)}, u32[]{:S(2)}, u32[]{:S(2)}) collective-permute-start(f32[2,48,256]{2,1,0:T(8,128)S(1)} %collective-permute-done.3.refs_6_.refs_2_), channel_id=1, source_target_pairs={{0,4},{1,5},{2,6},{3,7},{4,0},{5,1},{6,2},{7,3},{8,12},{9,13},{10,... | collective-permute-start | bytes 294920 | tf_op jit(solution)/shard_map/ppermute | solution.py:374
  14.5 1.2 %collective-permute-done.8.refs_8_.refs_4_ = f32[2,48,256]{2,1,0:T(8,128)S(1)} collective-permute-done((f32[2,48,256]{2,1,0:T(8,128)S(1)}, f32[2,48,256]{2,1,0:T(8,128)S(1)}, u32[]{:S(2)}, u32[]{:S(2)}) %collective-permute-start.8) | collective-permute-done | bytes 98336 | tf_op jit(solution)/shard_map/ppermute | solution.py:374
  15.6 2.1 %collective-permute-done.9.refs_9_.refs_5_ = f32[2,48,256]{2,1,0:T(8,128)S(1)} collective-permute-done((f32[2,48,256]{2,1,0:T(8,128)S(1)}, f32[2,48,256]{2,1,0:T(8,128)S(1)}, u32[]{:S(2)}, u32[]{:S(2)}) %collective-permute-start.9) | collective-permute-done | bytes 98336 | tf_op jit(solution)/shard_map/ppermute | solution.py:374
  17.7 1.8 %collective-permute-done.10.refs_10_.refs_6_ = f32[2,48,256]{2,1,0:T(8,128)S(1)} collective-permute-done((f32[2,48,256]{2,1,0:T(8,128)S(1)}, f32[2,48,256]{2,1,0:T(8,128)S(1)}, u32[]{:S(2)}, u32[]{:S(2)}) %collective-permute-start.10) | collective-permute-done | bytes 98336 | tf_op jit(solution)/shard_map/ppermute | solution.py:374
  19.5 1.1 %collective-permute-done.11.refs_11_.refs_7_ = f32[2,48,256]{2,1,0:T(8,128)S(1)} collective-permute-done((f32[2,48,256]{2,1,0:T(8,128)S(1)}, f32[2,48,256]{2,1,0:T(8,128)S(1)}, u32[]{:S(2)}, u32[]{:S(2)}) %collective-permute-start.11) | collective-permute-done | bytes 98336 | tf_op jit(solution)/shard_map/ppermute | solution.py:374
  20.6 0.7 shard_map.40
  21.3 1.6 %collective-permute-start = (f32[2,48,256]{2,1,0:T(8,128)S(1)}, f32[2,48,256]{2,1,0:T(8,128)S(1)}, u32[]{:S(2)}, u32[]{:S(2)}) collective-permute-start(f32[2,48,256]{2,1,0:T(8,128)S(1)} %get-tuple-element.29.refs_4_.refs_0_), channel_id=1, source_target_pairs={{0,2},{1,3},{2,0},{3,1},{4,6},{5,7},{6,4},{7,5},{8,10},{9,11},{10,... | collective-permute-start | bytes 294920 | tf_op jit(solution)/shard_map/ppermute | solution.py:374
  23.4 1.5 %collective-permute-start.4 = (f32[2,48,256]{2,1,0:T(8,128)S(1)}, f32[2,48,256]{2,1,0:T(8,128)S(1)}, u32[]{:S(2)}, u32[]{:S(2)}) collective-permute-start(f32[2,48,256]{2,1,0:T(8,128)S(1)} %collective-permute-done.3.refs_6_.refs_2_), channel_id=1, source_target_pairs={{0,2},{1,3},{2,0},{3,1},{4,6},{5,7},{6,4},{7,5},{8,10},{9,11},{10,... | collective-permute-start | bytes 294920 | tf_op jit(solution)/shard_map/ppermute | solution.py:374
  25.4 0.5 shard_map.41
  26.0 1.6 %collective-permute-start.15 = (f32[2,48,256]{2,1,0:T(8,128)S(1)}, f32[2,48,256]{2,1,0:T(8,128)S(1)}, u32[]{:S(2)}, u32[]{:S(2)}) collective-permute-start(f32[2,48,256]{2,1,0:T(8,128)S(1)} %slice_bitcast_fusion.2), channel_id=1, source_target_pairs={{0,2},{1,3},{2,0},{3,1},{4,6},{5,7},{6,4},{7,5},{8,10},{9,11},{10,... | collective-permute-start | bytes 294920 | tf_op jit(solution)/shard_map/ppermute | solution.py:374
  27.6 1.6 %collective-permute-done.6 = f32[2,48,256]{2,1,0:T(8,128)S(1)} collective-permute-done((f32[2,48,256]{2,1,0:T(8,128)S(1)}, f32[2,48,256]{2,1,0:T(8,128)S(1)}, u32[]{:S(2)}, u32[]{:S(2)}) %collective-permute-start.6) | collective-permute-done | bytes 98336 | tf_op jit(solution)/shard_map/ppermute | solution.py:374
  29.1 2.1 %collective-permute-done.4 = f32[2,48,256]{2,1,0:T(8,128)S(1)} collective-permute-done((f32[2,48,256]{2,1,0:T(8,128)S(1)}, f32[2,48,256]{2,1,0:T(8,128)S(1)}, u32[]{:S(2)}, u32[]{:S(2)}) %collective-permute-start.4) | collective-permute-done | bytes 98336 | tf_op jit(solution)/shard_map/ppermute | solution.py:374
  31.2 2.1 %collective-permute-done.2 = f32[2,48,256]{2,1,0:T(8,128)S(1)} collective-permute-done((f32[2,48,256]{2,1,0:T(8,128)S(1)}, f32[2,48,256]{2,1,0:T(8,128)S(1)}, u32[]{:S(2)}, u32[]{:S(2)}) %collective-permute-start.2) | collective-permute-done | bytes 98336 | tf_op jit(solution)/shard_map/ppermute | solution.py:374
  33.4 1.4 %collective-permute-start.7 = (f32[4,2,48,256]{3,2,1,0:T(8,128)S(1)}, f32[4,2,48,256]{3,2,1,0:T(8,128)S(1)}, u32[]{:S(2)}, u32[]{:S(2)}) collective-permute-start(f32[4,2,48,256]{3,2,1,0:T(8,128)S(1)} %pad_maximum_fusion.refs_2_), channel_id=1, source_target_pairs={{0,4},{1,5},{2,6},{3,7},{4,0},{5,1},{6,2},{7,3},{8,12},{9,13},{10,... | collective-permute-start | bytes 1179656 | tf_op jit(solution)/shard_map/ppermute | solution.py:374
  34.9 1.7 %collective-permute-start.16 = (f32[2,48,256]{2,1,0:T(8,128)S(1)}, f32[2,48,256]{2,1,0:T(8,128)S(1)}, u32[]{:S(2)}, u32[]{:S(2)}) collective-permute-start(f32[2,48,256]{2,1,0:T(8,128)S(1)} %fusion.refs_19_), channel_id=1, source_target_pairs={{0,24},{1,0},{2,26},{3,2},{4,28},{5,4},{6,30},{7,6},{8,9},{9,1},{1... | collective-permute-start | bytes 294920 | tf_op jit(solution)/shard_map/ppermute | solution.py:374
  36.6 1.5 %collective-permute-start.17 = (f32[2,48,256]{2,1,0:T(8,128)S(1)}, f32[2,48,256]{2,1,0:T(8,128)S(1)}, u32[]{:S(2)}, u32[]{:S(2)}) collective-permute-start(f32[2,48,256]{2,1,0:T(8,128)S(1)} %fusion.refs_19_), channel_id=1, source_target_pairs={{0,2},{1,24},{2,0},{3,26},{4,6},{5,28},{6,4},{7,30},{8,1},{9,11},{... | collective-permute-start | bytes 294920 | tf_op jit(solution)/shard_map/ppermute | solution.py:374
  38.6 1.2 %collective-permute-done.16 = f32[2,48,256]{2,1,0:T(8,128)S(1)} collective-permute-done((f32[2,48,256]{2,1,0:T(8,128)S(1)}, f32[2,48,256]{2,1,0:T(8,128)S(1)}, u32[]{:S(2)}, u32[]{:S(2)}) %collective-permute-start.16) | collective-permute-done | bytes 98336 | tf_op jit(solution)/shard_map/ppermute | solution.py:374
  39.9 1.4 %collective-permute-done.17 = f32[2,48,256]{2,1,0:T(8,128)S(1)} collective-permute-done((f32[2,48,256]{2,1,0:T(8,128)S(1)}, f32[2,48,256]{2,1,0:T(8,128)S(1)}, u32[]{:S(2)}, u32[]{:S(2)}) %collective-permute-start.17) | collective-permute-done | bytes 98336 | tf_op jit(solution)/shard_map/ppermute | solution.py:374
  41.3 1.6 %collective-permute-start.19 = (f32[2,2,48,256]{3,2,1,0:T(8,128)S(1)}, f32[2,2,48,256]{3,2,1,0:T(8,128)S(1)}, u32[]{:S(2)}, u32[]{:S(2)}) collective-permute-start(f32[2,2,48,256]{3,2,1,0:T(8,128)S(1)} %maximum_select_fusion.refs_7_.near), channel_id=1, source_target_pairs={{0,2},{1,3},{2,0},{3,1},{4,6},{5,7},{6,4},{7,5},{8,10},{9,11},{10,... | collective-permute-start | bytes 589832 | tf_op jit(solution)/shard_map/ppermute | solution.py:374
  42.8 1.1 %collective-permute-done.20.refs_10_.f_own = f32[2,48,256]{2,1,0:T(8,128)S(1)} collective-permute-done((f32[2,48,256]{2,1,0:T(8,128)S(1)}, f32[2,48,256]{2,1,0:T(8,128)S(1)}, u32[]{:S(2)}, u32[]{:S(2)}) %collective-permute-start.20) | collective-permute-done | bytes 98336 | tf_op jit(solution)/shard_map/ppermute | solution.py:374
  43.9 1.3 %collective-permute-start.22 = (f32[2,48,256]{2,1,0:T(8,128)S(1)}, f32[2,48,256]{2,1,0:T(8,128)S(1)}, u32[]{:S(2)}, u32[]{:S(2)}) collective-permute-start(f32[2,48,256]{2,1,0:T(8,128)S(1)} %collective-permute-done.20.refs_10_.f_own), channel_id=1, source_target_pairs={{0,2},{1,3},{2,0},{3,1},{4,6},{5,7},{6,4},{7,5},{8,10},{9,11},{10,... | collective-permute-start | bytes 294920 | tf_op jit(solution)/shard_map/ppermute | solution.py:374
  45.2 1.0 %collective-permute-start.21 = (f32[2,48,256]{2,1,0:T(8,128)S(1)}, f32[2,48,256]{2,1,0:T(8,128)S(1)}, u32[]{:S(2)}, u32[]{:S(2)}) collective-permute-start(f32[2,48,256]{2,1,0:T(8,128)S(1)} %collective-permute-done.20.refs_10_.f_own), channel_id=1, source_target_pairs={{0,4},{1,5},{2,6},{3,7},{4,0},{5,1},{6,2},{7,3},{8,12},{9,13},{10,... | collective-permute-start | bytes 294920 | tf_op jit(solution)/shard_map/ppermute | solution.py:374
  46.3 1.0 %collective-permute-start.18 = (f32[2,2,48,256]{3,2,1,0:T(8,128)S(1)}, f32[2,2,48,256]{3,2,1,0:T(8,128)S(1)}, u32[]{:S(2)}, u32[]{:S(2)}) collective-permute-start(f32[2,2,48,256]{3,2,1,0:T(8,128)S(1)} %maximum_select_fusion.refs_7_.near), channel_id=1, source_target_pairs={{0,4},{1,5},{2,6},{3,7},{4,0},{5,1},{6,2},{7,3},{8,12},{9,13},{10,... | collective-permute-start | bytes 589832 | tf_op jit(solution)/shard_map/ppermute | solution.py:374
  47.3 1.3 %shard_map.38 = (bf16[256,768]{1,0:T(8,128)(2,1)S(1)}, bf16[256,768]{1,0:T(8,128)(2,1)S(1)}, f32[256,768]{1,0:T(8,128)S(1)}, bf16[256,768]{1,0:T(8,128)(2,1)S(1)...) custom-call(bf16[2,256,256]{2,1,0:T(8,128)(2,1)S(1)} %get-tuple-element.27.refs_0_.factor_high, ...), custom_call_target="tpu_custom_call" | custom-call | flops 905969664 | bytes 7208960 | tf_op jit(solution)/shard_map/pallas_call | solution.py:100
  48.5 0.6 collective-permute-done.22.refs_12_.f_x
  49.8 0.6 copy-done.4
  50.5 0.8 %slice-done = f32[1,48,256]{2,1,0:T(8,128)S(1)} async-done(((f32[2,48,256]{2,1,0:T(8,128)}), f32[1,48,256]{2,1,0:T(8,128)S(1)}, s32[]{:S(2)}) %slice-start) | async-done | bytes 49176 | tf_op jit(solution)/shard_map/slice | solution.py:475
  51.3 1.1 %collective-permute-start.27 = (f32[3,48,256]{2,1,0:T(8,128)S(1)}, f32[3,48,256]{2,1,0:T(8,128)S(1)}, u32[]{:S(2)}, u32[]{:S(2)}) collective-permute-start(f32[3,48,256]{2,1,0:T(8,128)S(1)} %pad_maximum_fusion.1), channel_id=1, source_target_pairs={{0,4},{1,5},{2,6},{3,7},{4,0},{5,1},{6,2},{7,3},{8,12},{9,13},{10,... | collective-permute-start | bytes 442376 | tf_op jit(solution)/shard_map/ppermute | solution.py:374
  52.4 1.4 %collective-permute-done.18.refs_8_.near_y = f32[2,2,48,256]{3,2,1,0:T(8,128)S(1)} collective-permute-done((f32[2,2,48,256]{3,2,1,0:T(8,128)S(1)}, f32[2,2,48,256]{3,2,1,0:T(8,128)S(1)}, u32[]{:S(2)}, u32[]{:S(2)}) %collective-permute-start.18) | collective-permute-done | bytes 196640 | tf_op jit(solution)/shard_map/ppermute | solution.py:374
  53.9 0.9 %collective-permute-start.28 = (f32[3,48,256]{2,1,0:T(8,128)S(1)}, f32[3,48,256]{2,1,0:T(8,128)S(1)}, u32[]{:S(2)}, u32[]{:S(2)}) collective-permute-start(f32[3,48,256]{2,1,0:T(8,128)S(1)} %pad_maximum_fusion.2), channel_id=1, source_target_pairs={{0,2},{1,3},{2,0},{3,1},{4,6},{5,7},{6,4},{7,5},{8,10},{9,11},{10,... | collective-permute-start | bytes 442376 | tf_op jit(solution)/shard_map/ppermute | solution.py:374
  54.8 1.1 %collective-permute-start.24 = (f32[2,48,256]{2,1,0:T(8,128)S(1)}, f32[2,48,256]{2,1,0:T(8,128)S(1)}, u32[]{:S(2)}, u32[]{:S(2)}) collective-permute-start(f32[2,48,256]{2,1,0:T(8,128)S(1)} %collective-permute-done.23.refs_13_.g_own), channel_id=1, source_target_pairs={{0,4},{1,5},{2,6},{3,7},{4,0},{5,1},{6,2},{7,3},{8,12},{9,13},{10,... | collective-permute-start | bytes 294920 | tf_op jit(solution)/shard_map/ppermute | solution.py:374
  55.9 1.1 %collective-permute-start.25 = (f32[2,48,256]{2,1,0:T(8,128)S(1)}, f32[2,48,256]{2,1,0:T(8,128)S(1)}, u32[]{:S(2)}, u32[]{:S(2)}) collective-permute-start(f32[2,48,256]{2,1,0:T(8,128)S(1)} %collective-permute-done.23.refs_13_.g_own), channel_id=1, source_target_pairs={{0,2},{1,3},{2,0},{3,1},{4,6},{5,7},{6,4},{7,5},{8,10},{9,11},{10,... | collective-permute-start | bytes 294920 | tf_op jit(solution)/shard_map/ppermute | solution.py:374
  57.0 1.2 %collective-permute-start.26 = (f32[2,48,256]{2,1,0:T(8,128)S(1)}, f32[2,48,256]{2,1,0:T(8,128)S(1)}, u32[]{:S(2)}, u32[]{:S(2)}) collective-permute-start(f32[2,48,256]{2,1,0:T(8,128)S(1)} %collective-permute-done.23.refs_13_.g_own), channel_id=1, source_target_pairs={{0,6},{1,7},{2,4},{3,5},{4,2},{5,3},{6,0},{7,1},{8,14},{9,15},{10,... | collective-permute-start | bytes 294920 | tf_op jit(solution)/shard_map/ppermute | solution.py:374
  58.3 0.9 %shard_map.39 = (bf16[256,256]{1,0:T(8,128)(2,1)S(1)}, bf16[256,256]{1,0:T(8,128)(2,1)S(1)}, bf16[256,768]{1,0:T(8,128)(2,1)S(1)}, bf16[256,768]{1,0:T(8,128)(2,1)S(1)}) custom-call(bf16[2,256,256]{2,1,0:T(8,128)(2,1)S(1)} %get-tuple-element.27.refs_0_.factor_high, bf16[2,256,256]{2,1,0:T(8,128)(2,1)S(1)} %get-tuple-element.28.refs_1_.factor_low, ...), custom_call_target="tpu_custom_call" | custom-call | flops 301989888 | bytes 6029312 | tf_op jit(solution)/shard_map/pallas_call | solution.py:100
  59.3 0.7 shard_map.43.before
  60.0 2.8 %collective-permute-done.25.refs_15_.g_x = f32[2,48,256]{2,1,0:T(8,128)S(1)} collective-permute-done((f32[2,48,256]{2,1,0:T(8,128)S(1)}, f32[2,48,256]{2,1,0:T(8,128)S(1)}, u32[]{:S(2)}, u32[]{:S(2)}) %collective-permute-start.25) | collective-permute-done | bytes 98336 | tf_op jit(solution)/shard_map/ppermute | solution.py:374
  62.8 1.8 %collective-permute-done.26.refs_16_.g_d = f32[2,48,256]{2,1,0:T(8,128)S(1)} collective-permute-done((f32[2,48,256]{2,1,0:T(8,128)S(1)}, f32[2,48,256]{2,1,0:T(8,128)S(1)}, u32[]{:S(2)}, u32[]{:S(2)}) %collective-permute-start.26) | collective-permute-done | bytes 98336 | tf_op jit(solution)/shard_map/ppermute | solution.py:374
  64.5 0.7 shard_map.44.inner_a
  66.3 2.2 %collective-permute-done.29.refs_20_ = f32[2,48,256]{2,1,0:T(8,128)S(1)} collective-permute-done((f32[2,48,256]{2,1,0:T(8,128)S(1)}, f32[2,48,256]{2,1,0:T(8,128)S(1)}, u32[]{:S(2)}, u32[]{:S(2)}) %collective-permute-start.29) | collective-permute-done | bytes 98336 | tf_op jit(solution)/shard_map/ppermute | solution.py:374
  68.6 1.4 %shard_map.42 = (f32[192,384]{1,0:T(8,128)S(1)}, bf16[192,512]{1,0:T(8,128)(2,1)S(1)}, bf16[192,512]{1,0:T(8,128)(2,1)S(1)}) custom-call(f32[192,384]{1,0:T(8,128)S(1)} %copy-done.1, bf16[256,256]{1,0:T(8,128)(2,1)S(1)} %get-tuple-element.34.refs_1_.cross_high, bf16[256,256]{1,0:T(8,128)(2,1)S(1)} %get-tuple-element.35.refs_2_.cross_low, ...), custom_call_target="tpu_custom_call" | custom-call | flops 679477248 | bytes 6225920 | tf_op jit(solution)/shard_map/pallas_call | solution.py:100
  70.0 2.0 %shard_map.45 = f32[192,384]{1,0:T(8,128)} custom-call(f32[192,384]{1,0:T(8,128)S(1)} %get-tuple-element.42.base_ref, f32[3,256,256]{2,1,0:T(8,128)S(1)} %shard_map.44.inner_a, f32[3,256,256]{2,1,0:T(8,128)S(1)} %collective-permute-done.31.inner_b, bf16[256,256]{1,0:T(8,128)(2,1)S(1)} %get-tuple-element.34.refs_1_.cross_high, ...), custom_call_target="tpu_custom_call" | custom-call | flops 679477248 | bytes 5046272 | tf_op jit(solution)/shard_map/pallas_call | solution.py:100
  (54 shorter events, 5.3 us)
Async XLA Ops:
  0.0 11.9 %collective-permute-start.1 = (f32[2,48,256]{2,1,0:T(8,128)}, f32[2,48,256]{2,1,0:T(8,128)S(1)}, u32[]{:S(2)}, u32[]{:S(2)}) collective-permute-start(f32[2,48,256]{2,1,0:T(8,128)} %panels_hbm.1), channel_id=1, source_target_pairs={{0,8},{1,9},{2,10},{3,11},{4,12},{5,13},{6,14},{7,15},{8,16},{9,17... | collective-permute-start | bytes 294920 | tf_op jit(solution)/shard_map/ppermute | solution.py:374
  3.1 9.4 %collective-permute-start.3 = (f32[2,48,256]{2,1,0:T(8,128)}, f32[2,48,256]{2,1,0:T(8,128)S(1)}, u32[]{:S(2)}, u32[]{:S(2)}) collective-permute-start(f32[2,48,256]{2,1,0:T(8,128)} %panels_hbm.1), channel_id=1, source_target_pairs={{0,16},{1,17},{2,18},{3,19},{4,20},{5,21},{6,22},{7,23},{8,24},{9,... | collective-permute-start | bytes 294920 | tf_op jit(solution)/shard_map/ppermute | solution.py:374
  5.6 8.3 %collective-permute-start.5 = (f32[2,48,256]{2,1,0:T(8,128)}, f32[2,48,256]{2,1,0:T(8,128)S(1)}, u32[]{:S(2)}, u32[]{:S(2)}) collective-permute-start(f32[2,48,256]{2,1,0:T(8,128)} %panels_hbm.1), channel_id=1, source_target_pairs={{0,24},{1,25},{2,26},{3,27},{4,28},{5,29},{6,30},{7,31},{8,0},{9,1... | collective-permute-start | bytes 294920 | tf_op jit(solution)/shard_map/ppermute | solution.py:374
  7.0 1.0 %copy-start = (f32[192,384]{1,0:T(8,128)S(1)}, f32[192,384]{1,0:T(8,128)}, u32[]{:S(2)}) copy-start(f32[192,384]{1,0:T(8,128)} %refs_0_.1) | copy-start | bytes 884740
  8.0 1.0 %copy-start.6 = (f32[2,256,256]{2,1,0:T(8,128)S(1)}, f32[2,256,256]{2,1,0:T(8,128)}, u32[]{:S(2)}) copy-start(f32[2,256,256]{2,1,0:T(8,128)} %factors_hbm.1) | copy-start | bytes 1572868
  9.0 0.9 %copy-start.7 = (f32[2,48,256]{2,1,0:T(8,128)S(1)}, f32[2,48,256]{2,1,0:T(8,128)}, u32[]{:S(2)}) copy-start(f32[2,48,256]{2,1,0:T(8,128)} %panels_hbm.1) | copy-start | bytes 294916
  10.3 5.3 %collective-permute-start.8 = (f32[2,48,256]{2,1,0:T(8,128)S(1)}, f32[2,48,256]{2,1,0:T(8,128)S(1)}, u32[]{:S(2)}, u32[]{:S(2)}) collective-permute-start(f32[2,48,256]{2,1,0:T(8,128)S(1)} %get-tuple-element.29.refs_4_.refs_0_), channel_id=1, source_target_pairs={{0,4},{1,5},{2,6},{3,7},{4,0},{5,1},{6,2},{7,3},{8,12},{9,13},{10,... | collective-permute-start | bytes 294920 | tf_op jit(solution)/shard_map/ppermute | solution.py:374
  11.9 5.9 %collective-permute-start.9 = (f32[2,48,256]{2,1,0:T(8,128)S(1)}, f32[2,48,256]{2,1,0:T(8,128)S(1)}, u32[]{:S(2)}, u32[]{:S(2)}) collective-permute-start(f32[2,48,256]{2,1,0:T(8,128)S(1)} %collective-permute-done.1.refs_5_.refs_1_), channel_id=1, source_target_pairs={{0,4},{1,5},{2,6},{3,7},{4,0},{5,1},{6,2},{7,3},{8,12},{9,13},{10,... | collective-permute-start | bytes 294920 | tf_op jit(solution)/shard_map/ppermute | solution.py:374
  12.4 7.1 %collective-permute-start.10 = (f32[2,48,256]{2,1,0:T(8,128)S(1)}, f32[2,48,256]{2,1,0:T(8,128)S(1)}, u32[]{:S(2)}, u32[]{:S(2)}) collective-permute-start(f32[2,48,256]{2,1,0:T(8,128)S(1)} %collective-permute-done.3.refs_6_.refs_2_), channel_id=1, source_target_pairs={{0,4},{1,5},{2,6},{3,7},{4,0},{5,1},{6,2},{7,3},{8,12},{9,13},{10,... | collective-permute-start | bytes 294920 | tf_op jit(solution)/shard_map/ppermute | solution.py:374
  14.0 6.6 %collective-permute-start.11 = (f32[2,48,256]{2,1,0:T(8,128)S(1)}, f32[2,48,256]{2,1,0:T(8,128)S(1)}, u32[]{:S(2)}, u32[]{:S(2)}) collective-permute-start(f32[2,48,256]{2,1,0:T(8,128)S(1)} %collective-permute-done.5.refs_7_.refs_3_), channel_id=1, source_target_pairs={{0,4},{1,5},{2,6},{3,7},{4,0},{5,1},{6,2},{7,3},{8,12},{9,13},{10,... | collective-permute-start | bytes 294920 | tf_op jit(solution)/shard_map/ppermute | solution.py:374
  21.2 4.7 %collective-permute-start.14 = (f32[2,2,48,256]{3,2,1,0:T(8,128)S(1)}, f32[2,2,48,256]{3,2,1,0:T(8,128)S(1)}, u32[]{:S(2)}, u32[]{:S(2)}) collective-permute-start(f32[2,2,48,256]{3,2,1,0:T(8,128)S(1)} %get-tuple-element.41), channel_id=1, source_target_pairs={{0,1},{1,0},{2,3},{3,2},{4,5},{5,4},{6,7},{7,6},{8,9},{9,8},{10,11... | collective-permute-start | bytes 589832 | tf_op jit(solution)/shard_map/ppermute | solution.py:374
  21.3 6.3 %collective-permute-start = (f32[2,48,256]{2,1,0:T(8,128)S(1)}, f32[2,48,256]{2,1,0:T(8,128)S(1)}, u32[]{:S(2)}, u32[]{:S(2)}) collective-permute-start(f32[2,48,256]{2,1,0:T(8,128)S(1)} %get-tuple-element.29.refs_4_.refs_0_), channel_id=1, source_target_pairs={{0,2},{1,3},{2,0},{3,1},{4,6},{5,7},{6,4},{7,5},{8,10},{9,11},{10,... | collective-permute-start | bytes 294920 | tf_op jit(solution)/shard_map/ppermute | solution.py:374
  22.9 6.3 %collective-permute-start.6 = (f32[2,48,256]{2,1,0:T(8,128)S(1)}, f32[2,48,256]{2,1,0:T(8,128)S(1)}, u32[]{:S(2)}, u32[]{:S(2)}) collective-permute-start(f32[2,48,256]{2,1,0:T(8,128)S(1)} %collective-permute-done.5.refs_7_.refs_3_), channel_id=1, source_target_pairs={{0,2},{1,3},{2,0},{3,1},{4,6},{5,7},{6,4},{7,5},{8,10},{9,11},{10,... | collective-permute-start | bytes 294920 | tf_op jit(solution)/shard_map/ppermute | solution.py:374
  23.4 7.9 %collective-permute-start.4 = (f32[2,48,256]{2,1,0:T(8,128)S(1)}, f32[2,48,256]{2,1,0:T(8,128)S(1)}, u32[]{:S(2)}, u32[]{:S(2)}) collective-permute-start(f32[2,48,256]{2,1,0:T(8,128)S(1)} %collective-permute-done.3.refs_6_.refs_2_), channel_id=1, source_target_pairs={{0,2},{1,3},{2,0},{3,1},{4,6},{5,7},{6,4},{7,5},{8,10},{9,11},{10,... | collective-permute-start | bytes 294920 | tf_op jit(solution)/shard_map/ppermute | solution.py:374
  24.9 8.5 %collective-permute-start.2 = (f32[2,48,256]{2,1,0:T(8,128)S(1)}, f32[2,48,256]{2,1,0:T(8,128)S(1)}, u32[]{:S(2)}, u32[]{:S(2)}) collective-permute-start(f32[2,48,256]{2,1,0:T(8,128)S(1)} %collective-permute-done.1.refs_5_.refs_1_), channel_id=1, source_target_pairs={{0,2},{1,3},{2,0},{3,1},{4,6},{5,7},{6,4},{7,5},{8,10},{9,11},{10,... | collective-permute-start | bytes 294920 | tf_op jit(solution)/shard_map/ppermute | solution.py:374
  26.0 8.9 %collective-permute-start.15 = (f32[2,48,256]{2,1,0:T(8,128)S(1)}, f32[2,48,256]{2,1,0:T(8,128)S(1)}, u32[]{:S(2)}, u32[]{:S(2)}) collective-permute-start(f32[2,48,256]{2,1,0:T(8,128)S(1)} %slice_bitcast_fusion.2), channel_id=1, source_target_pairs={{0,2},{1,3},{2,0},{3,1},{4,6},{5,7},{6,4},{7,5},{8,10},{9,11},{10,... | collective-permute-start | bytes 294920 | tf_op jit(solution)/shard_map/ppermute | solution.py:374
  33.4 12.9 %collective-permute-start.7 = (f32[4,2,48,256]{3,2,1,0:T(8,128)S(1)}, f32[4,2,48,256]{3,2,1,0:T(8,128)S(1)}, u32[]{:S(2)}, u32[]{:S(2)}) collective-permute-start(f32[4,2,48,256]{3,2,1,0:T(8,128)S(1)} %pad_maximum_fusion.refs_2_), channel_id=1, source_target_pairs={{0,4},{1,5},{2,6},{3,7},{4,0},{5,1},{6,2},{7,3},{8,12},{9,13},{10,... | collective-permute-start | bytes 1179656 | tf_op jit(solution)/shard_map/ppermute | solution.py:374
  34.9 4.9 %collective-permute-start.16 = (f32[2,48,256]{2,1,0:T(8,128)S(1)}, f32[2,48,256]{2,1,0:T(8,128)S(1)}, u32[]{:S(2)}, u32[]{:S(2)}) collective-permute-start(f32[2,48,256]{2,1,0:T(8,128)S(1)} %fusion.refs_19_), channel_id=1, source_target_pairs={{0,24},{1,0},{2,26},{3,2},{4,28},{5,4},{6,30},{7,6},{8,9},{9,1},{1... | collective-permute-start | bytes 294920 | tf_op jit(solution)/shard_map/ppermute | solution.py:374
  36.6 4.6 %collective-permute-start.17 = (f32[2,48,256]{2,1,0:T(8,128)S(1)}, f32[2,48,256]{2,1,0:T(8,128)S(1)}, u32[]{:S(2)}, u32[]{:S(2)}) collective-permute-start(f32[2,48,256]{2,1,0:T(8,128)S(1)} %fusion.refs_19_), channel_id=1, source_target_pairs={{0,2},{1,24},{2,0},{3,26},{4,6},{5,28},{6,4},{7,30},{8,1},{9,11},{... | collective-permute-start | bytes 294920 | tf_op jit(solution)/shard_map/ppermute | solution.py:374
  38.1 5.8 %collective-permute-start.20 = (f32[2,48,256]{2,1,0:T(8,128)S(1)}, f32[2,48,256]{2,1,0:T(8,128)S(1)}, u32[]{:S(2)}, u32[]{:S(2)}) collective-permute-start(f32[2,48,256]{2,1,0:T(8,128)S(1)} %fusion.refs_19_), channel_id=1, source_target_pairs={{0,16},{1,8},{2,18},{3,10},{4,20},{5,12},{6,22},{7,14},{8,17},{9,2... | collective-permute-start | bytes 294920 | tf_op jit(solution)/shard_map/ppermute | solution.py:374
  41.3 9.2 %collective-permute-start.19 = (f32[2,2,48,256]{3,2,1,0:T(8,128)S(1)}, f32[2,2,48,256]{3,2,1,0:T(8,128)S(1)}, u32[]{:S(2)}, u32[]{:S(2)}) collective-permute-start(f32[2,2,48,256]{3,2,1,0:T(8,128)S(1)} %maximum_select_fusion.refs_7_.near), channel_id=1, source_target_pairs={{0,2},{1,3},{2,0},{3,1},{4,6},{5,7},{6,4},{7,5},{8,10},{9,11},{10,... | collective-permute-start | bytes 589832 | tf_op jit(solution)/shard_map/ppermute | solution.py:374
  43.9 5.2 %collective-permute-start.22 = (f32[2,48,256]{2,1,0:T(8,128)S(1)}, f32[2,48,256]{2,1,0:T(8,128)S(1)}, u32[]{:S(2)}, u32[]{:S(2)}) collective-permute-start(f32[2,48,256]{2,1,0:T(8,128)S(1)} %collective-permute-done.20.refs_10_.f_own), channel_id=1, source_target_pairs={{0,2},{1,3},{2,0},{3,1},{4,6},{5,7},{6,4},{7,5},{8,10},{9,11},{10,... | collective-permute-start | bytes 294920 | tf_op jit(solution)/shard_map/ppermute | solution.py:374
  45.2 4.6 %collective-permute-start.21 = (f32[2,48,256]{2,1,0:T(8,128)S(1)}, f32[2,48,256]{2,1,0:T(8,128)S(1)}, u32[]{:S(2)}, u32[]{:S(2)}) collective-permute-start(f32[2,48,256]{2,1,0:T(8,128)S(1)} %collective-permute-done.20.refs_10_.f_own), channel_id=1, source_target_pairs={{0,4},{1,5},{2,6},{3,7},{4,0},{5,1},{6,2},{7,3},{8,12},{9,13},{10,... | collective-permute-start | bytes 294920 | tf_op jit(solution)/shard_map/ppermute | solution.py:374
  46.3 8.5 %collective-permute-start.23 = (f32[2,48,256]{2,1,0:T(8,128)S(1)}, f32[2,48,256]{2,1,0:T(8,128)S(1)}, u32[]{:S(2)}, u32[]{:S(2)}) collective-permute-start(f32[2,48,256]{2,1,0:T(8,128)S(1)} %fusion.refs_19_), channel_id=1, source_target_pairs={{0,8},{1,16},{2,10},{3,18},{4,12},{5,20},{6,14},{7,22},{8,25},{9,1... | collective-permute-start | bytes 294920 | tf_op jit(solution)/shard_map/ppermute | solution.py:374
  46.3 7.6 %collective-permute-start.18 = (f32[2,2,48,256]{3,2,1,0:T(8,128)S(1)}, f32[2,2,48,256]{3,2,1,0:T(8,128)S(1)}, u32[]{:S(2)}, u32[]{:S(2)}) collective-permute-start(f32[2,2,48,256]{3,2,1,0:T(8,128)S(1)} %maximum_select_fusion.refs_7_.near), channel_id=1, source_target_pairs={{0,4},{1,5},{2,6},{3,7},{4,0},{5,1},{6,2},{7,3},{8,12},{9,13},{10,... | collective-permute-start | bytes 589832 | tf_op jit(solution)/shard_map/ppermute | solution.py:374
  49.1 0.6 copy-start.2
  49.1 7.9 %collective-permute-start.12 = (f32[256,256]{1,0:T(8,128)S(1)}, f32[256,256]{1,0:T(8,128)S(1)}, u32[]{:S(2)}, u32[]{:S(2)}) collective-permute-start(f32[256,256]{1,0:T(8,128)S(1)} %get-tuple-element.30.cross_a), channel_id=1, source_target_pairs={{0,1},{1,0},{2,3},{3,2},{4,5},{5,4},{6,7},{7,6},{8,9},{9,8},{10,11... | collective-permute-start | bytes 786440 | tf_op jit(solution)/shard_map/ppermute | solution.py:374
  49.8 0.6 copy-start.4
  50.5 0.8 %slice-start = ((f32[2,48,256]{2,1,0:T(8,128)}), f32[1,48,256]{2,1,0:T(8,128)S(1)}, s32[]{:S(2)}) async-start(f32[2,48,256]{2,1,0:T(8,128)} %copy-done.2), calls=%async_computation | async-start | bytes 98304 | tf_op jit(solution)/shard_map/slice | solution.py:475
  51.3 2.6 %slice-start.1 = ((f32[2,48,256]{2,1,0:T(8,128)}), f32[1,48,256]{2,1,0:T(8,128)S(1)}, s32[]{:S(2)}) async-start(f32[2,48,256]{2,1,0:T(8,128)} %copy-done.4), calls=%async_computation.1 | async-start | bytes 98304 | tf_op jit(solution)/shard_map/slice | solution.py:476
  51.3 13.2 %collective-permute-start.27 = (f32[3,48,256]{2,1,0:T(8,128)S(1)}, f32[3,48,256]{2,1,0:T(8,128)S(1)}, u32[]{:S(2)}, u32[]{:S(2)}) collective-permute-start(f32[3,48,256]{2,1,0:T(8,128)S(1)} %pad_maximum_fusion.1), channel_id=1, source_target_pairs={{0,4},{1,5},{2,6},{3,7},{4,0},{5,1},{6,2},{7,3},{8,12},{9,13},{10,... | collective-permute-start | bytes 442376 | tf_op jit(solution)/shard_map/ppermute | solution.py:374
  53.9 10.7 %collective-permute-start.28 = (f32[3,48,256]{2,1,0:T(8,128)S(1)}, f32[3,48,256]{2,1,0:T(8,128)S(1)}, u32[]{:S(2)}, u32[]{:S(2)}) collective-permute-start(f32[3,48,256]{2,1,0:T(8,128)S(1)} %pad_maximum_fusion.2), channel_id=1, source_target_pairs={{0,2},{1,3},{2,0},{3,1},{4,6},{5,7},{6,4},{7,5},{8,10},{9,11},{10,... | collective-permute-start | bytes 442376 | tf_op jit(solution)/shard_map/ppermute | solution.py:374
  54.8 5.2 %collective-permute-start.24 = (f32[2,48,256]{2,1,0:T(8,128)S(1)}, f32[2,48,256]{2,1,0:T(8,128)S(1)}, u32[]{:S(2)}, u32[]{:S(2)}) collective-permute-start(f32[2,48,256]{2,1,0:T(8,128)S(1)} %collective-permute-done.23.refs_13_.g_own), channel_id=1, source_target_pairs={{0,4},{1,5},{2,6},{3,7},{4,0},{5,1},{6,2},{7,3},{8,12},{9,13},{10,... | collective-permute-start | bytes 294920 | tf_op jit(solution)/shard_map/ppermute | solution.py:374
  55.9 6.8 %collective-permute-start.25 = (f32[2,48,256]{2,1,0:T(8,128)S(1)}, f32[2,48,256]{2,1,0:T(8,128)S(1)}, u32[]{:S(2)}, u32[]{:S(2)}) collective-permute-start(f32[2,48,256]{2,1,0:T(8,128)S(1)} %collective-permute-done.23.refs_13_.g_own), channel_id=1, source_target_pairs={{0,2},{1,3},{2,0},{3,1},{4,6},{5,7},{6,4},{7,5},{8,10},{9,11},{10,... | collective-permute-start | bytes 294920 | tf_op jit(solution)/shard_map/ppermute | solution.py:374
  57.0 7.5 %collective-permute-start.26 = (f32[2,48,256]{2,1,0:T(8,128)S(1)}, f32[2,48,256]{2,1,0:T(8,128)S(1)}, u32[]{:S(2)}, u32[]{:S(2)}) collective-permute-start(f32[2,48,256]{2,1,0:T(8,128)S(1)} %collective-permute-done.23.refs_13_.g_own), channel_id=1, source_target_pairs={{0,6},{1,7},{2,4},{3,5},{4,2},{5,3},{6,0},{7,1},{8,14},{9,15},{10,... | collective-permute-start | bytes 294920 | tf_op jit(solution)/shard_map/ppermute | solution.py:374
  58.3 0.9 %copy-start.5 = (f32[2,48,256]{2,1,0:T(8,128)S(1)}, f32[2,48,256]{2,1,0:T(8,128)}, u32[]{:S(2)}) copy-start(f32[2,48,256]{2,1,0:T(8,128)} %copy-done.4) | copy-start | bytes 294916
  59.2 5.3 %copy-start.3 = (f32[2,48,256]{2,1,0:T(8,128)S(1)}, f32[2,48,256]{2,1,0:T(8,128)}, u32[]{:S(2)}) copy-start(f32[2,48,256]{2,1,0:T(8,128)} %copy-done.2) | copy-start | bytes 294916
  59.9 8.6 %copy-start.1 = (f32[192,384]{1,0:T(8,128)S(1)}, f32[192,384]{1,0:T(8,128)}, u32[]{:S(2)}) copy-start(f32[192,384]{1,0:T(8,128)} %refs_0_.1) | copy-start | bytes 884740
  65.2 4.8 %collective-permute-start.31 = (f32[3,256,256]{2,1,0:T(8,128)S(1)}, f32[3,256,256]{2,1,0:T(8,128)S(1)}, u32[]{:S(2)}, u32[]{:S(2)}) collective-permute-start(f32[3,256,256]{2,1,0:T(8,128)S(1)} %shard_map.44.inner_a), channel_id=1, source_target_pairs={{0,1},{1,0},{2,3},{3,2},{4,5},{5,4},{6,7},{7,6},{8,9},{9,8},{10,11... | collective-permute-start | bytes 2359304 | tf_op jit(solution)/shard_map/ppermute | solution.py:374
  65.3 3.3 %collective-permute-start.13 = (f32[192,512]{1,0:T(8,128)S(1)}, f32[192,512]{1,0:T(8,128)S(1)}, u32[]{:S(2)}, u32[]{:S(2)}) collective-permute-start(f32[192,512]{1,0:T(8,128)S(1)} %get-tuple-element.40.refs_5_), channel_id=1, source_target_pairs={{0,1},{1,0},{2,3},{3,2},{4,5},{5,4},{6,7},{7,6},{8,9},{9,8},{10,11... | collective-permute-start | bytes 1179656 | tf_op jit(solution)/shard_map/ppermute | solution.py:374
  65.8 2.8 %collective-permute-start.30 = (f32[2,2,48,256]{3,2,1,0:T(8,128)S(1)}, f32[2,2,48,256]{3,2,1,0:T(8,128)S(1)}, u32[]{:S(2)}, u32[]{:S(2)}) collective-permute-start(f32[2,2,48,256]{3,2,1,0:T(8,128)S(1)} %collective-permute-done.19.refs_9_.near_x), channel_id=1, source_target_pairs={{0,1},{1,0},{2,3},{3,2},{4,5},{5,4},{6,7},{7,6},{8,9},{9,8},{10,11... | collective-permute-start | bytes 589832 | tf_op jit(solution)/shard_map/ppermute | solution.py:374
  65.9 2.7 %collective-permute-start.29 = (f32[2,48,256]{2,1,0:T(8,128)S(1)}, f32[2,48,256]{2,1,0:T(8,128)S(1)}, u32[]{:S(2)}, u32[]{:S(2)}) collective-permute-start(f32[2,48,256]{2,1,0:T(8,128)S(1)} %fusion.refs_19_), channel_id=1, source_target_pairs={{0,1},{1,0},{2,3},{3,2},{4,5},{5,4},{6,7},{7,6},{8,9},{9,8},{10,11... | collective-permute-start | bytes 294920 | tf_op jit(solution)/shard_map/ppermute | solution.py:374

commit v3 on v2

--- a/solution.py
+++ b/solution.py
@@ -169,10 +169,11 @@
     z, y, x, k = place()
     owner = z % 2 == k
     if kind in "ab":
-        plane = jnp.where(owner, z, lax.rem(z + 1, depth))
+        plane = jnp.where(owner, z, z + 1 - 2 * (z % 2))
     else:
-        plane = jnp.where(owner, lax.rem(z + 2, depth), lax.rem(z - 1 + depth, depth))
-    core = {"a": k, "b": 1 - k, "f": z % 2, "g": 1 - z % 2}[kind]
+        plane = jnp.where(owner, lax.rem(z + 2, depth), depth - 1 - z)
+    inner = jnp.where((z == 0) | (z == depth - 1), k, 1 - k)
+    core = {"a": k, "b": 1 - k, "f": inner, "g": 1 - inner}[kind]
     y_from = 1 - y if flip & 1 else y
     x_from = 1 - x if flip & 2 else x
     block = (plane // 2) * 4 + y_from * 2 + x_from
@@ -346,10 +347,11 @@
     m1 = inner_a[0] + inner_b[0]
     mixed_t = inner_a[1] + inner_b[1]
     m2 = inner_a[2] + inner_b[2]
-    m2 = m2 - apart3(split(mixed_t), cross)
+    taken = split(apart3(split(mixed_t), cross))
     side = split(mixed_t.T - apart3(split(m1), cross))
     left = apart3(v1, split(m1 + m1.T)) + apart3(v2, side, (1, 1))
-    right = apart3(v1, side) + apart3(v2, split(m2 + m2.T))
+    right = apart3(v2, split(m2 + m2.T)) - apart3(v2, taken) - apart3(v2, taken, (1, 1))
+    right = right + apart3(v1, side)
     out_ref[...] = (
         base_ref[...]
         + apart3(split(left), (high_ref[:, first], low_ref[:, first]), (1, 1))
@@ -388,17 +390,19 @@
     def to_core(z, y, x, k):
         return z, y, x, 1 - k
 
-    def ahead_first(z, y, x, k):
-        return (z + (2 if k == z % 2 else 1)) % depth, y, x, z % 2
-
-    def ahead_second(z, y, x, k):
-        return (z + (1 if k == z % 2 else 2)) % depth, y, x, z % 2
+    def ahead(first):
+        def target(z, y, x, k):
+            outer = z in (0, depth - 1)
+            far = ((k == z % 2) == first) == outer
+            return (depth - 1 - z if far else (z + 2) % depth), y, x, z % 2
+
+        return target
 
     def back_first(z, y, x, k):
-        return (z - 1) % depth if k == z % 2 else z, y, x, z % 2
+        return z ^ 1 if k == z % 2 else z, y, x, z % 2
 
     def back_second(z, y, x, k):
-        return (z, y, 1 - x, k) if k == z % 2 else ((z - 1) % depth, y, x, z % 2)
+        return (z, y, 1 - x, k) if k == z % 2 else (z ^ 1, y, x, z % 2)
 
     _, _, width = panels.shape
     block, cols = matrix.shape
@@ -466,7 +470,7 @@
     panel_rows_other = send(panel_rows, to_core)
 
     back1, back2 = send(piece, back_first), send(piece, back_second)
-    f_own, g_own = send(piece, ahead_first), send(piece, ahead_second)
+    f_own, g_own = send(piece, ahead(True)), send(piece, ahead(False))
     near = jnp.where(owner, jnp.stack([piece, back1]), jnp.stack([back1, back2]))
     near_y, near_x = send(near, to_y), send(near, to_x)
     f_y, f_x = send(f_own, to_y), send(f_own, to_x)

time: 72.3 us -> 72.6 us (level)
  waiting for transfers between devices: 24.6 us -> 26.1 us
  starting transfers between devices: 33.9 us -> 32.9 us
    ppermute x32, waiting for transfers between devices: 24.6 us -> 26.1 us  [send(): return lax.ppermute(value, ('row', 'col'), pairs)]
    ppermute x32, starting transfers between devices: 33.9 us -> 32.9 us  [send(): return lax.ppermute(value, ('row', 'col'), pairs)]
where the time goes in v3:
time: 72.6 us; the launch traced here: 72.4 us
  starting transfers between devices  32.9 us (45%)
  waiting for transfers between devices  26.1 us (36%)
  Pallas kernels  8.59 us (12%)
  local copies, waits for them, and re-layouts  4.39 us (6%)
    ppermute x32, starting transfers between devices, send(): return lax.ppermute(value, ('row', 'col'), pairs)  32.9 us
    ppermute x32, waiting for transfers between devices, send(): return lax.ppermute(value, ('row', 'col'), pairs)  26.1 us
    pallas_call x9, Pallas kernels, call(): pl.pallas_call(body, out_shape=shapes, in_specs=[pl.BlockSpec(memory_spac...  8.59 us
    unnamed x16, local copies, waits for them, and re-layouts  3.58 us
  transfers between devices with their start and end apart: 32, of which 18 were waited for; matrix products, arithmetic and copies ran while one was open for 0% of the time, Pallas kernels for 7%

profile of v3, /device:TPU:0, one launch (start us, length us, event | category | flops | bytes accessed | tf_op | source)
XLA Modules:
  0.0 72.4 jit_solution(4171868657866079716)
XLA Ops:
  0.0 3.1 %collective-permute-start.1 = (f32[2,48,256]{2,1,0:T(8,128)}, f32[2,48,256]{2,1,0:T(8,128)S(1)}, u32[]{:S(2)}, u32[]{:S(2)}) collective-permute-start(f32[2,48,256]{2,1,0:T(8,128)} %panels_hbm.1), channel_id=1, source_target_pairs={{0,8},{1,9},{2,10},{3,11},{4,12},{5,13},{6,14},{7,15},{8,16},{9,17... | collective-permute-start | bytes 294920 | tf_op jit(solution)/shard_map/ppermute | solution.py:376
  3.1 2.6 %collective-permute-start.3 = (f32[2,48,256]{2,1,0:T(8,128)}, f32[2,48,256]{2,1,0:T(8,128)S(1)}, u32[]{:S(2)}, u32[]{:S(2)}) collective-permute-start(f32[2,48,256]{2,1,0:T(8,128)} %panels_hbm.1), channel_id=1, source_target_pairs={{0,16},{1,17},{2,18},{3,19},{4,20},{5,21},{6,22},{7,23},{8,24},{9,... | collective-permute-start | bytes 294920 | tf_op jit(solution)/shard_map/ppermute | solution.py:376
  5.6 1.3 %collective-permute-start.5 = (f32[2,48,256]{2,1,0:T(8,128)}, f32[2,48,256]{2,1,0:T(8,128)S(1)}, u32[]{:S(2)}, u32[]{:S(2)}) collective-permute-start(f32[2,48,256]{2,1,0:T(8,128)} %panels_hbm.1), channel_id=1, source_target_pairs={{0,24},{1,25},{2,26},{3,27},{4,28},{5,29},{6,30},{7,31},{8,0},{9,1... | collective-permute-start | bytes 294920 | tf_op jit(solution)/shard_map/ppermute | solution.py:376
  7.0 1.0 %copy-done = f32[192,384]{1,0:T(8,128)S(1)} copy-done((f32[192,384]{1,0:T(8,128)S(1)}, f32[192,384]{1,0:T(8,128)}, u32[]{:S(2)}) %copy-start) | copy-done | bytes 294936
  8.0 1.0 %copy-done.6 = f32[2,256,256]{2,1,0:T(8,128)S(1)} copy-done((f32[2,256,256]{2,1,0:T(8,128)S(1)}, f32[2,256,256]{2,1,0:T(8,128)}, u32[]{:S(2)}) %copy-start.6) | copy-done | bytes 524312
  9.0 0.9 %copy-done.7 = f32[2,48,256]{2,1,0:T(8,128)S(1)} copy-done((f32[2,48,256]{2,1,0:T(8,128)S(1)}, f32[2,48,256]{2,1,0:T(8,128)}, u32[]{:S(2)}) %copy-start.7) | copy-done | bytes 98328
  10.3 1.6 %collective-permute-start.8 = (f32[2,48,256]{2,1,0:T(8,128)S(1)}, f32[2,48,256]{2,1,0:T(8,128)S(1)}, u32[]{:S(2)}, u32[]{:S(2)}) collective-permute-start(f32[2,48,256]{2,1,0:T(8,128)S(1)} %get-tuple-element.29.refs_4_.refs_0_), channel_id=1, source_target_pairs={{0,4},{1,5},{2,6},{3,7},{4,0},{5,1},{6,2},{7,3},{8,12},{9,13},{10,... | collective-permute-start | bytes 294920 | tf_op jit(solution)/shard_map/ppermute | solution.py:376
  12.4 1.5 %collective-permute-start.10 = (f32[2,48,256]{2,1,0:T(8,128)S(1)}, f32[2,48,256]{2,1,0:T(8,128)S(1)}, u32[]{:S(2)}, u32[]{:S(2)}) collective-permute-start(f32[2,48,256]{2,1,0:T(8,128)S(1)} %collective-permute-done.3.refs_6_.refs_2_), channel_id=1, source_target_pairs={{0,4},{1,5},{2,6},{3,7},{4,0},{5,1},{6,2},{7,3},{8,12},{9,13},{10,... | collective-permute-start | bytes 294920 | tf_op jit(solution)/shard_map/ppermute | solution.py:376
  14.5 1.2 %collective-permute-done.8.refs_8_.refs_4_ = f32[2,48,256]{2,1,0:T(8,128)S(1)} collective-permute-done((f32[2,48,256]{2,1,0:T(8,128)S(1)}, f32[2,48,256]{2,1,0:T(8,128)S(1)}, u32[]{:S(2)}, u32[]{:S(2)}) %collective-permute-start.8) | collective-permute-done | bytes 98336 | tf_op jit(solution)/shard_map/ppermute | solution.py:376
  15.6 2.1 %collective-permute-done.9.refs_9_.refs_5_ = f32[2,48,256]{2,1,0:T(8,128)S(1)} collective-permute-done((f32[2,48,256]{2,1,0:T(8,128)S(1)}, f32[2,48,256]{2,1,0:T(8,128)S(1)}, u32[]{:S(2)}, u32[]{:S(2)}) %collective-permute-start.9) | collective-permute-done | bytes 98336 | tf_op jit(solution)/shard_map/ppermute | solution.py:376
  17.7 1.8 %collective-permute-done.10.refs_10_.refs_6_ = f32[2,48,256]{2,1,0:T(8,128)S(1)} collective-permute-done((f32[2,48,256]{2,1,0:T(8,128)S(1)}, f32[2,48,256]{2,1,0:T(8,128)S(1)}, u32[]{:S(2)}, u32[]{:S(2)}) %collective-permute-start.10) | collective-permute-done | bytes 98336 | tf_op jit(solution)/shard_map/ppermute | solution.py:376
  19.5 1.1 %collective-permute-done.11.refs_11_.refs_7_ = f32[2,48,256]{2,1,0:T(8,128)S(1)} collective-permute-done((f32[2,48,256]{2,1,0:T(8,128)S(1)}, f32[2,48,256]{2,1,0:T(8,128)S(1)}, u32[]{:S(2)}, u32[]{:S(2)}) %collective-permute-start.11) | collective-permute-done | bytes 98336 | tf_op jit(solution)/shard_map/ppermute | solution.py:376
  20.6 0.7 shard_map.40
  21.3 1.6 %collective-permute-start = (f32[2,48,256]{2,1,0:T(8,128)S(1)}, f32[2,48,256]{2,1,0:T(8,128)S(1)}, u32[]{:S(2)}, u32[]{:S(2)}) collective-permute-start(f32[2,48,256]{2,1,0:T(8,128)S(1)} %get-tuple-element.29.refs_4_.refs_0_), channel_id=1, source_target_pairs={{0,2},{1,3},{2,0},{3,1},{4,6},{5,7},{6,4},{7,5},{8,10},{9,11},{10,... | collective-permute-start | bytes 294920 | tf_op jit(solution)/shard_map/ppermute | solution.py:376
  22.9 0.5 collective-permute-start.6
  23.4 1.5 %collective-permute-start.4 = (f32[2,48,256]{2,1,0:T(8,128)S(1)}, f32[2,48,256]{2,1,0:T(8,128)S(1)}, u32[]{:S(2)}, u32[]{:S(2)}) collective-permute-start(f32[2,48,256]{2,1,0:T(8,128)S(1)} %collective-permute-done.3.refs_6_.refs_2_), channel_id=1, source_target_pairs={{0,2},{1,3},{2,0},{3,1},{4,6},{5,7},{6,4},{7,5},{8,10},{9,11},{10,... | collective-permute-start | bytes 294920 | tf_op jit(solution)/shard_map/ppermute | solution.py:376
  25.4 0.5 shard_map.41
  26.0 1.6 %collective-permute-start.15 = (f32[2,48,256]{2,1,0:T(8,128)S(1)}, f32[2,48,256]{2,1,0:T(8,128)S(1)}, u32[]{:S(2)}, u32[]{:S(2)}) collective-permute-start(f32[2,48,256]{2,1,0:T(8,128)S(1)} %slice_bitcast_fusion.2), channel_id=1, source_target_pairs={{0,2},{1,3},{2,0},{3,1},{4,6},{5,7},{6,4},{7,5},{8,10},{9,11},{10,... | collective-permute-start | bytes 294920 | tf_op jit(solution)/shard_map/ppermute | solution.py:376
  27.6 1.6 %collective-permute-done.6 = f32[2,48,256]{2,1,0:T(8,128)S(1)} collective-permute-done((f32[2,48,256]{2,1,0:T(8,128)S(1)}, f32[2,48,256]{2,1,0:T(8,128)S(1)}, u32[]{:S(2)}, u32[]{:S(2)}) %collective-permute-start.6) | collective-permute-done | bytes 98336 | tf_op jit(solution)/shard_map/ppermute | solution.py:376
  29.1 2.1 %collective-permute-done.4 = f32[2,48,256]{2,1,0:T(8,128)S(1)} collective-permute-done((f32[2,48,256]{2,1,0:T(8,128)S(1)}, f32[2,48,256]{2,1,0:T(8,128)S(1)}, u32[]{:S(2)}, u32[]{:S(2)}) %collective-permute-start.4) | collective-permute-done | bytes 98336 | tf_op jit(solution)/shard_map/ppermute | solution.py:376
  31.2 2.1 %collective-permute-done.2 = f32[2,48,256]{2,1,0:T(8,128)S(1)} collective-permute-done((f32[2,48,256]{2,1,0:T(8,128)S(1)}, f32[2,48,256]{2,1,0:T(8,128)S(1)}, u32[]{:S(2)}, u32[]{:S(2)}) %collective-permute-start.2) | collective-permute-done | bytes 98336 | tf_op jit(solution)/shard_map/ppermute | solution.py:376
  33.4 1.4 %collective-permute-start.7 = (f32[4,2,48,256]{3,2,1,0:T(8,128)S(1)}, f32[4,2,48,256]{3,2,1,0:T(8,128)S(1)}, u32[]{:S(2)}, u32[]{:S(2)}) collective-permute-start(f32[4,2,48,256]{3,2,1,0:T(8,128)S(1)} %pad_maximum_fusion.refs_2_), channel_id=1, source_target_pairs={{0,4},{1,5},{2,6},{3,7},{4,0},{5,1},{6,2},{7,3},{8,12},{9,13},{10,... | collective-permute-start | bytes 1179656 | tf_op jit(solution)/shard_map/ppermute | solution.py:376
  34.9 0.7 %collective-permute-start.16 = (f32[2,48,256]{2,1,0:T(8,128)S(1)}, f32[2,48,256]{2,1,0:T(8,128)S(1)}, u32[]{:S(2)}, u32[]{:S(2)}) collective-permute-start(f32[2,48,256]{2,1,0:T(8,128)S(1)} %fusion.refs_19_), channel_id=1, source_target_pairs={{0,8},{1,0},{2,10},{3,2},{4,12},{5,4},{6,14},{7,6},{8,9},{9,1},{10... | collective-permute-start | bytes 294920 | tf_op jit(solution)/shard_map/ppermute | solution.py:376
  35.7 1.5 %collective-permute-start.17 = (f32[2,48,256]{2,1,0:T(8,128)S(1)}, f32[2,48,256]{2,1,0:T(8,128)S(1)}, u32[]{:S(2)}, u32[]{:S(2)}) collective-permute-start(f32[2,48,256]{2,1,0:T(8,128)S(1)} %fusion.refs_19_), channel_id=1, source_target_pairs={{0,2},{1,8},{2,0},{3,10},{4,6},{5,12},{6,4},{7,14},{8,1},{9,11},{1... | collective-permute-start | bytes 294920 | tf_op jit(solution)/shard_map/ppermute | solution.py:376
  37.3 1.1 %collective-permute-done.16 = f32[2,48,256]{2,1,0:T(8,128)S(1)} collective-permute-done((f32[2,48,256]{2,1,0:T(8,128)S(1)}, f32[2,48,256]{2,1,0:T(8,128)S(1)}, u32[]{:S(2)}, u32[]{:S(2)}) %collective-permute-start.16) | collective-permute-done | bytes 98336 | tf_op jit(solution)/shard_map/ppermute | solution.py:376
  38.4 1.9 %collective-permute-done.17 = f32[2,48,256]{2,1,0:T(8,128)S(1)} collective-permute-done((f32[2,48,256]{2,1,0:T(8,128)S(1)}, f32[2,48,256]{2,1,0:T(8,128)S(1)}, u32[]{:S(2)}, u32[]{:S(2)}) %collective-permute-start.17) | collective-permute-done | bytes 98336 | tf_op jit(solution)/shard_map/ppermute | solution.py:376
  40.3 1.6 %collective-permute-start.19 = (f32[2,2,48,256]{3,2,1,0:T(8,128)S(1)}, f32[2,2,48,256]{3,2,1,0:T(8,128)S(1)}, u32[]{:S(2)}, u32[]{:S(2)}) collective-permute-start(f32[2,2,48,256]{3,2,1,0:T(8,128)S(1)} %maximum_select_fusion.refs_7_.near), channel_id=1, source_target_pairs={{0,2},{1,3},{2,0},{3,1},{4,6},{5,7},{6,4},{7,5},{8,10},{9,11},{10,... | collective-permute-start | bytes 589832 | tf_op jit(solution)/shard_map/ppermute | solution.py:376
  41.9 1.9 %collective-permute-done.20.refs_10_.f_own = f32[2,48,256]{2,1,0:T(8,128)S(1)} collective-permute-done((f32[2,48,256]{2,1,0:T(8,128)S(1)}, f32[2,48,256]{2,1,0:T(8,128)S(1)}, u32[]{:S(2)}, u32[]{:S(2)}) %collective-permute-start.20) | collective-permute-done | bytes 98336 | tf_op jit(solution)/shard_map/ppermute | solution.py:376
  43.8 1.5 %collective-permute-start.22 = (f32[2,48,256]{2,1,0:T(8,128)S(1)}, f32[2,48,256]{2,1,0:T(8,128)S(1)}, u32[]{:S(2)}, u32[]{:S(2)}) collective-permute-start(f32[2,48,256]{2,1,0:T(8,128)S(1)} %collective-permute-done.20.refs_10_.f_own), channel_id=1, source_target_pairs={{0,2},{1,3},{2,0},{3,1},{4,6},{5,7},{6,4},{7,5},{8,10},{9,11},{10,... | collective-permute-start | bytes 294920 | tf_op jit(solution)/shard_map/ppermute | solution.py:376
  45.3 1.3 %collective-permute-start.21 = (f32[2,48,256]{2,1,0:T(8,128)S(1)}, f32[2,48,256]{2,1,0:T(8,128)S(1)}, u32[]{:S(2)}, u32[]{:S(2)}) collective-permute-start(f32[2,48,256]{2,1,0:T(8,128)S(1)} %collective-permute-done.20.refs_10_.f_own), channel_id=1, source_target_pairs={{0,4},{1,5},{2,6},{3,7},{4,0},{5,1},{6,2},{7,3},{8,12},{9,13},{10,... | collective-permute-start | bytes 294920 | tf_op jit(solution)/shard_map/ppermute | solution.py:376
  46.6 0.7 collective-permute-start.18
  47.3 1.3 %shard_map.38 = (bf16[256,768]{1,0:T(8,128)(2,1)S(1)}, bf16[256,768]{1,0:T(8,128)(2,1)S(1)}, f32[256,768]{1,0:T(8,128)S(1)}, bf16[256,768]{1,0:T(8,128)(2,1)S(1)...) custom-call(bf16[2,256,256]{2,1,0:T(8,128)(2,1)S(1)} %get-tuple-element.27.refs_0_.factor_high, ...), custom_call_target="tpu_custom_call" | custom-call | flops 905969664 | bytes 7208960 | tf_op jit(solution)/shard_map/pallas_call | solution.py:100
  48.9 0.6 collective-permute-start.12
  49.9 0.6 copy-done.4
  50.6 0.8 %slice-done = f32[1,48,256]{2,1,0:T(8,128)S(1)} async-done(((f32[2,48,256]{2,1,0:T(8,128)}), f32[1,48,256]{2,1,0:T(8,128)S(1)}, s32[]{:S(2)}) %slice-start) | async-done | bytes 49176 | tf_op jit(solution)/shard_map/slice | solution.py:479
  51.4 1.6 %collective-permute-start.27 = (f32[3,48,256]{2,1,0:T(8,128)S(1)}, f32[3,48,256]{2,1,0:T(8,128)S(1)}, u32[]{:S(2)}, u32[]{:S(2)}) collective-permute-start(f32[3,48,256]{2,1,0:T(8,128)S(1)} %pad_maximum_fusion.1), channel_id=1, source_target_pairs={{0,4},{1,5},{2,6},{3,7},{4,0},{5,1},{6,2},{7,3},{8,12},{9,13},{10,... | collective-permute-start | bytes 442376 | tf_op jit(solution)/shard_map/ppermute | solution.py:376
  53.0 1.3 %collective-permute-done.18.refs_8_.near_y = f32[2,2,48,256]{3,2,1,0:T(8,128)S(1)} collective-permute-done((f32[2,2,48,256]{3,2,1,0:T(8,128)S(1)}, f32[2,2,48,256]{3,2,1,0:T(8,128)S(1)}, u32[]{:S(2)}, u32[]{:S(2)}) %collective-permute-start.18) | collective-permute-done | bytes 196640 | tf_op jit(solution)/shard_map/ppermute | solution.py:376
  54.8 1.3 %collective-permute-start.24 = (f32[2,48,256]{2,1,0:T(8,128)S(1)}, f32[2,48,256]{2,1,0:T(8,128)S(1)}, u32[]{:S(2)}, u32[]{:S(2)}) collective-permute-start(f32[2,48,256]{2,1,0:T(8,128)S(1)} %collective-permute-done.23.refs_13_.g_own), channel_id=1, source_target_pairs={{0,4},{1,5},{2,6},{3,7},{4,0},{5,1},{6,2},{7,3},{8,12},{9,13},{10,... | collective-permute-start | bytes 294920 | tf_op jit(solution)/shard_map/ppermute | solution.py:376
  56.1 1.5 %collective-permute-start.25 = (f32[2,48,256]{2,1,0:T(8,128)S(1)}, f32[2,48,256]{2,1,0:T(8,128)S(1)}, u32[]{:S(2)}, u32[]{:S(2)}) collective-permute-start(f32[2,48,256]{2,1,0:T(8,128)S(1)} %collective-permute-done.23.refs_13_.g_own), channel_id=1, source_target_pairs={{0,2},{1,3},{2,0},{3,1},{4,6},{5,7},{6,4},{7,5},{8,10},{9,11},{10,... | collective-permute-start | bytes 294920 | tf_op jit(solution)/shard_map/ppermute | solution.py:376
  57.6 0.7 collective-permute-start.26
  58.2 0.9 %shard_map.39 = (bf16[256,256]{1,0:T(8,128)(2,1)S(1)}, bf16[256,256]{1,0:T(8,128)(2,1)S(1)}, bf16[256,768]{1,0:T(8,128)(2,1)S(1)}, bf16[256,768]{1,0:T(8,128)(2,1)S(1)}) custom-call(bf16[2,256,256]{2,1,0:T(8,128)(2,1)S(1)} %get-tuple-element.27.refs_0_.factor_high, bf16[2,256,256]{2,1,0:T(8,128)(2,1)S(1)} %get-tuple-element.28.refs_1_.factor_low, ...), custom_call_target="tpu_custom_call" | custom-call | flops 301989888 | bytes 6029312 | tf_op jit(solution)/shard_map/pallas_call | solution.py:100
  59.2 0.7 shard_map.43.before
  59.9 3.3 %collective-permute-done.25.refs_15_.g_x = f32[2,48,256]{2,1,0:T(8,128)S(1)} collective-permute-done((f32[2,48,256]{2,1,0:T(8,128)S(1)}, f32[2,48,256]{2,1,0:T(8,128)S(1)}, u32[]{:S(2)}, u32[]{:S(2)}) %collective-permute-start.25) | collective-permute-done | bytes 98336 | tf_op jit(solution)/shard_map/ppermute | solution.py:376
  63.2 1.6 %collective-permute-done.26.refs_16_.g_d = f32[2,48,256]{2,1,0:T(8,128)S(1)} collective-permute-done((f32[2,48,256]{2,1,0:T(8,128)S(1)}, f32[2,48,256]{2,1,0:T(8,128)S(1)}, u32[]{:S(2)}, u32[]{:S(2)}) %collective-permute-start.26) | collective-permute-done | bytes 98336 | tf_op jit(solution)/shard_map/ppermute | solution.py:376
  64.8 0.7 shard_map.44.inner_a
  66.6 2.2 %collective-permute-done.29.refs_20_ = f32[2,48,256]{2,1,0:T(8,128)S(1)} collective-permute-done((f32[2,48,256]{2,1,0:T(8,128)S(1)}, f32[2,48,256]{2,1,0:T(8,128)S(1)}, u32[]{:S(2)}, u32[]{:S(2)}) %collective-permute-start.29) | collective-permute-done | bytes 98336 | tf_op jit(solution)/shard_map/ppermute | solution.py:376
  68.9 1.4 %shard_map.42 = (f32[192,384]{1,0:T(8,128)S(1)}, bf16[192,512]{1,0:T(8,128)(2,1)S(1)}, bf16[192,512]{1,0:T(8,128)(2,1)S(1)}) custom-call(f32[192,384]{1,0:T(8,128)S(1)} %copy-done.1, bf16[256,256]{1,0:T(8,128)(2,1)S(1)} %get-tuple-element.34.refs_1_.cross_high, bf16[256,256]{1,0:T(8,128)(2,1)S(1)} %get-tuple-element.35.refs_2_.cross_low, ...), custom_call_target="tpu_custom_call" | custom-call | flops 679477248 | bytes 6225920 | tf_op jit(solution)/shard_map/pallas_call | solution.py:100
  70.3 2.0 %shard_map.45 = f32[192,384]{1,0:T(8,128)} custom-call(f32[192,384]{1,0:T(8,128)S(1)} %get-tuple-element.42.base_ref, f32[3,256,256]{2,1,0:T(8,128)S(1)} %shard_map.44.inner_a, f32[3,256,256]{2,1,0:T(8,128)S(1)} %collective-permute-done.31.inner_b, bf16[256,256]{1,0:T(8,128)(2,1)S(1)} %get-tuple-element.34.refs_1_.cross_high, ...), custom_call_target="tpu_custom_call" | custom-call | flops 679477248 | bytes 5046272 | tf_op jit(solution)/shard_map/pallas_call | solution.py:100
  (54 shorter events, 4.8 us)
Async XLA Ops:
  0.0 11.9 %collective-permute-start.1 = (f32[2,48,256]{2,1,0:T(8,128)}, f32[2,48,256]{2,1,0:T(8,128)S(1)}, u32[]{:S(2)}, u32[]{:S(2)}) collective-permute-start(f32[2,48,256]{2,1,0:T(8,128)} %panels_hbm.1), channel_id=1, source_target_pairs={{0,8},{1,9},{2,10},{3,11},{4,12},{5,13},{6,14},{7,15},{8,16},{9,17... | collective-permute-start | bytes 294920 | tf_op jit(solution)/shard_map/ppermute | solution.py:376
  3.1 9.4 %collective-permute-start.3 = (f32[2,48,256]{2,1,0:T(8,128)}, f32[2,48,256]{2,1,0:T(8,128)S(1)}, u32[]{:S(2)}, u32[]{:S(2)}) collective-permute-start(f32[2,48,256]{2,1,0:T(8,128)} %panels_hbm.1), channel_id=1, source_target_pairs={{0,16},{1,17},{2,18},{3,19},{4,20},{5,21},{6,22},{7,23},{8,24},{9,... | collective-permute-start | bytes 294920 | tf_op jit(solution)/shard_map/ppermute | solution.py:376
  5.6 8.3 %collective-permute-start.5 = (f32[2,48,256]{2,1,0:T(8,128)}, f32[2,48,256]{2,1,0:T(8,128)S(1)}, u32[]{:S(2)}, u32[]{:S(2)}) collective-permute-start(f32[2,48,256]{2,1,0:T(8,128)} %panels_hbm.1), channel_id=1, source_target_pairs={{0,24},{1,25},{2,26},{3,27},{4,28},{5,29},{6,30},{7,31},{8,0},{9,1... | collective-permute-start | bytes 294920 | tf_op jit(solution)/shard_map/ppermute | solution.py:376
  7.0 1.0 %copy-start = (f32[192,384]{1,0:T(8,128)S(1)}, f32[192,384]{1,0:T(8,128)}, u32[]{:S(2)}) copy-start(f32[192,384]{1,0:T(8,128)} %refs_0_.1) | copy-start | bytes 884740
  8.0 1.0 %copy-start.6 = (f32[2,256,256]{2,1,0:T(8,128)S(1)}, f32[2,256,256]{2,1,0:T(8,128)}, u32[]{:S(2)}) copy-start(f32[2,256,256]{2,1,0:T(8,128)} %factors_hbm.1) | copy-start | bytes 1572868
  9.0 0.9 %copy-start.7 = (f32[2,48,256]{2,1,0:T(8,128)S(1)}, f32[2,48,256]{2,1,0:T(8,128)}, u32[]{:S(2)}) copy-start(f32[2,48,256]{2,1,0:T(8,128)} %panels_hbm.1) | copy-start | bytes 294916
  10.3 5.3 %collective-permute-start.8 = (f32[2,48,256]{2,1,0:T(8,128)S(1)}, f32[2,48,256]{2,1,0:T(8,128)S(1)}, u32[]{:S(2)}, u32[]{:S(2)}) collective-permute-start(f32[2,48,256]{2,1,0:T(8,128)S(1)} %get-tuple-element.29.refs_4_.refs_0_), channel_id=1, source_target_pairs={{0,4},{1,5},{2,6},{3,7},{4,0},{5,1},{6,2},{7,3},{8,12},{9,13},{10,... | collective-permute-start | bytes 294920 | tf_op jit(solution)/shard_map/ppermute | solution.py:376
  11.9 5.9 %collective-permute-start.9 = (f32[2,48,256]{2,1,0:T(8,128)S(1)}, f32[2,48,256]{2,1,0:T(8,128)S(1)}, u32[]{:S(2)}, u32[]{:S(2)}) collective-permute-start(f32[2,48,256]{2,1,0:T(8,128)S(1)} %collective-permute-done.1.refs_5_.refs_1_), channel_id=1, source_target_pairs={{0,4},{1,5},{2,6},{3,7},{4,0},{5,1},{6,2},{7,3},{8,12},{9,13},{10,... | collective-permute-start | bytes 294920 | tf_op jit(solution)/shard_map/ppermute | solution.py:376
  12.4 7.1 %collective-permute-start.10 = (f32[2,48,256]{2,1,0:T(8,128)S(1)}, f32[2,48,256]{2,1,0:T(8,128)S(1)}, u32[]{:S(2)}, u32[]{:S(2)}) collective-permute-start(f32[2,48,256]{2,1,0:T(8,128)S(1)} %collective-permute-done.3.refs_6_.refs_2_), channel_id=1, source_target_pairs={{0,4},{1,5},{2,6},{3,7},{4,0},{5,1},{6,2},{7,3},{8,12},{9,13},{10,... | collective-permute-start | bytes 294920 | tf_op jit(solution)/shard_map/ppermute | solution.py:376
  14.0 6.6 %collective-permute-start.11 = (f32[2,48,256]{2,1,0:T(8,128)S(1)}, f32[2,48,256]{2,1,0:T(8,128)S(1)}, u32[]{:S(2)}, u32[]{:S(2)}) collective-permute-start(f32[2,48,256]{2,1,0:T(8,128)S(1)} %collective-permute-done.5.refs_7_.refs_3_), channel_id=1, source_target_pairs={{0,4},{1,5},{2,6},{3,7},{4,0},{5,1},{6,2},{7,3},{8,12},{9,13},{10,... | collective-permute-start | bytes 294920 | tf_op jit(solution)/shard_map/ppermute | solution.py:376
  21.2 4.7 %collective-permute-start.14 = (f32[2,2,48,256]{3,2,1,0:T(8,128)S(1)}, f32[2,2,48,256]{3,2,1,0:T(8,128)S(1)}, u32[]{:S(2)}, u32[]{:S(2)}) collective-permute-start(f32[2,2,48,256]{3,2,1,0:T(8,128)S(1)} %get-tuple-element.41), channel_id=1, source_target_pairs={{0,1},{1,0},{2,3},{3,2},{4,5},{5,4},{6,7},{7,6},{8,9},{9,8},{10,11... | collective-permute-start | bytes 589832 | tf_op jit(solution)/shard_map/ppermute | solution.py:376
  21.3 6.3 %collective-permute-start = (f32[2,48,256]{2,1,0:T(8,128)S(1)}, f32[2,48,256]{2,1,0:T(8,128)S(1)}, u32[]{:S(2)}, u32[]{:S(2)}) collective-permute-start(f32[2,48,256]{2,1,0:T(8,128)S(1)} %get-tuple-element.29.refs_4_.refs_0_), channel_id=1, source_target_pairs={{0,2},{1,3},{2,0},{3,1},{4,6},{5,7},{6,4},{7,5},{8,10},{9,11},{10,... | collective-permute-start | bytes 294920 | tf_op jit(solution)/shard_map/ppermute | solution.py:376
  22.9 6.3 %collective-permute-start.6 = (f32[2,48,256]{2,1,0:T(8,128)S(1)}, f32[2,48,256]{2,1,0:T(8,128)S(1)}, u32[]{:S(2)}, u32[]{:S(2)}) collective-permute-start(f32[2,48,256]{2,1,0:T(8,128)S(1)} %collective-permute-done.5.refs_7_.refs_3_), channel_id=1, source_target_pairs={{0,2},{1,3},{2,0},{3,1},{4,6},{5,7},{6,4},{7,5},{8,10},{9,11},{10,... | collective-permute-start | bytes 294920 | tf_op jit(solution)/shard_map/ppermute | solution.py:376
  23.4 7.9 %collective-permute-start.4 = (f32[2,48,256]{2,1,0:T(8,128)S(1)}, f32[2,48,256]{2,1,0:T(8,128)S(1)}, u32[]{:S(2)}, u32[]{:S(2)}) collective-permute-start(f32[2,48,256]{2,1,0:T(8,128)S(1)} %collective-permute-done.3.refs_6_.refs_2_), channel_id=1, source_target_pairs={{0,2},{1,3},{2,0},{3,1},{4,6},{5,7},{6,4},{7,5},{8,10},{9,11},{10,... | collective-permute-start | bytes 294920 | tf_op jit(solution)/shard_map/ppermute | solution.py:376
  24.9 8.5 %collective-permute-start.2 = (f32[2,48,256]{2,1,0:T(8,128)S(1)}, f32[2,48,256]{2,1,0:T(8,128)S(1)}, u32[]{:S(2)}, u32[]{:S(2)}) collective-permute-start(f32[2,48,256]{2,1,0:T(8,128)S(1)} %collective-permute-done.1.refs_5_.refs_1_), channel_id=1, source_target_pairs={{0,2},{1,3},{2,0},{3,1},{4,6},{5,7},{6,4},{7,5},{8,10},{9,11},{10,... | collective-permute-start | bytes 294920 | tf_op jit(solution)/shard_map/ppermute | solution.py:376
  26.0 8.9 %collective-permute-start.15 = (f32[2,48,256]{2,1,0:T(8,128)S(1)}, f32[2,48,256]{2,1,0:T(8,128)S(1)}, u32[]{:S(2)}, u32[]{:S(2)}) collective-permute-start(f32[2,48,256]{2,1,0:T(8,128)S(1)} %slice_bitcast_fusion.2), channel_id=1, source_target_pairs={{0,2},{1,3},{2,0},{3,1},{4,6},{5,7},{6,4},{7,5},{8,10},{9,11},{10,... | collective-permute-start | bytes 294920 | tf_op jit(solution)/shard_map/ppermute | solution.py:376
  33.4 13.2 %collective-permute-start.7 = (f32[4,2,48,256]{3,2,1,0:T(8,128)S(1)}, f32[4,2,48,256]{3,2,1,0:T(8,128)S(1)}, u32[]{:S(2)}, u32[]{:S(2)}) collective-permute-start(f32[4,2,48,256]{3,2,1,0:T(8,128)S(1)} %pad_maximum_fusion.refs_2_), channel_id=1, source_target_pairs={{0,4},{1,5},{2,6},{3,7},{4,0},{5,1},{6,2},{7,3},{8,12},{9,13},{10,... | collective-permute-start | bytes 1179656 | tf_op jit(solution)/shard_map/ppermute | solution.py:376
  34.9 3.4 %collective-permute-start.16 = (f32[2,48,256]{2,1,0:T(8,128)S(1)}, f32[2,48,256]{2,1,0:T(8,128)S(1)}, u32[]{:S(2)}, u32[]{:S(2)}) collective-permute-start(f32[2,48,256]{2,1,0:T(8,128)S(1)} %fusion.refs_19_), channel_id=1, source_target_pairs={{0,8},{1,0},{2,10},{3,2},{4,12},{5,4},{6,14},{7,6},{8,9},{9,1},{10... | collective-permute-start | bytes 294920 | tf_op jit(solution)/shard_map/ppermute | solution.py:376
  35.7 4.6 %collective-permute-start.17 = (f32[2,48,256]{2,1,0:T(8,128)S(1)}, f32[2,48,256]{2,1,0:T(8,128)S(1)}, u32[]{:S(2)}, u32[]{:S(2)}) collective-permute-start(f32[2,48,256]{2,1,0:T(8,128)S(1)} %fusion.refs_19_), channel_id=1, source_target_pairs={{0,2},{1,8},{2,0},{3,10},{4,6},{5,12},{6,4},{7,14},{8,1},{9,11},{1... | collective-permute-start | bytes 294920 | tf_op jit(solution)/shard_map/ppermute | solution.py:376
  37.2 6.6 %collective-permute-start.20 = (f32[2,48,256]{2,1,0:T(8,128)S(1)}, f32[2,48,256]{2,1,0:T(8,128)S(1)}, u32[]{:S(2)}, u32[]{:S(2)}) collective-permute-start(f32[2,48,256]{2,1,0:T(8,128)S(1)} %fusion.refs_19_), channel_id=1, source_target_pairs={{0,24},{1,16},{2,26},{3,18},{4,28},{5,20},{6,30},{7,22},{8,17},{9,... | collective-permute-start | bytes 294920 | tf_op jit(solution)/shard_map/ppermute | solution.py:376
  40.3 10.2 %collective-permute-start.19 = (f32[2,2,48,256]{3,2,1,0:T(8,128)S(1)}, f32[2,2,48,256]{3,2,1,0:T(8,128)S(1)}, u32[]{:S(2)}, u32[]{:S(2)}) collective-permute-start(f32[2,2,48,256]{3,2,1,0:T(8,128)S(1)} %maximum_select_fusion.refs_7_.near), channel_id=1, source_target_pairs={{0,2},{1,3},{2,0},{3,1},{4,6},{5,7},{6,4},{7,5},{8,10},{9,11},{10,... | collective-permute-start | bytes 589832 | tf_op jit(solution)/shard_map/ppermute | solution.py:376
  43.8 5.1 %collective-permute-start.22 = (f32[2,48,256]{2,1,0:T(8,128)S(1)}, f32[2,48,256]{2,1,0:T(8,128)S(1)}, u32[]{:S(2)}, u32[]{:S(2)}) collective-permute-start(f32[2,48,256]{2,1,0:T(8,128)S(1)} %collective-permute-done.20.refs_10_.f_own), channel_id=1, source_target_pairs={{0,2},{1,3},{2,0},{3,1},{4,6},{5,7},{6,4},{7,5},{8,10},{9,11},{10,... | collective-permute-start | bytes 294920 | tf_op jit(solution)/shard_map/ppermute | solution.py:376
  45.3 4.6 %collective-permute-start.21 = (f32[2,48,256]{2,1,0:T(8,128)S(1)}, f32[2,48,256]{2,1,0:T(8,128)S(1)}, u32[]{:S(2)}, u32[]{:S(2)}) collective-permute-start(f32[2,48,256]{2,1,0:T(8,128)S(1)} %collective-permute-done.20.refs_10_.f_own), channel_id=1, source_target_pairs={{0,4},{1,5},{2,6},{3,7},{4,0},{5,1},{6,2},{7,3},{8,12},{9,13},{10,... | collective-permute-start | bytes 294920 | tf_op jit(solution)/shard_map/ppermute | solution.py:376
  46.6 8.1 %collective-permute-start.23 = (f32[2,48,256]{2,1,0:T(8,128)S(1)}, f32[2,48,256]{2,1,0:T(8,128)S(1)}, u32[]{:S(2)}, u32[]{:S(2)}) collective-permute-start(f32[2,48,256]{2,1,0:T(8,128)S(1)} %fusion.refs_19_), channel_id=1, source_target_pairs={{0,16},{1,24},{2,18},{3,26},{4,20},{5,28},{6,22},{7,30},{8,25},{9,... | collective-permute-start | bytes 294920 | tf_op jit(solution)/shard_map/ppermute | solution.py:376
  46.6 7.7 %collective-permute-start.18 = (f32[2,2,48,256]{3,2,1,0:T(8,128)S(1)}, f32[2,2,48,256]{3,2,1,0:T(8,128)S(1)}, u32[]{:S(2)}, u32[]{:S(2)}) collective-permute-start(f32[2,2,48,256]{3,2,1,0:T(8,128)S(1)} %maximum_select_fusion.refs_7_.near), channel_id=1, source_target_pairs={{0,4},{1,5},{2,6},{3,7},{4,0},{5,1},{6,2},{7,3},{8,12},{9,13},{10,... | collective-permute-start | bytes 589832 | tf_op jit(solution)/shard_map/ppermute | solution.py:376
  48.9 0.6 copy-start.2
  48.9 8.7 %collective-permute-start.12 = (f32[256,256]{1,0:T(8,128)S(1)}, f32[256,256]{1,0:T(8,128)S(1)}, u32[]{:S(2)}, u32[]{:S(2)}) collective-permute-start(f32[256,256]{1,0:T(8,128)S(1)} %get-tuple-element.30.cross_a), channel_id=1, source_target_pairs={{0,1},{1,0},{2,3},{3,2},{4,5},{5,4},{6,7},{7,6},{8,9},{9,8},{10,11... | collective-permute-start | bytes 786440 | tf_op jit(solution)/shard_map/ppermute | solution.py:376
  49.9 0.6 copy-start.4
  50.5 0.8 %slice-start = ((f32[2,48,256]{2,1,0:T(8,128)}), f32[1,48,256]{2,1,0:T(8,128)S(1)}, s32[]{:S(2)}) async-start(f32[2,48,256]{2,1,0:T(8,128)} %copy-done.2), calls=%async_computation | async-start | bytes 98304 | tf_op jit(solution)/shard_map/slice | solution.py:479
  51.3 2.9 %slice-start.1 = ((f32[2,48,256]{2,1,0:T(8,128)}), f32[1,48,256]{2,1,0:T(8,128)S(1)}, s32[]{:S(2)}) async-start(f32[2,48,256]{2,1,0:T(8,128)} %copy-done.4), calls=%async_computation.1 | async-start | bytes 98304 | tf_op jit(solution)/shard_map/slice | solution.py:480
  51.4 13.5 %collective-permute-start.27 = (f32[3,48,256]{2,1,0:T(8,128)S(1)}, f32[3,48,256]{2,1,0:T(8,128)S(1)}, u32[]{:S(2)}, u32[]{:S(2)}) collective-permute-start(f32[3,48,256]{2,1,0:T(8,128)S(1)} %pad_maximum_fusion.1), channel_id=1, source_target_pairs={{0,4},{1,5},{2,6},{3,7},{4,0},{5,1},{6,2},{7,3},{8,12},{9,13},{10,... | collective-permute-start | bytes 442376 | tf_op jit(solution)/shard_map/ppermute | solution.py:376
  54.3 10.5 %collective-permute-start.28 = (f32[3,48,256]{2,1,0:T(8,128)S(1)}, f32[3,48,256]{2,1,0:T(8,128)S(1)}, u32[]{:S(2)}, u32[]{:S(2)}) collective-permute-start(f32[3,48,256]{2,1,0:T(8,128)S(1)} %pad_maximum_fusion.2), channel_id=1, source_target_pairs={{0,2},{1,3},{2,0},{3,1},{4,6},{5,7},{6,4},{7,5},{8,10},{9,11},{10,... | collective-permute-start | bytes 442376 | tf_op jit(solution)/shard_map/ppermute | solution.py:376
  54.8 5.2 %collective-permute-start.24 = (f32[2,48,256]{2,1,0:T(8,128)S(1)}, f32[2,48,256]{2,1,0:T(8,128)S(1)}, u32[]{:S(2)}, u32[]{:S(2)}) collective-permute-start(f32[2,48,256]{2,1,0:T(8,128)S(1)} %collective-permute-done.23.refs_13_.g_own), channel_id=1, source_target_pairs={{0,4},{1,5},{2,6},{3,7},{4,0},{5,1},{6,2},{7,3},{8,12},{9,13},{10,... | collective-permute-start | bytes 294920 | tf_op jit(solution)/shard_map/ppermute | solution.py:376
  56.1 7.1 %collective-permute-start.25 = (f32[2,48,256]{2,1,0:T(8,128)S(1)}, f32[2,48,256]{2,1,0:T(8,128)S(1)}, u32[]{:S(2)}, u32[]{:S(2)}) collective-permute-start(f32[2,48,256]{2,1,0:T(8,128)S(1)} %collective-permute-done.23.refs_13_.g_own), channel_id=1, source_target_pairs={{0,2},{1,3},{2,0},{3,1},{4,6},{5,7},{6,4},{7,5},{8,10},{9,11},{10,... | collective-permute-start | bytes 294920 | tf_op jit(solution)/shard_map/ppermute | solution.py:376
  57.6 7.3 %collective-permute-start.26 = (f32[2,48,256]{2,1,0:T(8,128)S(1)}, f32[2,48,256]{2,1,0:T(8,128)S(1)}, u32[]{:S(2)}, u32[]{:S(2)}) collective-permute-start(f32[2,48,256]{2,1,0:T(8,128)S(1)} %collective-permute-done.23.refs_13_.g_own), channel_id=1, source_target_pairs={{0,6},{1,7},{2,4},{3,5},{4,2},{5,3},{6,0},{7,1},{8,14},{9,15},{10,... | collective-permute-start | bytes 294920 | tf_op jit(solution)/shard_map/ppermute | solution.py:376
  58.2 0.9 %copy-start.5 = (f32[2,48,256]{2,1,0:T(8,128)S(1)}, f32[2,48,256]{2,1,0:T(8,128)}, u32[]{:S(2)}) copy-start(f32[2,48,256]{2,1,0:T(8,128)} %copy-done.4) | copy-start | bytes 294916
  59.2 5.6 %copy-start.3 = (f32[2,48,256]{2,1,0:T(8,128)S(1)}, f32[2,48,256]{2,1,0:T(8,128)}, u32[]{:S(2)}) copy-start(f32[2,48,256]{2,1,0:T(8,128)} %copy-done.2) | copy-start | bytes 294916
  59.9 9.0 %copy-start.1 = (f32[192,384]{1,0:T(8,128)S(1)}, f32[192,384]{1,0:T(8,128)}, u32[]{:S(2)}) copy-start(f32[192,384]{1,0:T(8,128)} %refs_0_.1) | copy-start | bytes 884740
  65.5 4.8 %collective-permute-start.31 = (f32[3,256,256]{2,1,0:T(8,128)S(1)}, f32[3,256,256]{2,1,0:T(8,128)S(1)}, u32[]{:S(2)}, u32[]{:S(2)}) collective-permute-start(f32[3,256,256]{2,1,0:T(8,128)S(1)} %shard_map.44.inner_a), channel_id=1, source_target_pairs={{0,1},{1,0},{2,3},{3,2},{4,5},{5,4},{6,7},{7,6},{8,9},{9,8},{10,11... | collective-permute-start | bytes 2359304 | tf_op jit(solution)/shard_map/ppermute | solution.py:376
  65.6 3.3 %collective-permute-start.13 = (f32[192,512]{1,0:T(8,128)S(1)}, f32[192,512]{1,0:T(8,128)S(1)}, u32[]{:S(2)}, u32[]{:S(2)}) collective-permute-start(f32[192,512]{1,0:T(8,128)S(1)} %get-tuple-element.40.refs_5_), channel_id=1, source_target_pairs={{0,1},{1,0},{2,3},{3,2},{4,5},{5,4},{6,7},{7,6},{8,9},{9,8},{10,11... | collective-permute-start | bytes 1179656 | tf_op jit(solution)/shard_map/ppermute | solution.py:376
  66.1 2.8 %collective-permute-start.30 = (f32[2,2,48,256]{3,2,1,0:T(8,128)S(1)}, f32[2,2,48,256]{3,2,1,0:T(8,128)S(1)}, u32[]{:S(2)}, u32[]{:S(2)}) collective-permute-start(f32[2,2,48,256]{3,2,1,0:T(8,128)S(1)} %collective-permute-done.19.refs_9_.near_x), channel_id=1, source_target_pairs={{0,1},{1,0},{2,3},{3,2},{4,5},{5,4},{6,7},{7,6},{8,9},{9,8},{10,11... | collective-permute-start | bytes 589832 | tf_op jit(solution)/shard_map/ppermute | solution.py:376
  66.2 2.7 %collective-permute-start.29 = (f32[2,48,256]{2,1,0:T(8,128)S(1)}, f32[2,48,256]{2,1,0:T(8,128)S(1)}, u32[]{:S(2)}, u32[]{:S(2)}) collective-permute-start(f32[2,48,256]{2,1,0:T(8,128)S(1)} %fusion.refs_19_), channel_id=1, source_target_pairs={{0,1},{1,0},{2,3},{3,2},{4,5},{5,4},{6,7},{7,6},{8,9},{9,8},{10,11... | collective-permute-start | bytes 294920 | tf_op jit(solution)/shard_map/ppermute | solution.py:376

commit v4 on v3

--- a/solution.py
+++ b/solution.py
@@ -146,7 +146,7 @@
     for flip in range(2):
         for shift in range(depth):
             slab = slabs[flip * depth + shift]
-            at = 2 * lax.rem(z - shift + depth, depth) + (1 - y if flip else y)
+            at = 2 * (z ^ shift) + (1 - y if flip else y)
             rows = pl.ds(pl.multiple_of(at * share, share), share)
             for step in range(2):
                 h, l = split(slab[step])
@@ -219,7 +219,7 @@
                     slab = (opposite_ref if flip else across_ref).at[shift]
                 else:
                     slab = slabs[flip * depth + shift]
-                at = 2 * lax.rem(z - shift + depth, depth) + (1 - y if flip else y)
+                at = 2 * (z ^ shift) + (1 - y if flip else y)
                 start = (1 - x if across else x) * column + at * share
                 fill(full, pl.multiple_of(start, share), steps(slab))
     for at, (kind, flip) in enumerate(EARLY + LATE):
@@ -376,7 +376,7 @@
         return lax.ppermute(value, ("row", "col"), pairs)
 
     def along_z(shift):
-        return lambda z, y, x, k: ((z + shift) % depth, y, x, k)
+        return lambda z, y, x, k: (z ^ shift, y, x, k)
 
     def to_y(z, y, x, k):
         return z, 1 - y, x, k

time: 72.6 us -> 73 us (level)
  transfers between devices with their start and end apart: 32 -> 32, of which waited for: 18 -> 14; matrix products, arithmetic and copies ran while one was open for 0% -> 0% of each run, Pallas kernels for 7% -> 7%
where the time goes in v4:
time: 73 us; the launch traced here: 72.7 us
  starting transfers between devices  33.1 us (45%)
  waiting for transfers between devices  26.3 us (36%)
  Pallas kernels  8.58 us (12%)
  local copies, waits for them, and re-layouts  4.37 us (6%)
    ppermute x32, starting transfers between devices, send(): return lax.ppermute(value, ('row', 'col'), pairs)  33.1 us
    ppermute x32, waiting for transfers between devices, send(): return lax.ppermute(value, ('row', 'col'), pairs)  26.3 us
    pallas_call x9, Pallas kernels, call(): pl.pallas_call(body, out_shape=shapes, in_specs=[pl.BlockSpec(memory_spac...  8.58 us
    unnamed x16, local copies, waits for them, and re-layouts  3.55 us
  transfers between devices with their start and end apart: 32, of which 14 were waited for; matrix products, arithmetic and copies ran while one was open for 0% of the time, Pallas kernels for 7%

profile of v4, /device:TPU:0, one launch (start us, length us, event | category | flops | bytes accessed | tf_op | source)
XLA Modules:
  0.0 72.7 jit_solution(9036797303073065521)
XLA Ops:
  0.0 3.1 %collective-permute-start.1 = (f32[2,48,256]{2,1,0:T(8,128)}, f32[2,48,256]{2,1,0:T(8,128)S(1)}, u32[]{:S(2)}, u32[]{:S(2)}) collective-permute-start(f32[2,48,256]{2,1,0:T(8,128)} %panels_hbm.1), channel_id=1, source_target_pairs={{0,8},{1,9},{2,10},{3,11},{4,12},{5,13},{6,14},{7,15},{8,0},{9,1},... | collective-permute-start | bytes 294920 | tf_op jit(solution)/shard_map/ppermute | solution.py:376
  3.1 2.6 %collective-permute-start.3 = (f32[2,48,256]{2,1,0:T(8,128)}, f32[2,48,256]{2,1,0:T(8,128)S(1)}, u32[]{:S(2)}, u32[]{:S(2)}) collective-permute-start(f32[2,48,256]{2,1,0:T(8,128)} %panels_hbm.1), channel_id=1, source_target_pairs={{0,16},{1,17},{2,18},{3,19},{4,20},{5,21},{6,22},{7,23},{8,24},{9,... | collective-permute-start | bytes 294920 | tf_op jit(solution)/shard_map/ppermute | solution.py:376
  5.6 1.0 %copy-done = f32[192,384]{1,0:T(8,128)S(1)} copy-done((f32[192,384]{1,0:T(8,128)S(1)}, f32[192,384]{1,0:T(8,128)}, u32[]{:S(2)}) %copy-start) | copy-done | bytes 294936
  6.6 1.0 %copy-done.6 = f32[2,256,256]{2,1,0:T(8,128)S(1)} copy-done((f32[2,256,256]{2,1,0:T(8,128)S(1)}, f32[2,256,256]{2,1,0:T(8,128)}, u32[]{:S(2)}) %copy-start.6) | copy-done | bytes 524312
  7.7 0.9 %copy-done.7 = f32[2,48,256]{2,1,0:T(8,128)S(1)} copy-done((f32[2,48,256]{2,1,0:T(8,128)S(1)}, f32[2,48,256]{2,1,0:T(8,128)}, u32[]{:S(2)}) %copy-start.7) | copy-done | bytes 98328
  8.9 1.8 %collective-permute-start.8 = (f32[2,48,256]{2,1,0:T(8,128)S(1)}, f32[2,48,256]{2,1,0:T(8,128)S(1)}, u32[]{:S(2)}, u32[]{:S(2)}) collective-permute-start(f32[2,48,256]{2,1,0:T(8,128)S(1)} %get-tuple-element.29.refs_4_.refs_0_), channel_id=1, source_target_pairs={{0,4},{1,5},{2,6},{3,7},{4,0},{5,1},{6,2},{7,3},{8,12},{9,13},{10,... | collective-permute-start | bytes 294920 | tf_op jit(solution)/shard_map/ppermute | solution.py:376
  11.0 2.7 %collective-permute-done.3.refs_6_.refs_2_ = f32[2,48,256]{2,1,0:T(8,128)S(1)} collective-permute-done((f32[2,48,256]{2,1,0:T(8,128)}, f32[2,48,256]{2,1,0:T(8,128)S(1)}, u32[]{:S(2)}, u32[]{:S(2)}) %collective-permute-start.3) | collective-permute-done | bytes 98336 | tf_op jit(solution)/shard_map/ppermute | solution.py:376
  13.7 1.5 %collective-permute-start.10 = (f32[2,48,256]{2,1,0:T(8,128)S(1)}, f32[2,48,256]{2,1,0:T(8,128)S(1)}, u32[]{:S(2)}, u32[]{:S(2)}) collective-permute-start(f32[2,48,256]{2,1,0:T(8,128)S(1)} %collective-permute-done.3.refs_6_.refs_2_), channel_id=1, source_target_pairs={{0,4},{1,5},{2,6},{3,7},{4,0},{5,1},{6,2},{7,3},{8,12},{9,13},{10,... | collective-permute-start | bytes 294920 | tf_op jit(solution)/shard_map/ppermute | solution.py:376
  15.7 1.0 %collective-permute-done.9.refs_9_.refs_5_ = f32[2,48,256]{2,1,0:T(8,128)S(1)} collective-permute-done((f32[2,48,256]{2,1,0:T(8,128)S(1)}, f32[2,48,256]{2,1,0:T(8,128)S(1)}, u32[]{:S(2)}, u32[]{:S(2)}) %collective-permute-start.9) | collective-permute-done | bytes 98336 | tf_op jit(solution)/shard_map/ppermute | solution.py:376
  16.8 1.7 %collective-permute-done.10.refs_10_.refs_6_ = f32[2,48,256]{2,1,0:T(8,128)S(1)} collective-permute-done((f32[2,48,256]{2,1,0:T(8,128)S(1)}, f32[2,48,256]{2,1,0:T(8,128)S(1)}, u32[]{:S(2)}, u32[]{:S(2)}) %collective-permute-start.10) | collective-permute-done | bytes 98336 | tf_op jit(solution)/shard_map/ppermute | solution.py:376
  18.4 1.4 %collective-permute-done.11.refs_11_.refs_7_ = f32[2,48,256]{2,1,0:T(8,128)S(1)} collective-permute-done((f32[2,48,256]{2,1,0:T(8,128)S(1)}, f32[2,48,256]{2,1,0:T(8,128)S(1)}, u32[]{:S(2)}, u32[]{:S(2)}) %collective-permute-start.11) | collective-permute-done | bytes 98336 | tf_op jit(solution)/shard_map/ppermute | solution.py:376
  19.8 0.6 shard_map.40
  20.6 1.6 %collective-permute-start = (f32[2,48,256]{2,1,0:T(8,128)S(1)}, f32[2,48,256]{2,1,0:T(8,128)S(1)}, u32[]{:S(2)}, u32[]{:S(2)}) collective-permute-start(f32[2,48,256]{2,1,0:T(8,128)S(1)} %get-tuple-element.29.refs_4_.refs_0_), channel_id=1, source_target_pairs={{0,2},{1,3},{2,0},{3,1},{4,6},{5,7},{6,4},{7,5},{8,10},{9,11},{10,... | collective-permute-start | bytes 294920 | tf_op jit(solution)/shard_map/ppermute | solution.py:376
  22.1 0.5 collective-permute-start.6
  22.7 1.5 %collective-permute-start.4 = (f32[2,48,256]{2,1,0:T(8,128)S(1)}, f32[2,48,256]{2,1,0:T(8,128)S(1)}, u32[]{:S(2)}, u32[]{:S(2)}) collective-permute-start(f32[2,48,256]{2,1,0:T(8,128)S(1)} %collective-permute-done.3.refs_6_.refs_2_), channel_id=1, source_target_pairs={{0,2},{1,3},{2,0},{3,1},{4,6},{5,7},{6,4},{7,5},{8,10},{9,11},{10,... | collective-permute-start | bytes 294920 | tf_op jit(solution)/shard_map/ppermute | solution.py:376
  24.2 0.5 collective-permute-start.2
  24.7 0.5 shard_map.41
  25.3 1.6 %collective-permute-start.15 = (f32[2,48,256]{2,1,0:T(8,128)S(1)}, f32[2,48,256]{2,1,0:T(8,128)S(1)}, u32[]{:S(2)}, u32[]{:S(2)}) collective-permute-start(f32[2,48,256]{2,1,0:T(8,128)S(1)} %slice_bitcast_fusion.2), channel_id=1, source_target_pairs={{0,2},{1,3},{2,0},{3,1},{4,6},{5,7},{6,4},{7,5},{8,10},{9,11},{10,... | collective-permute-start | bytes 294920 | tf_op jit(solution)/shard_map/ppermute | solution.py:376
  26.9 1.6 %collective-permute-done.6 = f32[2,48,256]{2,1,0:T(8,128)S(1)} collective-permute-done((f32[2,48,256]{2,1,0:T(8,128)S(1)}, f32[2,48,256]{2,1,0:T(8,128)S(1)}, u32[]{:S(2)}, u32[]{:S(2)}) %collective-permute-start.6) | collective-permute-done | bytes 98336 | tf_op jit(solution)/shard_map/ppermute | solution.py:376
  28.4 2.1 %collective-permute-done.4 = f32[2,48,256]{2,1,0:T(8,128)S(1)} collective-permute-done((f32[2,48,256]{2,1,0:T(8,128)S(1)}, f32[2,48,256]{2,1,0:T(8,128)S(1)}, u32[]{:S(2)}, u32[]{:S(2)}) %collective-permute-start.4) | collective-permute-done | bytes 98336 | tf_op jit(solution)/shard_map/ppermute | solution.py:376
  30.5 2.1 %collective-permute-done.2 = f32[2,48,256]{2,1,0:T(8,128)S(1)} collective-permute-done((f32[2,48,256]{2,1,0:T(8,128)S(1)}, f32[2,48,256]{2,1,0:T(8,128)S(1)}, u32[]{:S(2)}, u32[]{:S(2)}) %collective-permute-start.2) | collective-permute-done | bytes 98336 | tf_op jit(solution)/shard_map/ppermute | solution.py:376
  32.7 1.1 %collective-permute-start.7 = (f32[4,2,48,256]{3,2,1,0:T(8,128)S(1)}, f32[4,2,48,256]{3,2,1,0:T(8,128)S(1)}, u32[]{:S(2)}, u32[]{:S(2)}) collective-permute-start(f32[4,2,48,256]{3,2,1,0:T(8,128)S(1)} %pad_maximum_fusion.refs_2_), channel_id=1, source_target_pairs={{0,4},{1,5},{2,6},{3,7},{4,0},{5,1},{6,2},{7,3},{8,12},{9,13},{10,... | collective-permute-start | bytes 1179656 | tf_op jit(solution)/shard_map/ppermute | solution.py:376
  34.6 1.5 %collective-permute-start.17 = (f32[2,48,256]{2,1,0:T(8,128)S(1)}, f32[2,48,256]{2,1,0:T(8,128)S(1)}, u32[]{:S(2)}, u32[]{:S(2)}) collective-permute-start(f32[2,48,256]{2,1,0:T(8,128)S(1)} %fusion.refs_19_), channel_id=1, source_target_pairs={{0,2},{1,8},{2,0},{3,10},{4,6},{5,12},{6,4},{7,14},{8,1},{9,11},{1... | collective-permute-start | bytes 294920 | tf_op jit(solution)/shard_map/ppermute | solution.py:376
  36.1 1.6 %collective-permute-start.20 = (f32[2,48,256]{2,1,0:T(8,128)S(1)}, f32[2,48,256]{2,1,0:T(8,128)S(1)}, u32[]{:S(2)}, u32[]{:S(2)}) collective-permute-start(f32[2,48,256]{2,1,0:T(8,128)S(1)} %fusion.refs_19_), channel_id=1, source_target_pairs={{0,24},{1,16},{2,26},{3,18},{4,28},{5,20},{6,30},{7,22},{8,17},{9,... | collective-permute-start | bytes 294920 | tf_op jit(solution)/shard_map/ppermute | solution.py:376
  37.6 1.5 %collective-permute-done.17 = f32[2,48,256]{2,1,0:T(8,128)S(1)} collective-permute-done((f32[2,48,256]{2,1,0:T(8,128)S(1)}, f32[2,48,256]{2,1,0:T(8,128)S(1)}, u32[]{:S(2)}, u32[]{:S(2)}) %collective-permute-start.17) | collective-permute-done | bytes 98336 | tf_op jit(solution)/shard_map/ppermute | solution.py:376
  39.2 1.6 %collective-permute-start.19 = (f32[2,2,48,256]{3,2,1,0:T(8,128)S(1)}, f32[2,2,48,256]{3,2,1,0:T(8,128)S(1)}, u32[]{:S(2)}, u32[]{:S(2)}) collective-permute-start(f32[2,2,48,256]{3,2,1,0:T(8,128)S(1)} %maximum_select_fusion.refs_7_.near), channel_id=1, source_target_pairs={{0,2},{1,3},{2,0},{3,1},{4,6},{5,7},{6,4},{7,5},{8,10},{9,11},{10,... | collective-permute-start | bytes 589832 | tf_op jit(solution)/shard_map/ppermute | solution.py:376
  40.8 2.5 %collective-permute-done.20.refs_10_.f_own = f32[2,48,256]{2,1,0:T(8,128)S(1)} collective-permute-done((f32[2,48,256]{2,1,0:T(8,128)S(1)}, f32[2,48,256]{2,1,0:T(8,128)S(1)}, u32[]{:S(2)}, u32[]{:S(2)}) %collective-permute-start.20) | collective-permute-done | bytes 98336 | tf_op jit(solution)/shard_map/ppermute | solution.py:376
  43.3 1.5 %collective-permute-start.22 = (f32[2,48,256]{2,1,0:T(8,128)S(1)}, f32[2,48,256]{2,1,0:T(8,128)S(1)}, u32[]{:S(2)}, u32[]{:S(2)}) collective-permute-start(f32[2,48,256]{2,1,0:T(8,128)S(1)} %collective-permute-done.20.refs_10_.f_own), channel_id=1, source_target_pairs={{0,2},{1,3},{2,0},{3,1},{4,6},{5,7},{6,4},{7,5},{8,10},{9,11},{10,... | collective-permute-start | bytes 294920 | tf_op jit(solution)/shard_map/ppermute | solution.py:376
  44.8 1.3 %collective-permute-start.21 = (f32[2,48,256]{2,1,0:T(8,128)S(1)}, f32[2,48,256]{2,1,0:T(8,128)S(1)}, u32[]{:S(2)}, u32[]{:S(2)}) collective-permute-start(f32[2,48,256]{2,1,0:T(8,128)S(1)} %collective-permute-done.20.refs_10_.f_own), channel_id=1, source_target_pairs={{0,4},{1,5},{2,6},{3,7},{4,0},{5,1},{6,2},{7,3},{8,12},{9,13},{10,... | collective-permute-start | bytes 294920 | tf_op jit(solution)/shard_map/ppermute | solution.py:376
  46.1 1.0 %collective-permute-start.23 = (f32[2,48,256]{2,1,0:T(8,128)S(1)}, f32[2,48,256]{2,1,0:T(8,128)S(1)}, u32[]{:S(2)}, u32[]{:S(2)}) collective-permute-start(f32[2,48,256]{2,1,0:T(8,128)S(1)} %fusion.refs_19_), channel_id=1, source_target_pairs={{0,16},{1,24},{2,18},{3,26},{4,20},{5,28},{6,22},{7,30},{8,25},{9,... | collective-permute-start | bytes 294920 | tf_op jit(solution)/shard_map/ppermute | solution.py:376
  47.1 0.7 collective-permute-start.18
  47.8 1.2 %shard_map.38 = (bf16[256,768]{1,0:T(8,128)(2,1)S(1)}, bf16[256,768]{1,0:T(8,128)(2,1)S(1)}, f32[256,768]{1,0:T(8,128)S(1)}, bf16[256,768]{1,0:T(8,128)(2,1)S(1)...) custom-call(bf16[2,256,256]{2,1,0:T(8,128)(2,1)S(1)} %get-tuple-element.27.refs_0_.factor_high, ...), custom_call_target="tpu_custom_call" | custom-call | flops 905969664 | bytes 7208960 | tf_op jit(solution)/shard_map/pallas_call | solution.py:100
  49.1 0.9 %collective-permute-start.12 = (f32[256,256]{1,0:T(8,128)S(1)}, f32[256,256]{1,0:T(8,128)S(1)}, u32[]{:S(2)}, u32[]{:S(2)}) collective-permute-start(f32[256,256]{1,0:T(8,128)S(1)} %get-tuple-element.30.cross_a), channel_id=1, source_target_pairs={{0,1},{1,0},{2,3},{3,2},{4,5},{5,4},{6,7},{7,6},{8,9},{9,8},{10,11... | collective-permute-start | bytes 786440 | tf_op jit(solution)/shard_map/ppermute | solution.py:376
  50.0 0.6 copy-done.4
  50.6 0.8 %slice-done = f32[1,48,256]{2,1,0:T(8,128)S(1)} async-done(((f32[2,48,256]{2,1,0:T(8,128)}), f32[1,48,256]{2,1,0:T(8,128)S(1)}, s32[]{:S(2)}) %slice-start) | async-done | bytes 49176 | tf_op jit(solution)/shard_map/slice | solution.py:479
  51.4 1.4 %collective-permute-start.27 = (f32[3,48,256]{2,1,0:T(8,128)S(1)}, f32[3,48,256]{2,1,0:T(8,128)S(1)}, u32[]{:S(2)}, u32[]{:S(2)}) collective-permute-start(f32[3,48,256]{2,1,0:T(8,128)S(1)} %pad_maximum_fusion.1), channel_id=1, source_target_pairs={{0,4},{1,5},{2,6},{3,7},{4,0},{5,1},{6,2},{7,3},{8,12},{9,13},{10,... | collective-permute-start | bytes 442376 | tf_op jit(solution)/shard_map/ppermute | solution.py:376
  52.8 2.0 %collective-permute-done.18.refs_8_.near_y = f32[2,2,48,256]{3,2,1,0:T(8,128)S(1)} collective-permute-done((f32[2,2,48,256]{3,2,1,0:T(8,128)S(1)}, f32[2,2,48,256]{3,2,1,0:T(8,128)S(1)}, u32[]{:S(2)}, u32[]{:S(2)}) %collective-permute-start.18) | collective-permute-done | bytes 196640 | tf_op jit(solution)/shard_map/ppermute | solution.py:376
  54.9 0.8 %collective-permute-start.24 = (f32[2,48,256]{2,1,0:T(8,128)S(1)}, f32[2,48,256]{2,1,0:T(8,128)S(1)}, u32[]{:S(2)}, u32[]{:S(2)}) collective-permute-start(f32[2,48,256]{2,1,0:T(8,128)S(1)} %collective-permute-done.23.refs_13_.g_own), channel_id=1, source_target_pairs={{0,4},{1,5},{2,6},{3,7},{4,0},{5,1},{6,2},{7,3},{8,12},{9,13},{10,... | collective-permute-start | bytes 294920 | tf_op jit(solution)/shard_map/ppermute | solution.py:376
  55.7 1.9 %collective-permute-start.25 = (f32[2,48,256]{2,1,0:T(8,128)S(1)}, f32[2,48,256]{2,1,0:T(8,128)S(1)}, u32[]{:S(2)}, u32[]{:S(2)}) collective-permute-start(f32[2,48,256]{2,1,0:T(8,128)S(1)} %collective-permute-done.23.refs_13_.g_own), channel_id=1, source_target_pairs={{0,2},{1,3},{2,0},{3,1},{4,6},{5,7},{6,4},{7,5},{8,10},{9,11},{10,... | collective-permute-start | bytes 294920 | tf_op jit(solution)/shard_map/ppermute | solution.py:376
  57.7 0.9 %collective-permute-start.26 = (f32[2,48,256]{2,1,0:T(8,128)S(1)}, f32[2,48,256]{2,1,0:T(8,128)S(1)}, u32[]{:S(2)}, u32[]{:S(2)}) collective-permute-start(f32[2,48,256]{2,1,0:T(8,128)S(1)} %collective-permute-done.23.refs_13_.g_own), channel_id=1, source_target_pairs={{0,6},{1,7},{2,4},{3,5},{4,2},{5,3},{6,0},{7,1},{8,14},{9,15},{10,... | collective-permute-start | bytes 294920 | tf_op jit(solution)/shard_map/ppermute | solution.py:376
  58.5 0.9 %shard_map.39 = (bf16[256,256]{1,0:T(8,128)(2,1)S(1)}, bf16[256,256]{1,0:T(8,128)(2,1)S(1)}, bf16[256,768]{1,0:T(8,128)(2,1)S(1)}, bf16[256,768]{1,0:T(8,128)(2,1)S(1)}) custom-call(bf16[2,256,256]{2,1,0:T(8,128)(2,1)S(1)} %get-tuple-element.27.refs_0_.factor_high, bf16[2,256,256]{2,1,0:T(8,128)(2,1)S(1)} %get-tuple-element.28.refs_1_.factor_low, ...), custom_call_target="tpu_custom_call" | custom-call | flops 301989888 | bytes 6029312 | tf_op jit(solution)/shard_map/pallas_call | solution.py:100
  59.5 0.7 shard_map.43.before
  60.2 3.6 %collective-permute-done.25.refs_15_.g_x = f32[2,48,256]{2,1,0:T(8,128)S(1)} collective-permute-done((f32[2,48,256]{2,1,0:T(8,128)S(1)}, f32[2,48,256]{2,1,0:T(8,128)S(1)}, u32[]{:S(2)}, u32[]{:S(2)}) %collective-permute-start.25) | collective-permute-done | bytes 98336 | tf_op jit(solution)/shard_map/ppermute | solution.py:376
  63.8 1.4 %collective-permute-done.26.refs_16_.g_d = f32[2,48,256]{2,1,0:T(8,128)S(1)} collective-permute-done((f32[2,48,256]{2,1,0:T(8,128)S(1)}, f32[2,48,256]{2,1,0:T(8,128)S(1)}, u32[]{:S(2)}, u32[]{:S(2)}) %collective-permute-start.26) | collective-permute-done | bytes 98336 | tf_op jit(solution)/shard_map/ppermute | solution.py:376
  65.2 0.7 shard_map.44.inner_a
  66.9 2.2 %collective-permute-done.29.refs_20_ = f32[2,48,256]{2,1,0:T(8,128)S(1)} collective-permute-done((f32[2,48,256]{2,1,0:T(8,128)S(1)}, f32[2,48,256]{2,1,0:T(8,128)S(1)}, u32[]{:S(2)}, u32[]{:S(2)}) %collective-permute-start.29) | collective-permute-done | bytes 98336 | tf_op jit(solution)/shard_map/ppermute | solution.py:376
  69.2 1.4 %shard_map.42 = (f32[192,384]{1,0:T(8,128)S(1)}, bf16[192,512]{1,0:T(8,128)(2,1)S(1)}, bf16[192,512]{1,0:T(8,128)(2,1)S(1)}) custom-call(f32[192,384]{1,0:T(8,128)S(1)} %copy-done.1, bf16[256,256]{1,0:T(8,128)(2,1)S(1)} %get-tuple-element.34.refs_1_.cross_high, bf16[256,256]{1,0:T(8,128)(2,1)S(1)} %get-tuple-element.35.refs_2_.cross_low, ...), custom_call_target="tpu_custom_call" | custom-call | flops 679477248 | bytes 6225920 | tf_op jit(solution)/shard_map/pallas_call | solution.py:100
  70.6 2.0 %shard_map.45 = f32[192,384]{1,0:T(8,128)} custom-call(f32[192,384]{1,0:T(8,128)S(1)} %get-tuple-element.42.base_ref, f32[3,256,256]{2,1,0:T(8,128)S(1)} %shard_map.44.inner_a, f32[3,256,256]{2,1,0:T(8,128)S(1)} %collective-permute-done.31.inner_b, bf16[256,256]{1,0:T(8,128)(2,1)S(1)} %get-tuple-element.34.refs_1_.cross_high, ...), custom_call_target="tpu_custom_call" | custom-call | flops 679477248 | bytes 5046272 | tf_op jit(solution)/shard_map/pallas_call | solution.py:100
  (54 shorter events, 3.4 us)
Async XLA Ops:
  0.0 10.7 %collective-permute-start.1 = (f32[2,48,256]{2,1,0:T(8,128)}, f32[2,48,256]{2,1,0:T(8,128)S(1)}, u32[]{:S(2)}, u32[]{:S(2)}) collective-permute-start(f32[2,48,256]{2,1,0:T(8,128)} %panels_hbm.1), channel_id=1, source_target_pairs={{0,8},{1,9},{2,10},{3,11},{4,12},{5,13},{6,14},{7,15},{8,0},{9,1},... | collective-permute-start | bytes 294920 | tf_op jit(solution)/shard_map/ppermute | solution.py:376
  3.1 10.6 %collective-permute-start.3 = (f32[2,48,256]{2,1,0:T(8,128)}, f32[2,48,256]{2,1,0:T(8,128)S(1)}, u32[]{:S(2)}, u32[]{:S(2)}) collective-permute-start(f32[2,48,256]{2,1,0:T(8,128)} %panels_hbm.1), channel_id=1, source_target_pairs={{0,16},{1,17},{2,18},{3,19},{4,20},{5,21},{6,22},{7,23},{8,24},{9,... | collective-permute-start | bytes 294920 | tf_op jit(solution)/shard_map/ppermute | solution.py:376
  5.6 9.6 %collective-permute-start.5 = (f32[2,48,256]{2,1,0:T(8,128)}, f32[2,48,256]{2,1,0:T(8,128)S(1)}, u32[]{:S(2)}, u32[]{:S(2)}) collective-permute-start(f32[2,48,256]{2,1,0:T(8,128)} %panels_hbm.1), channel_id=1, source_target_pairs={{0,24},{1,25},{2,26},{3,27},{4,28},{5,29},{6,30},{7,31},{8,16},{9,... | collective-permute-start | bytes 294920 | tf_op jit(solution)/shard_map/ppermute | solution.py:376
  5.6 1.0 %copy-start = (f32[192,384]{1,0:T(8,128)S(1)}, f32[192,384]{1,0:T(8,128)}, u32[]{:S(2)}) copy-start(f32[192,384]{1,0:T(8,128)} %refs_0_.1) | copy-start | bytes 884740
  6.6 1.0 %copy-start.6 = (f32[2,256,256]{2,1,0:T(8,128)S(1)}, f32[2,256,256]{2,1,0:T(8,128)}, u32[]{:S(2)}) copy-start(f32[2,256,256]{2,1,0:T(8,128)} %factors_hbm.1) | copy-start | bytes 1572868
  7.7 0.9 %copy-start.7 = (f32[2,48,256]{2,1,0:T(8,128)S(1)}, f32[2,48,256]{2,1,0:T(8,128)}, u32[]{:S(2)}) copy-start(f32[2,48,256]{2,1,0:T(8,128)} %panels_hbm.1) | copy-start | bytes 294916
  8.9 6.8 %collective-permute-start.8 = (f32[2,48,256]{2,1,0:T(8,128)S(1)}, f32[2,48,256]{2,1,0:T(8,128)S(1)}, u32[]{:S(2)}, u32[]{:S(2)}) collective-permute-start(f32[2,48,256]{2,1,0:T(8,128)S(1)} %get-tuple-element.29.refs_4_.refs_0_), channel_id=1, source_target_pairs={{0,4},{1,5},{2,6},{3,7},{4,0},{5,1},{6,2},{7,3},{8,12},{9,13},{10,... | collective-permute-start | bytes 294920 | tf_op jit(solution)/shard_map/ppermute | solution.py:376
  10.7 6.0 %collective-permute-start.9 = (f32[2,48,256]{2,1,0:T(8,128)S(1)}, f32[2,48,256]{2,1,0:T(8,128)S(1)}, u32[]{:S(2)}, u32[]{:S(2)}) collective-permute-start(f32[2,48,256]{2,1,0:T(8,128)S(1)} %collective-permute-done.1.refs_5_.refs_1_), channel_id=1, source_target_pairs={{0,4},{1,5},{2,6},{3,7},{4,0},{5,1},{6,2},{7,3},{8,12},{9,13},{10,... | collective-permute-start | bytes 294920 | tf_op jit(solution)/shard_map/ppermute | solution.py:376
  13.7 4.7 %collective-permute-start.10 = (f32[2,48,256]{2,1,0:T(8,128)S(1)}, f32[2,48,256]{2,1,0:T(8,128)S(1)}, u32[]{:S(2)}, u32[]{:S(2)}) collective-permute-start(f32[2,48,256]{2,1,0:T(8,128)S(1)} %collective-permute-done.3.refs_6_.refs_2_), channel_id=1, source_target_pairs={{0,4},{1,5},{2,6},{3,7},{4,0},{5,1},{6,2},{7,3},{8,12},{9,13},{10,... | collective-permute-start | bytes 294920 | tf_op jit(solution)/shard_map/ppermute | solution.py:376
  15.2 4.6 %collective-permute-start.11 = (f32[2,48,256]{2,1,0:T(8,128)S(1)}, f32[2,48,256]{2,1,0:T(8,128)S(1)}, u32[]{:S(2)}, u32[]{:S(2)}) collective-permute-start(f32[2,48,256]{2,1,0:T(8,128)S(1)} %collective-permute-done.5.refs_7_.refs_3_), channel_id=1, source_target_pairs={{0,4},{1,5},{2,6},{3,7},{4,0},{5,1},{6,2},{7,3},{8,12},{9,13},{10,... | collective-permute-start | bytes 294920 | tf_op jit(solution)/shard_map/ppermute | solution.py:376
  20.5 4.7 %collective-permute-start.14 = (f32[2,2,48,256]{3,2,1,0:T(8,128)S(1)}, f32[2,2,48,256]{3,2,1,0:T(8,128)S(1)}, u32[]{:S(2)}, u32[]{:S(2)}) collective-permute-start(f32[2,2,48,256]{3,2,1,0:T(8,128)S(1)} %get-tuple-element.41), channel_id=1, source_target_pairs={{0,1},{1,0},{2,3},{3,2},{4,5},{5,4},{6,7},{7,6},{8,9},{9,8},{10,11... | collective-permute-start | bytes 589832 | tf_op jit(solution)/shard_map/ppermute | solution.py:376
  20.6 6.3 %collective-permute-start = (f32[2,48,256]{2,1,0:T(8,128)S(1)}, f32[2,48,256]{2,1,0:T(8,128)S(1)}, u32[]{:S(2)}, u32[]{:S(2)}) collective-permute-start(f32[2,48,256]{2,1,0:T(8,128)S(1)} %get-tuple-element.29.refs_4_.refs_0_), channel_id=1, source_target_pairs={{0,2},{1,3},{2,0},{3,1},{4,6},{5,7},{6,4},{7,5},{8,10},{9,11},{10,... | collective-permute-start | bytes 294920 | tf_op jit(solution)/shard_map/ppermute | solution.py:376
  22.1 6.3 %collective-permute-start.6 = (f32[2,48,256]{2,1,0:T(8,128)S(1)}, f32[2,48,256]{2,1,0:T(8,128)S(1)}, u32[]{:S(2)}, u32[]{:S(2)}) collective-permute-start(f32[2,48,256]{2,1,0:T(8,128)S(1)} %collective-permute-done.5.refs_7_.refs_3_), channel_id=1, source_target_pairs={{0,2},{1,3},{2,0},{3,1},{4,6},{5,7},{6,4},{7,5},{8,10},{9,11},{10,... | collective-permute-start | bytes 294920 | tf_op jit(solution)/shard_map/ppermute | solution.py:376
  22.7 7.9 %collective-permute-start.4 = (f32[2,48,256]{2,1,0:T(8,128)S(1)}, f32[2,48,256]{2,1,0:T(8,128)S(1)}, u32[]{:S(2)}, u32[]{:S(2)}) collective-permute-start(f32[2,48,256]{2,1,0:T(8,128)S(1)} %collective-permute-done.3.refs_6_.refs_2_), channel_id=1, source_target_pairs={{0,2},{1,3},{2,0},{3,1},{4,6},{5,7},{6,4},{7,5},{8,10},{9,11},{10,... | collective-permute-start | bytes 294920 | tf_op jit(solution)/shard_map/ppermute | solution.py:376
  24.2 8.5 %collective-permute-start.2 = (f32[2,48,256]{2,1,0:T(8,128)S(1)}, f32[2,48,256]{2,1,0:T(8,128)S(1)}, u32[]{:S(2)}, u32[]{:S(2)}) collective-permute-start(f32[2,48,256]{2,1,0:T(8,128)S(1)} %collective-permute-done.1.refs_5_.refs_1_), channel_id=1, source_target_pairs={{0,2},{1,3},{2,0},{3,1},{4,6},{5,7},{6,4},{7,5},{8,10},{9,11},{10,... | collective-permute-start | bytes 294920 | tf_op jit(solution)/shard_map/ppermute | solution.py:376
  25.3 8.9 %collective-permute-start.15 = (f32[2,48,256]{2,1,0:T(8,128)S(1)}, f32[2,48,256]{2,1,0:T(8,128)S(1)}, u32[]{:S(2)}, u32[]{:S(2)}) collective-permute-start(f32[2,48,256]{2,1,0:T(8,128)S(1)} %slice_bitcast_fusion.2), channel_id=1, source_target_pairs={{0,2},{1,3},{2,0},{3,1},{4,6},{5,7},{6,4},{7,5},{8,10},{9,11},{10,... | collective-permute-start | bytes 294920 | tf_op jit(solution)/shard_map/ppermute | solution.py:376
  32.7 14.5 %collective-permute-start.7 = (f32[4,2,48,256]{3,2,1,0:T(8,128)S(1)}, f32[4,2,48,256]{3,2,1,0:T(8,128)S(1)}, u32[]{:S(2)}, u32[]{:S(2)}) collective-permute-start(f32[4,2,48,256]{3,2,1,0:T(8,128)S(1)} %pad_maximum_fusion.refs_2_), channel_id=1, source_target_pairs={{0,4},{1,5},{2,6},{3,7},{4,0},{5,1},{6,2},{7,3},{8,12},{9,13},{10,... | collective-permute-start | bytes 1179656 | tf_op jit(solution)/shard_map/ppermute | solution.py:376
  34.2 3.4 %collective-permute-start.16 = (f32[2,48,256]{2,1,0:T(8,128)S(1)}, f32[2,48,256]{2,1,0:T(8,128)S(1)}, u32[]{:S(2)}, u32[]{:S(2)}) collective-permute-start(f32[2,48,256]{2,1,0:T(8,128)S(1)} %fusion.refs_19_), channel_id=1, source_target_pairs={{0,8},{1,0},{2,10},{3,2},{4,12},{5,4},{6,14},{7,6},{8,9},{9,1},{10... | collective-permute-start | bytes 294920 | tf_op jit(solution)/shard_map/ppermute | solution.py:376
  34.6 4.6 %collective-permute-start.17 = (f32[2,48,256]{2,1,0:T(8,128)S(1)}, f32[2,48,256]{2,1,0:T(8,128)S(1)}, u32[]{:S(2)}, u32[]{:S(2)}) collective-permute-start(f32[2,48,256]{2,1,0:T(8,128)S(1)} %fusion.refs_19_), channel_id=1, source_target_pairs={{0,2},{1,8},{2,0},{3,10},{4,6},{5,12},{6,4},{7,14},{8,1},{9,11},{1... | collective-permute-start | bytes 294920 | tf_op jit(solution)/shard_map/ppermute | solution.py:376
  36.1 7.2 %collective-permute-start.20 = (f32[2,48,256]{2,1,0:T(8,128)S(1)}, f32[2,48,256]{2,1,0:T(8,128)S(1)}, u32[]{:S(2)}, u32[]{:S(2)}) collective-permute-start(f32[2,48,256]{2,1,0:T(8,128)S(1)} %fusion.refs_19_), channel_id=1, source_target_pairs={{0,24},{1,16},{2,26},{3,18},{4,28},{5,20},{6,30},{7,22},{8,17},{9,... | collective-permute-start | bytes 294920 | tf_op jit(solution)/shard_map/ppermute | solution.py:376
  39.2 11.4 %collective-permute-start.19 = (f32[2,2,48,256]{3,2,1,0:T(8,128)S(1)}, f32[2,2,48,256]{3,2,1,0:T(8,128)S(1)}, u32[]{:S(2)}, u32[]{:S(2)}) collective-permute-start(f32[2,2,48,256]{3,2,1,0:T(8,128)S(1)} %maximum_select_fusion.refs_7_.near), channel_id=1, source_target_pairs={{0,2},{1,3},{2,0},{3,1},{4,6},{5,7},{6,4},{7,5},{8,10},{9,11},{10,... | collective-permute-start | bytes 589832 | tf_op jit(solution)/shard_map/ppermute | solution.py:376
  43.3 5.8 %collective-permute-start.22 = (f32[2,48,256]{2,1,0:T(8,128)S(1)}, f32[2,48,256]{2,1,0:T(8,128)S(1)}, u32[]{:S(2)}, u32[]{:S(2)}) collective-permute-start(f32[2,48,256]{2,1,0:T(8,128)S(1)} %collective-permute-done.20.refs_10_.f_own), channel_id=1, source_target_pairs={{0,2},{1,3},{2,0},{3,1},{4,6},{5,7},{6,4},{7,5},{8,10},{9,11},{10,... | collective-permute-start | bytes 294920 | tf_op jit(solution)/shard_map/ppermute | solution.py:376
  44.8 5.2 %collective-permute-start.21 = (f32[2,48,256]{2,1,0:T(8,128)S(1)}, f32[2,48,256]{2,1,0:T(8,128)S(1)}, u32[]{:S(2)}, u32[]{:S(2)}) collective-permute-start(f32[2,48,256]{2,1,0:T(8,128)S(1)} %collective-permute-done.20.refs_10_.f_own), channel_id=1, source_target_pairs={{0,4},{1,5},{2,6},{3,7},{4,0},{5,1},{6,2},{7,3},{8,12},{9,13},{10,... | collective-permute-start | bytes 294920 | tf_op jit(solution)/shard_map/ppermute | solution.py:376
  46.1 8.8 %collective-permute-start.23 = (f32[2,48,256]{2,1,0:T(8,128)S(1)}, f32[2,48,256]{2,1,0:T(8,128)S(1)}, u32[]{:S(2)}, u32[]{:S(2)}) collective-permute-start(f32[2,48,256]{2,1,0:T(8,128)S(1)} %fusion.refs_19_), channel_id=1, source_target_pairs={{0,16},{1,24},{2,18},{3,26},{4,20},{5,28},{6,22},{7,30},{8,25},{9,... | collective-permute-start | bytes 294920 | tf_op jit(solution)/shard_map/ppermute | solution.py:376
  47.1 7.7 %collective-permute-start.18 = (f32[2,2,48,256]{3,2,1,0:T(8,128)S(1)}, f32[2,2,48,256]{3,2,1,0:T(8,128)S(1)}, u32[]{:S(2)}, u32[]{:S(2)}) collective-permute-start(f32[2,2,48,256]{3,2,1,0:T(8,128)S(1)} %maximum_select_fusion.refs_7_.near), channel_id=1, source_target_pairs={{0,4},{1,5},{2,6},{3,7},{4,0},{5,1},{6,2},{7,3},{8,12},{9,13},{10,... | collective-permute-start | bytes 589832 | tf_op jit(solution)/shard_map/ppermute | solution.py:376
  49.1 0.9 %copy-start.2 = (f32[2,48,256]{2,1,0:T(8,128)}, f32[2,48,256]{2,1,0:T(8,128)S(1)}, u32[]{:S(2)}) copy-start(f32[2,48,256]{2,1,0:T(8,128)S(1)} %collective-permute-done.22.refs_12_.f_x) | copy-start | bytes 294916
  49.1 8.5 %collective-permute-start.12 = (f32[256,256]{1,0:T(8,128)S(1)}, f32[256,256]{1,0:T(8,128)S(1)}, u32[]{:S(2)}, u32[]{:S(2)}) collective-permute-start(f32[256,256]{1,0:T(8,128)S(1)} %get-tuple-element.30.cross_a), channel_id=1, source_target_pairs={{0,1},{1,0},{2,3},{3,2},{4,5},{5,4},{6,7},{7,6},{8,9},{9,8},{10,11... | collective-permute-start | bytes 786440 | tf_op jit(solution)/shard_map/ppermute | solution.py:376
  50.0 0.6 copy-start.4
  50.6 0.8 %slice-start = ((f32[2,48,256]{2,1,0:T(8,128)}), f32[1,48,256]{2,1,0:T(8,128)S(1)}, s32[]{:S(2)}) async-start(f32[2,48,256]{2,1,0:T(8,128)} %copy-done.2), calls=%async_computation | async-start | bytes 98304 | tf_op jit(solution)/shard_map/slice | solution.py:479
  51.4 3.4 %slice-start.1 = ((f32[2,48,256]{2,1,0:T(8,128)}), f32[1,48,256]{2,1,0:T(8,128)S(1)}, s32[]{:S(2)}) async-start(f32[2,48,256]{2,1,0:T(8,128)} %copy-done.4), calls=%async_computation.1 | async-start | bytes 98304 | tf_op jit(solution)/shard_map/slice | solution.py:480
  51.4 13.7 %collective-permute-start.27 = (f32[3,48,256]{2,1,0:T(8,128)S(1)}, f32[3,48,256]{2,1,0:T(8,128)S(1)}, u32[]{:S(2)}, u32[]{:S(2)}) collective-permute-start(f32[3,48,256]{2,1,0:T(8,128)S(1)} %pad_maximum_fusion.1), channel_id=1, source_target_pairs={{0,4},{1,5},{2,6},{3,7},{4,0},{5,1},{6,2},{7,3},{8,12},{9,13},{10,... | collective-permute-start | bytes 442376 | tf_op jit(solution)/shard_map/ppermute | solution.py:376
  54.9 10.3 %collective-permute-start.28 = (f32[3,48,256]{2,1,0:T(8,128)S(1)}, f32[3,48,256]{2,1,0:T(8,128)S(1)}, u32[]{:S(2)}, u32[]{:S(2)}) collective-permute-start(f32[3,48,256]{2,1,0:T(8,128)S(1)} %pad_maximum_fusion.2), channel_id=1, source_target_pairs={{0,2},{1,3},{2,0},{3,1},{4,6},{5,7},{6,4},{7,5},{8,10},{9,11},{10,... | collective-permute-start | bytes 442376 | tf_op jit(solution)/shard_map/ppermute | solution.py:376
  54.9 5.2 %collective-permute-start.24 = (f32[2,48,256]{2,1,0:T(8,128)S(1)}, f32[2,48,256]{2,1,0:T(8,128)S(1)}, u32[]{:S(2)}, u32[]{:S(2)}) collective-permute-start(f32[2,48,256]{2,1,0:T(8,128)S(1)} %collective-permute-done.23.refs_13_.g_own), channel_id=1, source_target_pairs={{0,4},{1,5},{2,6},{3,7},{4,0},{5,1},{6,2},{7,3},{8,12},{9,13},{10,... | collective-permute-start | bytes 294920 | tf_op jit(solution)/shard_map/ppermute | solution.py:376
  55.7 8.0 %collective-permute-start.25 = (f32[2,48,256]{2,1,0:T(8,128)S(1)}, f32[2,48,256]{2,1,0:T(8,128)S(1)}, u32[]{:S(2)}, u32[]{:S(2)}) collective-permute-start(f32[2,48,256]{2,1,0:T(8,128)S(1)} %collective-permute-done.23.refs_13_.g_own), channel_id=1, source_target_pairs={{0,2},{1,3},{2,0},{3,1},{4,6},{5,7},{6,4},{7,5},{8,10},{9,11},{10,... | collective-permute-start | bytes 294920 | tf_op jit(solution)/shard_map/ppermute | solution.py:376
  57.7 7.5 %collective-permute-start.26 = (f32[2,48,256]{2,1,0:T(8,128)S(1)}, f32[2,48,256]{2,1,0:T(8,128)S(1)}, u32[]{:S(2)}, u32[]{:S(2)}) collective-permute-start(f32[2,48,256]{2,1,0:T(8,128)S(1)} %collective-permute-done.23.refs_13_.g_own), channel_id=1, source_target_pairs={{0,6},{1,7},{2,4},{3,5},{4,2},{5,3},{6,0},{7,1},{8,14},{9,15},{10,... | collective-permute-start | bytes 294920 | tf_op jit(solution)/shard_map/ppermute | solution.py:376
  58.5 0.9 %copy-start.5 = (f32[2,48,256]{2,1,0:T(8,128)S(1)}, f32[2,48,256]{2,1,0:T(8,128)}, u32[]{:S(2)}) copy-start(f32[2,48,256]{2,1,0:T(8,128)} %copy-done.4) | copy-start | bytes 294916
  59.5 5.7 %copy-start.3 = (f32[2,48,256]{2,1,0:T(8,128)S(1)}, f32[2,48,256]{2,1,0:T(8,128)}, u32[]{:S(2)}) copy-start(f32[2,48,256]{2,1,0:T(8,128)} %copy-done.2) | copy-start | bytes 294916
  60.2 9.0 %copy-start.1 = (f32[192,384]{1,0:T(8,128)S(1)}, f32[192,384]{1,0:T(8,128)}, u32[]{:S(2)}) copy-start(f32[192,384]{1,0:T(8,128)} %refs_0_.1) | copy-start | bytes 884740
  65.8 4.8 %collective-permute-start.31 = (f32[3,256,256]{2,1,0:T(8,128)S(1)}, f32[3,256,256]{2,1,0:T(8,128)S(1)}, u32[]{:S(2)}, u32[]{:S(2)}) collective-permute-start(f32[3,256,256]{2,1,0:T(8,128)S(1)} %shard_map.44.inner_a), channel_id=1, source_target_pairs={{0,1},{1,0},{2,3},{3,2},{4,5},{5,4},{6,7},{7,6},{8,9},{9,8},{10,11... | collective-permute-start | bytes 2359304 | tf_op jit(solution)/shard_map/ppermute | solution.py:376
  65.9 3.3 %collective-permute-start.13 = (f32[192,512]{1,0:T(8,128)S(1)}, f32[192,512]{1,0:T(8,128)S(1)}, u32[]{:S(2)}, u32[]{:S(2)}) collective-permute-start(f32[192,512]{1,0:T(8,128)S(1)} %get-tuple-element.40.refs_5_), channel_id=1, source_target_pairs={{0,1},{1,0},{2,3},{3,2},{4,5},{5,4},{6,7},{7,6},{8,9},{9,8},{10,11... | collective-permute-start | bytes 1179656 | tf_op jit(solution)/shard_map/ppermute | solution.py:376
  66.4 2.8 %collective-permute-start.30 = (f32[2,2,48,256]{3,2,1,0:T(8,128)S(1)}, f32[2,2,48,256]{3,2,1,0:T(8,128)S(1)}, u32[]{:S(2)}, u32[]{:S(2)}) collective-permute-start(f32[2,2,48,256]{3,2,1,0:T(8,128)S(1)} %collective-permute-done.19.refs_9_.near_x), channel_id=1, source_target_pairs={{0,1},{1,0},{2,3},{3,2},{4,5},{5,4},{6,7},{7,6},{8,9},{9,8},{10,11... | collective-permute-start | bytes 589832 | tf_op jit(solution)/shard_map/ppermute | solution.py:376
  66.5 2.7 %collective-permute-start.29 = (f32[2,48,256]{2,1,0:T(8,128)S(1)}, f32[2,48,256]{2,1,0:T(8,128)S(1)}, u32[]{:S(2)}, u32[]{:S(2)}) collective-permute-start(f32[2,48,256]{2,1,0:T(8,128)S(1)} %fusion.refs_19_), channel_id=1, source_target_pairs={{0,1},{1,0},{2,3},{3,2},{4,5},{5,4},{6,7},{7,6},{8,9},{9,8},{10,11... | collective-permute-start | bytes 294920 | tf_op jit(solution)/shard_map/ppermute | solution.py:376
